TPU v7x, 32 devices: a whole 2x2x4 slice. The times are simulated.
32 devices in a mesh: dp: 8 (over y, x, core), seq: 4 (over z).
Axes of the slice: x: 2, y: 2, z: 4, core: 2. Of those that a mesh axis runs over, the one named last changes fastest.
Arguments:
- inputs: bfloat16 [24, 1024, 768], P('dp', 'seq'), may hold values from -6 to 6
- segments: int32 [24, 1024], P('dp'), may hold values from 0 to 3, never falling along the last dimension, each value on 1 to 512 neighbouring positions
- cotangent: bfloat16 [24, 1024, 768], P('dp', 'seq'), may hold values from -6 to 6
- weights: float32 [768, 9216], P(None, 'dp'), may hold values from -0.18042196 to 0.18042196
- first_moment: float32 [768, 9216], P(None, 'dp'), may hold values from -112 to 112
- second_moment: float32 [768, 9216], P(None, 'dp'), may hold values from 12.288 to 98.304
- bases: float32 [4, 768, 768], replicated, may hold values from -0.08660254 to 0.8866025
- right_bases: float32 [9216, 3072], P('dp'), may hold values from -0.08660254 to 0.8866025, as said below
- small: float32 [9216], replicated, may hold values from -2 to 2
- small_first: float32 [9216], replicated, may hold values from -112 to 112
- small_second: float32 [9216], replicated, may hold values from 12.288 to 98.304
Outputs:
- output: bfloat16 [24, 1024, 768], P('dp', 'seq')
- input_grad: bfloat16 [24, 1024, 768], P('dp', 'seq')
- weight_grad: float32 [768, 9216], P(None, 'dp')
- first_new: float32 [768, 9216], P(None, 'dp')
- second_new: float32 [768, 9216], P(None, 'dp')
- weights_new: float32 [768, 9216], P(None, 'dp')
- weights_low: bfloat16 [768, 9216], P(None, 'dp')
- small_grad: float32 [9216], replicated
- small_first_new: float32 [9216], replicated
- small_second_new: float32 [9216], replicated
- small_new: float32 [9216], replicated
Inputs may be any that keep to these rules, and one draw needn't show every extreme that they name: `segments`: along each row the ids never fall; every id covers 1 to 512 positions and one covers exactly 512. `right_bases`: entries of a row past the number of columns of that row's block are zero.
All inputs are finite; a program needn't handle non-finite values.
Results may differ from a plain program's by a relative error of at most 0.012.
Values may be sent and summed in bfloat16 or wider, within the bound.
A program may use at most 256 MiB of HBM per device.

v0:
```python
import jax
import jax.numpy as jnp
from jax import lax
from jax.sharding import PartitionSpec as P

D = 768
HEADS = 12
HD = 64
FF = 3072
STEP = 10


highest = lax.Precision.HIGHEST
norm_eps = 1e-12
beta_first = 0.9
beta_second = 0.999
adam_eps = 1e-08
learn_rate = 0.03
small_rate = 0.3


def contract_first(left, right):
    return lax.dot_general(
        left, right, (((0,), (0,)), ((), ())), preferred_element_type=jnp.float32
    )


def contract_last(left, right):
    return lax.dot_general(
        left, right, (((1,), (1,)), ((), ())), preferred_element_type=jnp.float32
    )


def exact_last(left, right):
    return lax.dot_general(
        left, right, (((1,), (1,)), ((), ())), precision=highest, preferred_element_type=jnp.float32
    )


def normalize(resid, gain, shift):
    centre = resid - jnp.mean(resid, axis=-1, keepdims=True)
    spread = jnp.mean(centre * centre, axis=-1, keepdims=True)
    inv_std = lax.rsqrt(spread + norm_eps)
    scaled = centre * inv_std
    return (scaled * gain + shift, scaled, inv_std)


def norm_back(grad, scaled, inv_std, gain):
    lifted = grad * gain
    return inv_std * (
        lifted
        - jnp.mean(lifted, axis=-1, keepdims=True)
        - scaled * jnp.mean(lifted * scaled, axis=-1, keepdims=True)
    )


def moments(grad, first, second):
    first_out = beta_first * first + (1.0 - beta_first) * grad
    second_out = beta_second * second + (1.0 - beta_second) * grad * grad
    heading = (
        first_out
        / (1.0 - beta_first**STEP)
        / (jnp.sqrt(second_out / (1.0 - beta_second**STEP)) + adam_eps)
    )
    return (first_out, second_out, heading)


def on_device(
    inputs,
    segments,
    cotangent,
    weights,
    first_moment,
    second_moment,
    bases,
    right_bases,
    small,
    small_first,
    small_second,
):
    number, quarter, width = inputs.shape
    length = segments.shape[1]
    groups = lax.axis_size("seq")
    owners = lax.axis_size("dp")
    heads_local = HEADS // groups
    group_width = width // groups
    scale = HD ** (-0.5)
    share = weights.shape[1]
    block_widths = [3 * D // owners, D // owners, FF // owners, FF // owners]
    block_starts = [
        0,
        block_widths[0],
        block_widths[0] + block_widths[1],
        block_widths[0] + block_widths[1] + block_widths[2],
    ]

    def split_wide(matrix):
        shaped = matrix.reshape(matrix.shape[0], owners, share)
        return [
            shaped[:, :, block_starts[which] : block_starts[which] + block_widths[which]].reshape(
                matrix.shape[0], owners * block_widths[which]
            )
            for which in range(4)
        ]

    def join_wide(parts):
        rows = parts[0].shape[0]
        return jnp.concatenate(
            [parts[which].reshape(rows, owners, block_widths[which]) for which in range(4)], axis=2
        ).reshape(rows, owners * share)

    wide = lax.all_gather(weights.astype(jnp.bfloat16), "dp", axis=1, tiled=True)
    w_qkv, w_out, w_up, w_down = split_wide(wide)
    pieces = [small[index * D : (index + 1) * D] for index in range(8)] + [small[8 * D :]]
    (
        gain_one,
        gain_two,
        shift_one,
        shift_two,
        bias_query,
        bias_value,
        bias_out,
        bias_down,
        bias_up,
    ) = pieces
    token_rows = inputs.reshape(number * quarter, width)
    acts = token_rows.astype(jnp.float32)
    project = jnp.dot(token_rows, w_qkv, preferred_element_type=jnp.float32)
    queries = (project[:, :D] + bias_query).astype(jnp.bfloat16)
    keys_all = project[:, D : 2 * D].astype(jnp.bfloat16)
    values = (project[:, 2 * D :] + bias_value).astype(jnp.bfloat16)

    def to_heads(array):
        return array.reshape(number, quarter, groups, group_width)

    head_q, head_k, head_v = (
        lax.all_to_all(to_heads(queries), "seq", split_axis=2, concat_axis=1, tiled=True),
        lax.all_to_all(to_heads(keys_all), "seq", split_axis=2, concat_axis=1, tiled=True),
        lax.all_to_all(to_heads(values), "seq", split_axis=2, concat_axis=1, tiled=True),
    )
    head_q = head_q.reshape(number, length, heads_local, HD)
    head_k = head_k.reshape(number, length, heads_local, HD)
    head_v = head_v.reshape(number, length, heads_local, HD)

    def attend_one(item):
        one_q, one_k, one_v, marks = item
        same = (marks[:, None] == marks[None, :])[None]
        raw = jnp.einsum("qhd,khd->hqk", one_q, one_k, preferred_element_type=jnp.float32) * scale
        masked = jnp.where(same, raw, -1e30)
        peak = jnp.max(masked, axis=-1, keepdims=True)
        expo = jnp.exp(masked - peak)
        totals = jnp.sum(expo, axis=-1, keepdims=True)
        probs = expo / totals
        log_sum = peak + jnp.log(totals)
        mixed = jnp.einsum(
            "hqk,khd->qhd", probs.astype(jnp.bfloat16), one_v, preferred_element_type=jnp.float32
        )
        return (mixed.astype(jnp.bfloat16), log_sum)

    mixed, log_sums = lax.map(attend_one, (head_q, head_k, head_v, segments))
    context_heads = mixed.reshape(number, length, 1, group_width)
    context = lax.all_to_all(context_heads, "seq", split_axis=1, concat_axis=2, tiled=True).reshape(
        number * quarter, width
    )
    attended = jnp.dot(context, w_out, preferred_element_type=jnp.float32) + bias_out
    first, scaled_one, inv_one = normalize(acts + attended, gain_one, shift_one)
    first_low = first.astype(jnp.bfloat16)
    upward = jnp.dot(first_low, w_up, preferred_element_type=jnp.float32) + bias_up
    active_full, gelu_pull = jax.vjp(lambda value: jax.nn.gelu(value, approximate=False), upward)
    active = active_full.astype(jnp.bfloat16)
    downward = contract_last(active, w_down) + bias_down
    output, scaled_two, inv_two = normalize(first + downward, gain_two, shift_two)
    grad_out = cotangent.reshape(number * quarter, width).astype(jnp.float32)
    d_two = norm_back(grad_out, scaled_two, inv_two, gain_two)
    grad_gain_two = jnp.sum(grad_out * scaled_two, axis=0)
    grad_shift_two = jnp.sum(grad_out, axis=0)
    d_down = d_two.astype(jnp.bfloat16)
    grad_bias_down = jnp.sum(d_down.astype(jnp.float32), axis=0)
    grad_w_down = contract_first(d_down, active)
    d_active = jnp.dot(d_down, w_down, preferred_element_type=jnp.float32)
    (d_up_full,) = gelu_pull(d_active)
    d_up = d_up_full.astype(jnp.bfloat16)
    grad_bias_up = jnp.sum(d_up.astype(jnp.float32), axis=0)
    grad_w_up = contract_first(first_low, d_up)
    d_first = d_two + contract_last(d_up, w_up)
    d_one = norm_back(d_first, scaled_one, inv_one, gain_one)
    grad_gain_one = jnp.sum(d_first * scaled_one, axis=0)
    grad_shift_one = jnp.sum(d_first, axis=0)
    d_att = d_one.astype(jnp.bfloat16)
    grad_bias_out = jnp.sum(d_att.astype(jnp.float32), axis=0)
    grad_w_out = contract_first(context, d_att)
    d_context = contract_last(d_att, w_out).astype(jnp.bfloat16)
    d_heads = lax.all_to_all(
        to_heads(d_context), "seq", split_axis=2, concat_axis=1, tiled=True
    ).reshape(number, length, heads_local, HD)

    def attend_back(item):
        one_q, one_k, one_v, marks, one_grad, one_log = item
        same = (marks[:, None] == marks[None, :])[None]
        raw = jnp.einsum("qhd,khd->hqk", one_q, one_k, preferred_element_type=jnp.float32) * scale
        again = jnp.where(same, jnp.exp(raw - one_log), 0.0)
        d_values = jnp.einsum(
            "hqk,qhd->khd", again.astype(jnp.bfloat16), one_grad, preferred_element_type=jnp.float32
        )
        d_probs = jnp.einsum("qhd,khd->hqk", one_grad, one_v, preferred_element_type=jnp.float32)
        d_scores = (again * (d_probs - jnp.sum(again * d_probs, axis=-1, keepdims=True))).astype(
            jnp.bfloat16
        )
        d_queries = (
            jnp.einsum("hqk,khd->qhd", d_scores, one_k, preferred_element_type=jnp.float32) * scale
        )
        d_keys = (
            jnp.einsum("hqk,qhd->khd", d_scores, one_q, preferred_element_type=jnp.float32) * scale
        )
        return (
            d_queries.astype(jnp.bfloat16),
            d_keys.astype(jnp.bfloat16),
            d_values.astype(jnp.bfloat16),
        )

    grads_q, grads_k, grads_v = lax.map(
        attend_back, (head_q, head_k, head_v, segments, d_heads, log_sums)
    )

    def to_send(array):
        return array.reshape(number, length, 1, group_width)

    back_q, back_k, back_v = (
        lax.all_to_all(to_send(grads_q), "seq", split_axis=1, concat_axis=2, tiled=True),
        lax.all_to_all(to_send(grads_k), "seq", split_axis=1, concat_axis=2, tiled=True),
        lax.all_to_all(to_send(grads_v), "seq", split_axis=1, concat_axis=2, tiled=True),
    )
    d_project = jnp.concatenate(
        [
            back_q.reshape(number * quarter, width),
            back_k.reshape(number * quarter, width),
            back_v.reshape(number * quarter, width),
        ],
        axis=1,
    )
    grad_bias_query = jnp.sum(back_q.reshape(number * quarter, width).astype(jnp.float32), axis=0)
    grad_bias_value = jnp.sum(back_v.reshape(number * quarter, width).astype(jnp.float32), axis=0)
    grad_w_qkv = contract_first(token_rows, d_project)
    input_grad = (d_one + contract_last(d_project, w_qkv)).astype(jnp.bfloat16)
    grad_full = join_wide([grad_w_qkv, grad_w_out, grad_w_up, grad_w_down])
    small_local = jnp.concatenate(
        [
            grad_gain_one,
            grad_gain_two,
            grad_shift_one,
            grad_shift_two,
            grad_bias_query,
            grad_bias_value,
            grad_bias_out,
            grad_bias_down,
            grad_bias_up,
        ]
    )
    small_grad = lax.psum(small_local, ("dp", "seq"))
    reduced = lax.psum_scatter(grad_full, "dp", scatter_dimension=1, tiled=True)
    reduced = lax.psum(reduced.astype(jnp.bfloat16), "seq").astype(jnp.float32)
    right_rows = []
    turned_parts = []
    for which in range(4):
        begin = block_starts[which]
        count = block_widths[which]
        extent = owners * count
        rows_here = right_bases[begin : begin + count, :extent]
        right_rows.append(rows_here)
        left_turned = jnp.dot(bases[which].T, reduced[:, begin : begin + count], precision=highest)
        turned_parts.append(jnp.dot(left_turned, rows_here, precision=highest))
    term = join_wide(turned_parts)
    rotated = lax.psum_scatter(term, "dp", scatter_dimension=1, tiled=True)
    first_new, second_new, heading = moments(rotated, first_moment, second_moment)
    left_step = jnp.concatenate(
        [
            jnp.dot(
                bases[which],
                heading[:, block_starts[which] : block_starts[which] + block_widths[which]],
                precision=highest,
            )
            for which in range(4)
        ],
        axis=1,
    )
    every_step = lax.all_gather(left_step.astype(jnp.bfloat16), "dp", axis=1, tiled=True).astype(
        left_step.dtype
    )
    step_parts = split_wide(every_step)
    update = jnp.concatenate(
        [exact_last(step_parts[which], right_rows[which]) for which in range(4)], axis=1
    )
    weights_new = weights - learn_rate * update
    small_first_new, small_second_new, small_heading = moments(
        small_grad, small_first, small_second
    )
    small_new = small - small_rate * small_heading
    return (
        output.astype(jnp.bfloat16).reshape(number, quarter, width),
        input_grad.reshape(number, quarter, width),
        reduced,
        first_new,
        second_new,
        weights_new,
        weights_new.astype(jnp.bfloat16),
        small_grad,
        small_first_new,
        small_second_new,
        small_new,
    )


def solution(mesh):
    return jax.shard_map(
        on_device,
        mesh=mesh,
        in_specs=(
            P("dp", "seq", None),
            P("dp", None),
            P("dp", "seq", None),
            P(None, "dp"),
            P(None, "dp"),
            P(None, "dp"),
            P(),
            P("dp", None),
            P(),
            P(),
            P(),
        ),
        out_specs=(
            P("dp", "seq", None),
            P("dp", "seq", None),
            P(None, "dp"),
            P(None, "dp"),
            P(None, "dp"),
            P(None, "dp"),
            P(None, "dp"),
            P(),
            P(),
            P(),
            P(),
        ),
        check_vma=False,
    )
```

profile of v0, /device:TPU:1, one launch (start us, length us, event | category | flops | bytes accessed | tf_op | source)
XLA Modules:
  0.0 1505.9 jit_solution(18342674644949686309)
XLA Ops:
  11.3 80.5 %all-gather.3.cloned.1.call-done = bf16[768,9216]{1,0:T(8,128)(2,1)} async-done(((bf16[768,1152]{1,0:T(8,128)(2,1)}), bf16[768,9216]{1,0:T(8,128)(2,1)}) %all-gather.3.cloned.1.call-update) | async-done | bytes 14155792 | tf_op jit(solution)/shard_map/all_gather | solution.py:112
  91.8 18.5 %copy.112 = bf16[768,9216]{0,1:T(8,128)(2,1)} copy(bf16[768,9216]{1,0:T(8,128)(2,1)} %all-gather.3.cloned.1.call-done) | data formatting | bytes 28311552 | tf_op jit(solution)/shard_map/all_gather | solution.py:112
  132.4 22.5 %all-to-all-done = bf16[3,256,4,192]{1,3,0,2:T(8,128)(2,1)S(1)} async-done(((bf16[3,256,4,192]{1,3,0,2:T(8,128)(2,1)}), bf16[3,256,4,192]{1,3,0,2:T(8,128)(2,1)S(1)}, u32[]{:S(2)}, u32[]{:S(2)}) %all-to-all-start) | async-done | bytes 1179680 | tf_op jit(solution)/shard_map/all_to_all | solution.py:139
  167.6 19.7 %all-to-all-done.1 = bf16[3,256,4,192]{1,3,0,2:T(8,128)(2,1)} async-done(((bf16[3,256,4,192]{1,3,0,2:T(8,128)(2,1)}), bf16[3,256,4,192]{1,3,0,2:T(8,128)(2,1)}, u32[]{:S(2)}, u32[]{:S(2)}) %all-to-all-start.1) | async-done | bytes 1179680 | tf_op jit(solution)/shard_map/all_to_all | solution.py:137
  200.2 18.8 %all-to-all-done.2 = bf16[3,256,4,192]{1,3,0,2:T(8,128)(2,1)S(1)} async-done(((bf16[3,256,4,192]{1,3,0,2:T(8,128)(2,1)}), bf16[3,256,4,192]{1,3,0,2:T(8,128)(2,1)S(1)}, u32[]{:S(2)}, u32[]{:S(2)}) %all-to-all-start.2) | async-done | bytes 1179680 | tf_op jit(solution)/shard_map/all_to_all | solution.py:138
  222.8 47.5 %while.26 = (s32[]{:T(128)}, bf16[3,1024,3,64]{1,3,2,0:T(8,128)(2,1)}, f32[3,3,1024,1]{2,1,3,0:T(4,128)}, bf16[3,1024,3,64]{1,3,2,0:T(8,128)(2,1)}, s32[3,1024]{...) while((s32[]{:T(128)}, ...), condition=%wide.region_3.4_spmd, body=%wide.region_0.3_spmd.sunk | while | flops 844297216 | bytes 47827072 | solution.py:160
  283.3 8.2 fusion.168
  291.5 35.5 %all-to-all-done.3 = bf16[3,1024,1,192]{3,0,2,1:T(4,128)(2,1)} async-done(((bf16[3,1024,1,192]{3,0,2,1:T(4,128)(2,1)}), bf16[3,1024,1,192]{3,0,2,1:T(4,128)(2,1)}, u32[]{:S(2)}, u32[]{:S(2)}) %all-to-all-start.3) | async-done | bytes 1179680 | tf_op jit(solution)/shard_map/all_to_all | solution.py:162
  340.5 28.4 %multiply_convert_fusion.1 = (bf16[768,3072]{1,0:T(8,128)(2,1)S(1)}, f32[768,3072]{1,0:T(8,128)}, f32[768,3072]{1,0:T(8,128)}) fusion(f32[3072]{0:T(1024)S(1)} %slice.124, bf16[768,3072]{0,1:T(8,128)(2,1)} %bitcast.308, f32[768,768]{1,0:T(8,128)S(1)} %get-tuple-element.239, f32[768]{0:T(1024)S(1)} %copy-done.32, f32[768]{0:T(1024)S(1)} %copy-done.28, ...), kind=kOutput, calls=%fused_computation.70 | convolution fusion | flops 3782541312 | bytes 30695424 | tf_op jit(solution)/shard_map/dot_general | solution.py:168
  377.5 13.2 convert_reduce_fusion
  403.4 30.2 %all_to_all.120 = bf16[3,256,4,192]{1,3,0,2:T(8,128)(2,1)S(1)} all-to-all(bf16[3,256,4,192]{1,3,0,2:T(8,128)(2,1)S(1)} %copy.122), channel_id=1, replica_groups=mesh['dp'=8,'seq'=4] {'seq'}, dimensions={2} | all-to-all | bytes 2359296 | tf_op jit(solution)/shard_map/all_to_all | solution.py:193
  441.8 81.4 %while.27 = (s32[]{:T(128)}, bf16[3,1024,3,64]{1,3,2,0:T(8,128)(2,1)}, bf16[3,1024,3,64]{1,3,2,0:T(8,128)(2,1)}, bf16[3,1024,3,64]{1,3,2,0:T(8,128)(2,1)}, bf16[...) while((s32[]{:T(128)}, ...), condition=%wide.region_14.15_spmd, body=%wide.region_12.14_spmd.sunk | while | flops 2062480384 | bytes 102610048 | solution.py:221
  445.7 7.7 multiply_reduce_fusion.7
  453.5 6.9 multiply_convert_fusion.3
  472.9 7.7 multiply_reduce_fusion.7
  480.6 6.9 multiply_convert_fusion.3
  500.0 7.7 multiply_reduce_fusion.7
  507.7 6.9 multiply_convert_fusion.3
  534.3 45.3 %all-to-all-done.5 = bf16[3,1024,1,192]{3,0,2,1:T(4,128)(2,1)} async-done(((bf16[3,1024,1,192]{3,0,2,1:T(4,128)(2,1)}), bf16[3,1024,1,192]{3,0,2,1:T(4,128)(2,1)}, u32[]{:S(2)}, u32[]{:S(2)}) %all-to-all-start.5) | async-done | bytes 1179680 | tf_op jit(solution)/shard_map/all_to_all | solution.py:229
  596.5 35.8 %all-to-all-done.6 = bf16[3,1024,1,192]{3,0,2,1:T(4,128)(2,1)} async-done(((bf16[3,1024,1,192]{3,0,2,1:T(4,128)(2,1)}), bf16[3,1024,1,192]{3,0,2,1:T(4,128)(2,1)}, u32[]{:S(2)}, u32[]{:S(2)}) %all-to-all-start.6) | async-done | bytes 1179680 | tf_op jit(solution)/shard_map/all_to_all | solution.py:230
  636.8 6.5 fusion.157
  643.3 5.9 copy.153
  653.3 5.8 copy.154
  676.9 7.6 all-to-all-done.7
  697.6 7.8 fusion.173
  705.5 9.1 copy.134
  714.6 30.4 %concatenate.20 = f32[768,8,1152]{2,1,0:T(8,128)} concatenate(f32[768,8,288]{2,1,0:T(8,128)} %copy.134, f32[768,8,96]{2,1,0:T(8,128)S(1)} %copy-done.7, f32[768,8,384]{2,1,0:T(8,128)} %bitcast.278, f32[768,8,384]{2,1,0:T(8,128)} %bitcast.279), dimensions={2} | concatenate | bytes 56623104 | tf_op jit(solution)/shard_map/concatenate | solution.py:108
  745.0 25.3 %copy.155 = f32[96,8,8,1152]{3,1,2,0:T(8,128)} copy(f32[96,8,8,1152]{3,2,1,0:T(8,128)} %bitcast.271) | data formatting | bytes 56623104
  770.3 169.5 %reduce-scatter.3.cloned.1.call-done = f32[768,1152]{1,0:T(8,128)} async-done(((f32[768,9216]{1,0:T(8,128)}), f32[768,1152]{1,0:T(8,128)}) %reduce-scatter.3.cloned.1.call-update) | async-done | bytes 3538960 | tf_op jit(solution)/shard_map/reduce_scatter | solution.py:260
  943.3 74.6 %all-reduce.2.cloned.1.call-done = bf16[768,1152]{1,0:T(8,128)(2,1)} async-done(((bf16[768,1152]{1,0:T(8,128)(2,1)}), bf16[768,1152]{1,0:T(8,128)(2,1)}) %all-reduce.2.cloned.1.call-update) | async-done | bytes 1769488 | tf_op jit(solution)/shard_map/psum | solution.py:261
  1021.2 15.1 %fusion.77 = f32[768,2304]{0,1:T(8,128)} fusion(f32[288,768]{1,0:T(8,128)S(1)} %fusion.95, f32[1152,3072]{1,0:T(8,128)} %param.22), kind=kOutput, calls=%fused_computation.100 | convolution fusion | flops 6115295232 | bytes 10616832 | tf_op jit(solution)/shard_map/dot_general | solution.py:271
  1036.2 9.0 copy.137
  1058.5 17.9 %fusion.71 = f32[768,3072]{1,0:T(8,128)S(1)} fusion(f32[384,768]{1,0:T(8,128)S(1)} %fusion.87, f32[1152,3072]{1,0:T(8,128)} %param.22), kind=kOutput, calls=%fused_computation.91 | convolution fusion | flops 10871635968 | bytes 15335424 | tf_op jit(solution)/shard_map/dot_general | solution.py:271
  1076.4 5.8 copy.156
  1085.9 17.7 %fusion.67 = f32[768,3072]{1,0:T(8,128)S(1)} fusion(f32[384,768]{1,0:T(8,128)S(1)} %fusion.83, f32[1152,3072]{1,0:T(8,128)} %param.22), kind=kOutput, calls=%fused_computation.87 | convolution fusion | flops 10871635968 | bytes 15335424 | tf_op jit(solution)/shard_map/dot_general | solution.py:271
  1109.2 30.4 %concatenate.21 = f32[768,8,1152]{2,1,0:T(8,128)} concatenate(f32[768,8,288]{2,1,0:T(8,128)} %copy.137, f32[768,8,96]{2,1,0:T(8,128)S(1)} %copy.138, f32[768,8,384]{2,1,0:T(8,128)} %bitcast.280, f32[768,8,384]{2,1,0:T(8,128)} %bitcast.281), dimensions={2} | concatenate | bytes 56623104 | tf_op jit(solution)/shard_map/concatenate | solution.py:108
  1139.6 25.3 %copy.158 = f32[96,8,8,1152]{3,1,2,0:T(8,128)} copy(f32[96,8,8,1152]{3,2,1,0:T(8,128)} %bitcast.272) | data formatting | bytes 56623104
  1165.2 170.6 %reduce-scatter.5.cloned.1.call-done = f32[768,1152]{1,0:T(8,128)} async-done(((f32[768,9216]{1,0:T(8,128)}), f32[768,1152]{1,0:T(8,128)}) %reduce-scatter.5.cloned.1.call-update) | async-done | bytes 3538960 | tf_op jit(solution)/shard_map/reduce_scatter | solution.py:273
  1335.8 8.2 add_divide_fusion
  1344.1 7.3 fusion.122
  1351.4 7.7 fusion.125
  1363.3 7.4 fusion.128
  1393.8 41.5 %psum.15 = f32[9216]{0:T(1024)} all-reduce(f32[9216]{0:T(1024)} %constant_dynamic-update-slice_fusion.6), channel_id=1, replica_groups=mesh['dp'=8,'seq'=4] {'dp','seq'}, use_global_device_ids=true, to_apply=%region_27.28 | all-reduce | flops 9216 | bytes 73728 | tf_op jit(solution)/shard_map/psum | solution.py:259
  1436.8 7.8 add_convert_fusion.1
  1446.6 6.0 all-gather.5.cloned.1.call-done
  1452.6 8.3 fusion.167
  1465.2 9.4 fusion.65
  1474.7 7.2 fusion.69
  (287 shorter events, 345.1 us)
Async XLA Ops:
  7.2 84.6 %all-gather.3.cloned.1.call-start = ((), (), s32[]{:S(2)}) async-start(), calls=%async_computation.10 | async-start | bytes 15925248 | tf_op jit(solution)/shard_map/all_gather | solution.py:112
  122.4 32.4 %all-to-all-start = ((bf16[3,256,4,192]{1,3,0,2:T(8,128)(2,1)}), bf16[3,256,4,192]{1,3,0,2:T(8,128)(2,1)S(1)}, u32[]{:S(2)}, u32[]{:S(2)}) async-start(bf16[3,256,4,192]{1,3,0,2:T(8,128)(2,1)} %copy.113), calls=%async_computation | async-start | bytes 2359296 | tf_op jit(solution)/shard_map/all_to_all | solution.py:139
  154.8 32.4 %all-to-all-start.1 = ((bf16[3,256,4,192]{1,3,0,2:T(8,128)(2,1)}), bf16[3,256,4,192]{1,3,0,2:T(8,128)(2,1)}, u32[]{:S(2)}, u32[]{:S(2)}) async-start(bf16[3,256,4,192]{1,3,0,2:T(8,128)(2,1)} %copy.115), calls=%async_computation.1 | async-start | bytes 2359296 | tf_op jit(solution)/shard_map/all_to_all | solution.py:137
  187.3 31.8 %all-to-all-start.2 = ((bf16[3,256,4,192]{1,3,0,2:T(8,128)(2,1)}), bf16[3,256,4,192]{1,3,0,2:T(8,128)(2,1)S(1)}, u32[]{:S(2)}, u32[]{:S(2)}) async-start(bf16[3,256,4,192]{1,3,0,2:T(8,128)(2,1)} %copy.117), calls=%async_computation.2 | async-start | bytes 2359296 | tf_op jit(solution)/shard_map/all_to_all | solution.py:138
  270.3 9.5 copy-start.10
  270.3 9.5 copy-start.35
  274.5 52.5 %all-to-all-start.3 = ((bf16[3,1024,1,192]{3,0,2,1:T(4,128)(2,1)}), bf16[3,1024,1,192]{3,0,2,1:T(4,128)(2,1)}, u32[]{:S(2)}, u32[]{:S(2)}) async-start(bf16[3,1024,1,192]{3,0,2,1:T(4,128)(2,1)} %copy.119), calls=%async_computation.3 | async-start | bytes 4194304 | tf_op jit(solution)/shard_map/all_to_all | solution.py:162
  336.6 32.2 %slice-start.8 = ((s8[4718592]{0:T(1024)(128)(4,1)}), s8[4194304]{0:T(1024)(128)(4,1)S(1)}, s32[]{:S(2)}) async-start(s8[4718592]{0:T(1024)(128)(4,1)} %bitcast.313), calls=%async_computation.23 | async-start | bytes 8388608
  340.0 56.9 %copy-start.3 = (f32[768,768]{1,0:T(8,128)}, f32[768,768]{1,0:T(8,128)S(1)}, u32[]{:S(2)}) copy-start(f32[768,768]{1,0:T(8,128)S(1)} %get-tuple-element.239) | copy-start | bytes 7077892
  340.0 56.9 %copy-start.26 = (f32[768]{0:T(1024)}, f32[768]{0:T(1024)S(1)}, u32[]{:S(2)}) copy-start(f32[768]{0:T(1024)S(1)} %broadcast_multiply_fusion.5) | copy-start | bytes 9220
  340.4 56.5 %copy-start.30 = (f32[768]{0:T(1024)}, f32[768]{0:T(1024)S(1)}, u32[]{:S(2)}) copy-start(f32[768]{0:T(1024)S(1)} %add_rsqrt_fusion.1) | copy-start | bytes 9220
  340.5 28.4 %slice-start.9 = ((s8[4718592]{0:T(1024)(128)(4,1)}), s8[524288]{0:T(1024)(128)(4,1)S(1)}, s32[]{:S(2)}) async-start(s8[4718592]{0:T(1024)(128)(4,1)} %bitcast.313), calls=%async_computation.24 | async-start | bytes 1048576
  340.5 28.4 %copy-start.41 = (f32[768]{0:T(1024)S(1)}, f32[768]{0:T(1024)}, u32[]{:S(2)}) copy-start(f32[768]{0:T(1024)} %get-tuple-element.231) | copy-start | bytes 9220
  374.9 15.8 %slice-start.6 = ((s8[4718592]{0:T(1024)(128)(4,1)}), s8[524288]{0:T(1024)(128)(4,1)S(1)}, s32[]{:S(2)}) async-start(s8[4718592]{0:T(1024)(128)(4,1)} %bitcast.309), calls=%async_computation.21 | async-start | bytes 1048576
  377.5 13.2 copy-start.12
  377.5 13.2 slice-start.7
  435.5 6.3 copy-start.1
  435.5 6.3 copy-start.2
  523.2 8.6 copy-start.17
  527.3 52.3 %all-to-all-start.5 = ((bf16[3,1024,1,192]{3,0,2,1:T(4,128)(2,1)}), bf16[3,1024,1,192]{3,0,2,1:T(4,128)(2,1)}, u32[]{:S(2)}, u32[]{:S(2)}) async-start(bf16[3,1024,1,192]{3,0,2,1:T(4,128)(2,1)} %copy.124), calls=%async_computation.5 | async-start | bytes 4194304 | tf_op jit(solution)/shard_map/all_to_all | solution.py:229
  531.8 52.7 %copy-start.6 = (bf16[3,256,4,1,192]{4,2,1,0,3:T(4,128)(2,1)S(1)}, bf16[3,256,4,1,192]{4,2,1,0,3:T(4,128)(2,1)}, u32[]{:S(2)}) copy-start(bf16[3,256,4,1,192]{4,2,1,0,3:T(4,128)(2,1)} %copy-done.5) | copy-start | bytes 3538948
  579.6 52.7 %all-to-all-start.6 = ((bf16[3,1024,1,192]{3,0,2,1:T(4,128)(2,1)}), bf16[3,1024,1,192]{3,0,2,1:T(4,128)(2,1)}, u32[]{:S(2)}, u32[]{:S(2)}) async-start(bf16[3,1024,1,192]{3,0,2,1:T(4,128)(2,1)} %copy.127), calls=%async_computation.6 | async-start | bytes 4194304 | tf_op jit(solution)/shard_map/all_to_all | solution.py:230
  593.9 42.9 %copy-start.4 = (f32[768,768]{1,0:T(8,128)S(1)}, f32[768,768]{1,0:T(8,128)}, u32[]{:S(2)}) copy-start(f32[768,768]{1,0:T(8,128)} %copy-done.3) | copy-start | bytes 7077892
  593.9 42.9 %copy-start.27 = (f32[768]{0:T(1024)S(1)}, f32[768]{0:T(1024)}, u32[]{:S(2)}) copy-start(f32[768]{0:T(1024)} %copy-done.26) | copy-start | bytes 9220
  593.9 42.9 %copy-start.29 = (f32[768]{0:T(1024)S(1)}, f32[768]{0:T(1024)}, u32[]{:S(2)}) copy-start(f32[768]{0:T(1024)} %get-tuple-element.233) | copy-start | bytes 9220
  593.9 42.9 %copy-start.31 = (f32[768]{0:T(1024)S(1)}, f32[768]{0:T(1024)}, u32[]{:S(2)}) copy-start(f32[768]{0:T(1024)} %copy-done.30) | copy-start | bytes 9220
  593.9 42.9 %copy-start.33 = (f32[768]{0:T(1024)S(1)}, f32[768]{0:T(1024)}, u32[]{:S(2)}) copy-start(f32[768]{0:T(1024)} %get-tuple-element.232) | copy-start | bytes 9220
  632.3 52.3 %all-to-all-start.7 = ((bf16[3,1024,1,192]{3,0,2,1:T(4,128)(2,1)}), bf16[3,1024,1,192]{3,0,2,1:T(4,128)(2,1)}, u32[]{:S(2)}, u32[]{:S(2)}) async-start(bf16[3,1024,1,192]{3,0,2,1:T(4,128)(2,1)} %copy.130), calls=%async_computation.7 | async-start | bytes 4194304 | tf_op jit(solution)/shard_map/all_to_all | solution.py:231
  636.7 303.1 %reduce-scatter.3.cloned.1.call-start = ((), (), s32[]{:S(2)}) async-start(), calls=%async_computation.11 | async-start | bytes 31850496 | tf_op jit(solution)/shard_map/reduce_scatter | solution.py:260
  636.8 12.4 slice-start.4
  643.3 5.9 copy-start.13
  663.0 8.5 copy-start.8
  688.4 6.9 copy-start.9
  705.5 9.1 copy-start.7
  770.3 247.6 %all-reduce.2.cloned.1.call-start = ((), (), s32[]{:S(2)}) async-start(), calls=%async_computation.12 | async-start | bytes 3538944 | tf_op jit(solution)/shard_map/psum | solution.py:261
  943.2 392.6 %reduce-scatter.5.cloned.1.call-start = ((), (), s32[]{:S(2)}) async-start(), calls=%async_computation.13 | async-start | bytes 31850496 | tf_op jit(solution)/shard_map/reduce_scatter | solution.py:273
  1164.9 170.9 %copy-start.24 = (f32[768,1152]{1,0:T(8,128)S(1)}, f32[768,1152]{1,0:T(8,128)}, u32[]{:S(2)}) copy-start(f32[768,1152]{1,0:T(8,128)} %param.20) | copy-start | bytes 10616836
  1164.9 287.7 %all-gather.5.cloned.1.call-start = ((), (), s32[]{:S(2)}) async-start(), calls=%async_computation.14 | async-start | bytes 15925248 | tf_op jit(solution)/shard_map/all_gather | solution.py:286
  1372.0 6.0 copy-start.37
  1372.0 17.9 %copy-start.39 = (f32[768]{0:T(1024)S(1)}, f32[768]{0:T(1024)}, u32[]{:S(2)}) copy-start(f32[768]{0:T(1024)} %get-tuple-element.210) | copy-start | bytes 9220
  1372.0 19.2 %copy-start.38 = (f32[768]{0:T(1024)S(1)}, f32[768]{0:T(1024)}, u32[]{:S(2)}) copy-start(f32[768]{0:T(1024)} %get-tuple-element.208) | copy-start | bytes 9220
  1436.8 7.8 copy-start.14
  1452.6 22.0 %slice-start = ((s8[14155776]{0:T(1024)(128)(4,1)}), s8[1572864]{0:T(1024)(128)(4,1)S(1)}, s32[]{:S(2)}) async-start(s8[14155776]{0:T(1024)(128)(4,1)} %bitcast.290), calls=%async_computation.15 | async-start | bytes 3145728
  1452.6 22.0 %slice-start.1 = ((s8[14155776]{0:T(1024)(128)(4,1)}), s8[4194304]{0:T(1024)(128)(4,1)S(1)}, s32[]{:S(2)}) async-start(s8[14155776]{0:T(1024)(128)(4,1)} %bitcast.290), calls=%async_computation.16 | async-start | bytes 8388608
  1460.9 13.7 slice-start.2
  1462.4 12.2 slice-start.10
  1465.2 9.5 slice-start.3
  1465.2 9.4 slice-start.11
  (23 other events, 87.1 us)
Sparse Core Ops, SparseCore 0:
  10.8 81.0 all-gather.2
  770.4 169.3 reduce-scatter.2
  943.3 74.4 all-reduce.1
  1165.1 170.6 reduce-scatter.4
  1372.1 80.4 all-gather.4
where the time goes:
time: 1520 us; the launch traced here: 1510 us
  waiting for transfers between devices  687 us (45%)
  local copies, waits for them, and re-layouts  334 us (22%)
  matrix products  287 us (19%)
  other arithmetic  80.2 us (5%)
  blocking collectives  71.6 us (5%)
  starting transfers between devices  31.1 us (2%)
    reduce_scatter x1, waiting for transfers between devices, on_device(): rotated = lax.psum_scatter(term, 'dp', scatter_dimension=1, tiled=True)  171 us
    reduce_scatter x1, waiting for transfers between devices, on_device(): reduced = lax.psum_scatter(grad_full, 'dp', scatter_dimension=1, tiled=True)  169 us
    unnamed x130, local copies, waits for them, and re-layouts  100 us
    all_gather x1, waiting for transfers between devices, on_device(): lax.all_gather(weights.astype(jnp.bfloat16), 'dp', axis=1, tiled=True)  80.5 us
    psum x1, waiting for transfers between devices, on_device(): reduced = lax.psum(reduced.astype(jnp.bfloat16), 'seq').astype(jnp.float32)  74.6 us
    concatenate x2, local copies, waits for them, and re-layouts, join_wide(): jnp.concatenate([parts[which].reshape(rows, owners, block_widths[which])...  60.8 us
    dot_general x4, matrix products, on_device(): turned_parts.append(jnp.dot(left_turned, rows_here, precision=highest))  55.1 us
    all_to_all x1, waiting for transfers between devices, on_device(): lax.all_to_all(to_send(grads_q), 'seq', split_axis=1, concat_axis=2, tile...  45.3 us
  transfers between devices with their start and end apart: 12, of which 12 were waited for; matrix products, arithmetic and copies ran while one was open for 8% of the time, Pallas kernels for 0%

commit v1 on v0

v1 whole, which is shorter than its diff:
```python
import functools
import math

import jax
import jax.numpy as jnp
from jax import lax
from jax.experimental import pallas as pl
from jax.experimental.pallas import tpu as pltpu
from jax.sharding import PartitionSpec as P

D = 768
HEADS = 12
HD = 64
FF = 3072
STEP = 10


norm_eps = 1e-12
beta_first = 0.9
beta_second = 0.999
adam_eps = 1e-08
learn_rate = 0.03
small_rate = 0.3

TILE = 256
LANES = 128
WINDOWS = (256, 512, 640, 768, 1024)
NEG = -1e30
VMEM_LIMIT = 60 * 1024 * 1024


def dot_dims(left, right, left_dim, right_dim):
    return lax.dot_general(
        left, right, (((left_dim,), (right_dim,)), ((), ())), preferred_element_type=jnp.float32
    )


def normalize(resid, gain, shift):
    centre = resid - jnp.mean(resid, axis=-1, keepdims=True)
    spread = jnp.mean(centre * centre, axis=-1, keepdims=True)
    inv_std = lax.rsqrt(spread + norm_eps)
    scaled = centre * inv_std
    return (scaled * gain + shift, scaled, inv_std)


def norm_back(grad, scaled, inv_std, gain):
    lifted = grad * gain
    return inv_std * (
        lifted
        - jnp.mean(lifted, axis=-1, keepdims=True)
        - scaled * jnp.mean(lifted * scaled, axis=-1, keepdims=True)
    )


def moments(grad, first, second):
    first_out = beta_first * first + (1.0 - beta_first) * grad
    second_out = beta_second * second + (1.0 - beta_second) * grad * grad
    heading = (
        first_out
        / (1.0 - beta_first**STEP)
        / (jnp.sqrt(second_out / (1.0 - beta_second**STEP)) + adam_eps)
    )
    return (first_out, second_out, heading)


def windows_of(length):
    return tuple(size for size in WINDOWS if size < length) + (length,)


def key_windows(marks):
    rows, length = marks.shape
    tile = min(TILE, length)
    sizes = windows_of(length)
    heads = marks[:, ::tile]
    tails = marks[:, tile - 1 :: tile]
    low = jnp.sum((marks[:, None, :] < heads[:, :, None]).astype(jnp.int32), axis=-1)
    high = jnp.sum((marks[:, None, :] <= tails[:, :, None]).astype(jnp.int32), axis=-1)
    begin = low // LANES * LANES
    need = high - begin
    which = jnp.zeros_like(need)
    for size in sizes[:-1]:
        which = which + (need > size).astype(jnp.int32)
    width = jnp.asarray(sizes, jnp.int32)[which]
    begin = jnp.minimum(begin, length - width)
    return jnp.stack([begin, which], axis=-1).reshape(rows, -1)


def head_lanes(half, shape):
    lane = lax.broadcasted_iota(jnp.int32, shape, 1)
    return (lane >= half * HD) & (lane < (half + 1) * HD)


def attend_kernel(sizes, tile, table, q_ref, k_ref, v_ref, col_ref, row_ref, ctx_ref, log_ref, vt_ref):
    length = k_ref.shape[0]
    row = pl.program_id(0)
    vt_ref[...] = v_ref[...].astype(jnp.float32).T.astype(jnp.bfloat16)

    @pl.loop(0, length // tile)
    def _(step):
        begin = pl.multiple_of(table[row, 2 * step], LANES)
        which = table[row, 2 * step + 1]
        rows = pl.ds(pl.multiple_of(step * tile, tile), tile)
        for number, size in enumerate(sizes):

            @pl.when(which == number)
            def _(size=size):
                keys = k_ref[pl.ds(begin, size), :]
                marks = col_ref[pl.ds(begin, size), :]
                same = jnp.concatenate([marks] * (tile // LANES), axis=1) == row_ref[0, :, rows]
                here = q_ref[rows, :]
                done = []
                for half in range(2):
                    mine = jnp.where(head_lanes(half, here.shape), here * HD ** (-0.5), 0.0).astype(
                        jnp.bfloat16
                    )
                    raw = jnp.where(same, dot_dims(keys, mine, 1, 1), NEG)
                    peak = jnp.max(raw, axis=0, keepdims=True)
                    expo = jnp.exp(raw - peak)
                    total = jnp.sum(expo, axis=0, keepdims=True)
                    mixed = jnp.dot(
                        vt_ref[half * HD : (half + 1) * HD, pl.ds(begin, size)],
                        expo.astype(jnp.bfloat16),
                        preferred_element_type=jnp.float32,
                    )
                    done.append(mixed * (1.0 / total))
                    log_ref[0, half : half + 1, rows] = peak + jnp.log(total)
                ctx_ref[rows, :] = jnp.concatenate(done, axis=0).T.astype(jnp.bfloat16)


def attend(table, project, marks_col, marks_row, rows, length):
    pairs = HEADS * HD // LANES
    tile = min(TILE, length)
    sizes = windows_of(length)
    columns = lambda part: pl.BlockSpec((length, LANES), lambda i, j, t: (i, part * pairs + j))
    flops = 4 * rows * HEADS * length * length * HD
    return pl.pallas_call(
        functools.partial(attend_kernel, sizes, tile),
        out_shape=(
            jax.ShapeDtypeStruct((rows * length, D), jnp.bfloat16),
            jax.ShapeDtypeStruct((rows * pairs, 2, length), jnp.float32),
        ),
        grid_spec=pltpu.PrefetchScalarGridSpec(
            num_scalar_prefetch=1,
            grid=(rows, pairs),
            in_specs=[
                columns(0),
                columns(1),
                columns(2),
                pl.BlockSpec((length, LANES), lambda i, j, t: (i, 0)),
                pl.BlockSpec((1, 1, length), lambda i, j, t: (i, 0, 0)),
            ],
            out_specs=[
                pl.BlockSpec((length, LANES), lambda i, j, t: (i, j)),
                pl.BlockSpec((1, 2, length), lambda i, j, t: (i * pairs + j, 0, 0)),
            ],
            scratch_shapes=[pltpu.VMEM((LANES, length), jnp.bfloat16)],
        ),
        compiler_params=pltpu.CompilerParams(vmem_limit_bytes=VMEM_LIMIT),
        cost_estimate=pl.CostEstimate(
            flops=flops, bytes_accessed=8 * rows * length * D, transcendentals=rows * HEADS * length * length
        ),
        name="attend",
    )(table, project, project, project, marks_col, marks_row)


def attend_back_kernel(
    sizes, tile, table, q_ref, k_ref, v_ref, g_ref, col_ref, row_ref, log_ref, out_ref, kt_ref, dk_ref, dv_ref
):
    length = k_ref.shape[0]
    row = pl.program_id(0)
    kt_ref[...] = k_ref[...].astype(jnp.float32).T.astype(jnp.bfloat16)
    dk_ref[...] = jnp.zeros_like(dk_ref)
    dv_ref[...] = jnp.zeros_like(dv_ref)
    scale = HD ** (-0.5)

    @pl.loop(0, length // tile)
    def _(step):
        begin = pl.multiple_of(table[row, 2 * step], LANES)
        which = table[row, 2 * step + 1]
        rows = pl.ds(pl.multiple_of(step * tile, tile), tile)
        for number, size in enumerate(sizes):

            @pl.when(which == number)
            def _(size=size):
                window = pl.ds(begin, size)
                keys = k_ref[window, :]
                vals = v_ref[window, :]
                marks = col_ref[window, :]
                same = jnp.concatenate([marks] * (tile // LANES), axis=1) == row_ref[0, :, rows]
                here = q_ref[rows, :]
                grad = g_ref[rows, :]
                done = []
                for half in range(2):
                    lanes = head_lanes(half, here.shape)
                    mine = jnp.where(lanes, here * scale, 0.0).astype(jnp.bfloat16)
                    own = jnp.where(lanes, grad, 0.0).astype(jnp.bfloat16)
                    raw = jnp.where(same, dot_dims(keys, mine, 1, 1), NEG)
                    probs = jnp.exp(raw - log_ref[0, half : half + 1, rows])
                    d_probs = dot_dims(vals, own, 1, 1)
                    dv_ref[window, :] += jnp.dot(
                        probs.astype(jnp.bfloat16), own, preferred_element_type=jnp.float32
                    )
                    product = probs * d_probs
                    inner = jnp.sum(product, axis=0, keepdims=True)
                    d_scores = (product - probs * inner).astype(jnp.bfloat16)
                    dk_ref[window, :] += jnp.dot(d_scores, mine, preferred_element_type=jnp.float32)
                    done.append(
                        jnp.dot(
                            kt_ref[half * HD : (half + 1) * HD, window],
                            d_scores,
                            preferred_element_type=jnp.float32,
                        )
                    )
                out_ref[0, rows, :] = (jnp.concatenate(done, axis=0) * scale).T.astype(jnp.bfloat16)

    out_ref[1, :, :] = dk_ref[...].astype(jnp.bfloat16)
    out_ref[2, :, :] = dv_ref[...].astype(jnp.bfloat16)


def attend_back(table, project, grad, marks_col, marks_row, log_sum, rows, length):
    pairs = HEADS * HD // LANES
    tile = min(TILE, length)
    sizes = windows_of(length)
    columns = lambda part: pl.BlockSpec((length, LANES), lambda i, j, t: (i, part * pairs + j))
    flops = 10 * rows * HEADS * length * length * HD
    return pl.pallas_call(
        functools.partial(attend_back_kernel, sizes, tile),
        out_shape=jax.ShapeDtypeStruct((3, rows * length, D), jnp.bfloat16),
        grid_spec=pltpu.PrefetchScalarGridSpec(
            num_scalar_prefetch=1,
            grid=(rows, pairs),
            in_specs=[
                columns(0),
                columns(1),
                columns(2),
                columns(0),
                pl.BlockSpec((length, LANES), lambda i, j, t: (i, 0)),
                pl.BlockSpec((1, 1, length), lambda i, j, t: (i, 0, 0)),
                pl.BlockSpec((1, 2, length), lambda i, j, t: (i * pairs + j, 0, 0)),
            ],
            out_specs=pl.BlockSpec((3, length, LANES), lambda i, j, t: (0, i, j)),
            scratch_shapes=[
                pltpu.VMEM((LANES, length), jnp.bfloat16),
                pltpu.VMEM((length, LANES), jnp.float32),
                pltpu.VMEM((length, LANES), jnp.float32),
            ],
        ),
        compiler_params=pltpu.CompilerParams(vmem_limit_bytes=VMEM_LIMIT),
        cost_estimate=pl.CostEstimate(
            flops=flops, bytes_accessed=14 * rows * length * D, transcendentals=rows * HEADS * length * length
        ),
        name="attend_back",
    )(table, project, project, project, grad, marks_col, marks_row, log_sum)


def on_device(
    inputs,
    segments,
    cotangent,
    weights,
    first_moment,
    second_moment,
    bases,
    right_bases,
    small,
    small_first,
    small_second,
):
    number, quarter, width = inputs.shape
    length = segments.shape[1]
    groups = lax.axis_size("seq")
    owners = lax.axis_size("dp")
    place = lax.axis_index("seq")
    rows = -(-number // groups)
    padded = rows * groups
    tokens = rows * length
    block_widths = [3 * D // owners, D // owners, FF // owners, FF // owners]
    block_starts = [sum(block_widths[:which]) for which in range(4)]

    def blocks_of(matrix):
        return [
            matrix[block_starts[which] : block_starts[which] + block_widths[which]]
            for which in range(4)
        ]

    def to_rows(array):
        array = jnp.pad(array, ((0, padded - number), (0, 0), (0, 0)))
        moved = lax.all_to_all(array, "seq", split_axis=0, concat_axis=1, tiled=True)
        return moved.reshape(tokens, width)

    def to_quarters(array):
        array = array.reshape(rows, length, width)
        moved = lax.all_to_all(array, "seq", split_axis=1, concat_axis=0, tiled=True)
        return moved[:number]

    x = to_rows(inputs)
    pull = to_rows(cotangent)
    low = weights.astype(jnp.bfloat16).T
    w_qkv, w_out, w_up, w_down = [
        lax.all_gather(block, "dp", axis=0, tiled=True) for block in blocks_of(low)
    ]
    pieces = [small[index * D : (index + 1) * D] for index in range(8)] + [small[8 * D :]]
    (
        gain_one,
        gain_two,
        shift_one,
        shift_two,
        bias_query,
        bias_value,
        bias_out,
        bias_down,
        bias_up,
    ) = pieces

    filler = jnp.broadcast_to(
        (jnp.arange(length, dtype=jnp.int32) // TILE)[None], (padded - number, length)
    )
    marks = lax.dynamic_slice_in_dim(
        jnp.concatenate([segments, filler], axis=0), place * rows, rows, axis=0
    )
    table = key_windows(marks)
    marks_col = jnp.broadcast_to(marks.reshape(tokens, 1), (tokens, LANES))
    marks_row = marks.reshape(rows, 1, length)

    acts = x.astype(jnp.float32)
    bias_qkv = jnp.concatenate([bias_query, jnp.zeros_like(bias_query), bias_value])
    project = (dot_dims(x, w_qkv, 1, 1) + bias_qkv).astype(jnp.bfloat16)
    context, log_sum = attend(table, project, marks_col, marks_row, rows, length)
    attended = dot_dims(context, w_out, 1, 1) + bias_out
    first, scaled_one, inv_one = normalize(acts + attended, gain_one, shift_one)
    first_low = first.astype(jnp.bfloat16)
    upward = dot_dims(first_low, w_up, 1, 1) + bias_up
    active_full, gelu_pull = jax.vjp(lambda value: jax.nn.gelu(value, approximate=False), upward)
    active = active_full.astype(jnp.bfloat16)
    downward = dot_dims(active, w_down, 1, 0) + bias_down
    output, scaled_two, inv_two = normalize(first + downward, gain_two, shift_two)
    grad_out = pull.astype(jnp.float32)
    d_two = norm_back(grad_out, scaled_two, inv_two, gain_two)
    grad_gain_two = jnp.sum(grad_out * scaled_two, axis=0)
    grad_shift_two = jnp.sum(grad_out, axis=0)
    d_down = d_two.astype(jnp.bfloat16)
    grad_bias_down = jnp.sum(d_down.astype(jnp.float32), axis=0)
    grad_down = dot_dims(active, d_down, 0, 0).astype(jnp.bfloat16)
    d_active = dot_dims(d_down, w_down, 1, 1)
    (d_up_full,) = gelu_pull(d_active)
    d_up = d_up_full.astype(jnp.bfloat16)
    grad_bias_up = jnp.sum(d_up.astype(jnp.float32), axis=0)
    grad_up = dot_dims(d_up, first_low, 0, 0).astype(jnp.bfloat16)
    d_first = d_two + dot_dims(d_up, w_up, 1, 0)
    d_one = norm_back(d_first, scaled_one, inv_one, gain_one)
    grad_gain_one = jnp.sum(d_first * scaled_one, axis=0)
    grad_shift_one = jnp.sum(d_first, axis=0)
    d_att = d_one.astype(jnp.bfloat16)
    grad_bias_out = jnp.sum(d_att.astype(jnp.float32), axis=0)
    grad_outw = dot_dims(d_att, context, 0, 0).astype(jnp.bfloat16)
    d_context = dot_dims(d_att, w_out, 1, 0).astype(jnp.bfloat16)
    d_qkv = attend_back(table, project, d_context, marks_col, marks_row, log_sum, rows, length)
    grad_bias_query = jnp.sum(d_qkv[0].astype(jnp.float32), axis=0)
    grad_bias_value = jnp.sum(d_qkv[2].astype(jnp.float32), axis=0)
    grad_qkv = jnp.concatenate([dot_dims(d_qkv[part], x, 0, 0) for part in range(3)], axis=0).astype(
        jnp.bfloat16
    )
    input_grad = d_one
    for part in range(3):
        input_grad = input_grad + dot_dims(d_qkv[part], w_qkv[part * D : (part + 1) * D], 1, 0)
    input_grad = to_quarters(input_grad.astype(jnp.bfloat16))
    output = to_quarters(output.astype(jnp.bfloat16))

    small_local = jnp.concatenate(
        [
            grad_gain_one,
            grad_gain_two,
            grad_shift_one,
            grad_shift_two,
            grad_bias_query,
            grad_bias_value,
            grad_bias_out,
            grad_bias_down,
            grad_bias_up,
        ]
    )
    small_grad = lax.psum(small_local, ("dp", "seq"))

    grads = [grad_qkv, grad_outw, grad_up, grad_down]
    mine = jnp.concatenate(
        [lax.psum_scatter(grad, "dp", scatter_dimension=0, tiled=True) for grad in grads], axis=0
    )
    mine = lax.psum(mine, "seq")
    reduced = mine.T.astype(jnp.float32)
    bases_low = bases.astype(jnp.bfloat16)
    rights = [
        right_bases[
            block_starts[which] : block_starts[which] + block_widths[which],
            : owners * block_widths[which],
        ].astype(jnp.bfloat16)
        for which in range(4)
    ]
    rotated = []
    for which, block in enumerate(blocks_of(mine)):
        turned = dot_dims(block, bases_low[which], 1, 0).astype(jnp.bfloat16)
        term = dot_dims(rights[which], turned, 0, 0).astype(jnp.bfloat16)
        rotated.append(lax.psum_scatter(term, "dp", scatter_dimension=0, tiled=True))
    rotated = jnp.concatenate(rotated, axis=0).T.astype(jnp.float32)
    first_new, second_new, heading = moments(rotated, first_moment, second_moment)
    heading = heading.astype(jnp.bfloat16)
    update = []
    for which in range(4):
        block = heading[:, block_starts[which] : block_starts[which] + block_widths[which]]
        step = dot_dims(block, bases_low[which], 0, 1).astype(jnp.bfloat16)
        every = lax.all_gather(step, "dp", axis=0, tiled=True)
        update.append(dot_dims(every, rights[which], 0, 1))
    weights_new = weights - learn_rate * jnp.concatenate(update, axis=1)
    small_first_new, small_second_new, small_heading = moments(
        small_grad, small_first, small_second
    )
    small_new = small - small_rate * small_heading
    return (
        output,
        input_grad,
        reduced,
        first_new,
        second_new,
        weights_new,
        weights_new.astype(jnp.bfloat16),
        small_grad,
        small_first_new,
        small_second_new,
        small_new,
    )


def solution(mesh):
    return jax.shard_map(
        on_device,
        mesh=mesh,
        in_specs=(
            P("dp", "seq", None),
            P("dp", None),
            P("dp", "seq", None),
            P(None, "dp"),
            P(None, "dp"),
            P(None, "dp"),
            P(),
            P("dp", None),
            P(),
            P(),
            P(),
        ),
        out_specs=(
            P("dp", "seq", None),
            P("dp", "seq", None),
            P(None, "dp"),
            P(None, "dp"),
            P(None, "dp"),
            P(None, "dp"),
            P(None, "dp"),
            P(),
            P(),
            P(),
            P(),
        ),
        check_vma=False,
    )
```

time: 1520 us -> 969 us (0.64)
  waiting for transfers between devices: 687 us -> 447 us
  local copies, waits for them, and re-layouts: 334 us -> 95.7 us
  matrix products: 287 us -> 195 us
  Pallas kernels: 0 us -> 62.8 us
  blocking collectives: 71.6 us -> 54.8 us
    reduce_scatter x2 -> x4, waiting for transfers between devices: 340 us -> 154 us  [on_device(): lax.psum_scatter(grad, 'dp', scatter_dimension=0, tiled=True)]
    unnamed x5 -> x21, waiting for transfers between devices: 0.08 us -> 161 us
    all_to_all x7 -> x4, waiting for transfers between devices: 185 us -> 72.6 us  [the longest x2 67.5 us: to_rows(): lax.all_to_all(array, 'seq', split_axis=0, concat_axis=1, tiled=True)]
    dot_general x49 -> x28, matrix products: 287 us -> 195 us  [dot_dims(): lax.dot_general(left, right, (((left_dim,), (right_dim,)), ((), ())), pre...]
    all_gather x2 -> x8, waiting for transfers between devices: 86.6 us -> 0.03 us  [the longest x4 0.02 us: on_device(): lax.all_gather(block, 'dp', axis=0, tiled=True)]
    pallas_call x0 -> x2, Pallas kernels: none -> 62.8 us  [the longest x1 33.6 us: attend_back(): pl.pallas_call(functools.partial(attend_back_kernel, sizes, tile), out_sh...]
    concatenate x3 -> x1, local copies, waits for them, and re-layouts: 63.1 us -> 2.01 us  [on_device(): rotated = jnp.concatenate(rotated, axis=0).T.astype(jnp.float32)]
    reshape x24 -> x4, local copies, waits for them, and re-layouts: 71.8 us -> 17.7 us  [the longest x2 14.5 us: to_quarters(): array = array.reshape(rows, length, width)]
  transfers between devices with their start and end apart: 12 -> 21, of which waited for: 12 -> 10; matrix products, arithmetic and copies ran while one was open for 8% -> 26% of each run, Pallas kernels for 0% -> 7%
where the time goes in v1:
time: 969 us; the launch traced here: 958 us
  waiting for transfers between devices  447 us (46%)
  matrix products  195 us (20%)
  local copies, waits for them, and re-layouts  95.7 us (10%)
  other arithmetic  67.9 us (7%)
  Pallas kernels  62.8 us (6%)
  blocking collectives  54.8 us (6%)
  starting transfers between devices  20.1 us (2%)
  between operations  15 us (2%)
    dot_general x28, matrix products, dot_dims(): lax.dot_general(left, right, (((left_dim,), (right_dim,)), ((), ())), pre...  195 us
    unnamed x21, waiting for transfers between devices  161 us
    reduce_scatter x4, waiting for transfers between devices, on_device(): lax.psum_scatter(grad, 'dp', scatter_dimension=0, tiled=True)  154 us
    all_to_all x2, waiting for transfers between devices, to_rows(): lax.all_to_all(array, 'seq', split_axis=0, concat_axis=1, tiled=True)  67.5 us
    unnamed x98, local copies, waits for them, and re-layouts  62.7 us
    psum x1, waiting for transfers between devices, on_device(): mine = lax.psum(mine, 'seq')  59.4 us
    psum x1, blocking collectives, on_device(): small_grad = lax.psum(small_local, ('dp', 'seq'))  54.8 us
    pallas_call x1, Pallas kernels, attend_back(): pl.pallas_call(functools.partial(attend_back_kernel, sizes, tile), out_sh...  33.6 us
  transfers between devices with their start and end apart: 21, of which 10 were waited for; matrix products, arithmetic and copies ran while one was open for 26% of the time, Pallas kernels for 7%

profile of v1, /device:TPU:1, one launch (start us, length us, event | category | flops | bytes accessed | tf_op | source)
XLA Modules:
  0.0 958.0 jit_solution(12542497371827141419)
XLA Ops:
  18.5 5.4 all-to-all-start.2
  25.2 35.3 %all-to-all-done.2 = bf16[4,256,768]{2,1,0:T(8,128)(2,1)S(1)} async-done(((bf16[4,256,768]{2,1,0:T(8,128)(2,1)}), bf16[4,256,768]{2,1,0:T(8,128)(2,1)S(1)}, u32[]{:S(2)}, u32[]{:S(2)}) %all-to-all-start.2) | async-done | bytes 1572896 | tf_op jit(solution)/shard_map/all_to_all | solution.py:288
  60.4 4.4 all-to-all-start
  69.2 32.2 %all-to-all-done = bf16[4,256,768]{2,1,0:T(8,128)(2,1)} async-done(((bf16[4,256,768]{2,1,0:T(8,128)(2,1)}), bf16[4,256,768]{2,1,0:T(8,128)(2,1)}, u32[]{:S(2)}, u32[]{:S(2)}) %all-to-all-start) | async-done | bytes 1572896 | tf_op jit(solution)/shard_map/all_to_all | solution.py:288
  106.8 8.5 add_convert_fusion.1.q_ref.k_ref.v_ref
  116.3 29.1 %attend.1 = (bf16[1024,768]{1,0:T(8,128)(2,1)}, f32[6,2,1024]{2,1,0:T(2,128)}) custom-call(s32[1,8]{1,0:T(1,128)} %reshape.454.table, bf16[1024,2304]{1,0:T(8,128)(2,1)} %add_convert_fusion.1.q_ref.k_ref.v_ref, bf16[1024,2304]{1,0:T(8,128)(2,1)} %add_convert_fusion.1.q_ref.k_ref.v_ref, bf16[1024,2304]{1,0:T(8,128)(2,1)} %add_convert_fusion.1.q_ref.k_ref.v_ref, ...), custom_call_target="tpu_custom_call" | custom-call | flops 3221225472 | bytes 6291456 | tf_op jit(solution)/shard_map/attend/pallas_call | solution.py:136
  145.5 3.7 fusion.68
  151.3 38.0 %multiply_convert_fusion = (bf16[1024,3072]{1,0:T(8,128)(2,1)}, f32[1024,3072]{1,0:T(8,128)}, f32[1024,3072]{1,0:T(8,128)}) fusion(f32[3072]{0:T(1024)S(1)} %slice.152, bf16[3072,768]{1,0:T(8,128)(2,1)} %all-gather.13.cloned.1.call-done, f32[1024,768]{0,1:T(8,128)} %copy-done.4, f32[768]{0:T(1024)S(1)} %get-tuple-element.103, ...), kind=kOutput, calls=%fused_computation.5 | convolution fusion | flops 5043388416 | bytes 39348224 | tf_op jit(solution)/shard_map/dot_general | solution.py:33
  189.3 19.2 %fusion.69 = (f32[1024]{0:T(1024)S(1)}, f32[1024,768]{0,1:T(8,128)S(1)}) fusion(f32[768]{0:T(1024)S(1)} %get-tuple-element.102, bf16[1024,3072]{1,0:T(8,128)(2,1)} %get-tuple-element.94, bf16[3072,768]{1,0:T(8,128)(2,1)} %all-gather.15.cloned.1.call-done, f32[768]{0:T(1024)S(1)} %get-tuple-element.103, f32[768]{0:T(1024)S(1)} %get-tuple-element.104, ...), kind=kOutput, calls=%fused_computation.173 | convolution fusion | flops 4837342208 | bytes 17323008 | tf_op jit(solution)/shard_map/dot_general | solution.py:33
  210.5 3.6 convert_reduce_fusion.1
  214.1 19.1 %convert_reduce_fusion = (f32[3072]{0:T(1024)S(1)}, bf16[1024,3072]{1,0:T(8,128)(2,1)}) fusion(f32[1024,3072]{1,0:T(8,128)} %get-tuple-element.95, bf16[3072,768]{1,0:T(8,128)(2,1)} %all-gather.15.cloned.1.call-done, f32[1024,768]{0,1:T(8,128)} %get-tuple-element.86, f32[1024,3072]{1,0:T(8,128)} %get-tuple-element.111, f32[3072]{0:T(1024)S(1)} %slice.152), kind=kOutput, calls=%fused_computation.3 | convolution fusion | flops 4886098944 | bytes 39346176 | tf_op jit(solution)/shard_map/dot_general | solution.py:33
  233.2 10.7 %multiply_reduce_fusion.1 = (f32[768]{0:T(1024)}, f32[1024]{0:T(1024)S(1)}, f32[1024]{0:T(1024)S(1)}, f32[768]{0:T(1024)}, f32[1024,768]{0,1:T(8,128)S(1)}) fusion(f32[1024,768]{0,1:T(8,128)S(1)} %copy-done.5, f32[1024]{0:T(1024)S(1)} %add_rsqrt_fusion.1, f32[1024]{0:T(1024)S(1)} %broadcast_multiply_fusion.4, f32[768]{0:T(1024)S(1)} %get-tuple-element.104, ...), kind=kOutput, calls=%fused_computation.42 | convolution fusion | flops 4839698432 | bytes 20472832 | tf_op jit(solution)/shard_map/dot_general | solution.py:33
  249.1 4.8 convolution_convert_fusion.5.g_ref
  253.9 33.6 %attend_back.1 = bf16[3,1024,768]{2,1,0:T(8,128)(2,1)} custom-call(s32[1,8]{1,0:T(1,128)} %reshape.454.table, bf16[1024,2304]{1,0:T(8,128)(2,1)} %add_convert_fusion.1.q_ref.k_ref.v_ref, bf16[1024,2304]{1,0:T(8,128)(2,1)} %add_convert_fusion.1.q_ref.k_ref.v_ref, bf16[1024,2304]{1,0:T(8,128)(2,1)} %add_convert_fusion.1.q_ref.k_ref.v_ref, ...), custom_call_target="tpu_custom_call" | custom-call | flops 8053063680 | bytes 11010048 | tf_op jit(solution)/shard_map/attend_back/pallas_call | solution.py:226
  287.6 3.5 convolution_convert_fusion.8
  298.9 10.1 %convolution_convert_fusion.1 = bf16[3072,768]{1,0:T(8,128)(2,1)} fusion(bf16[1024,3072]{1,0:T(8,128)(2,1)} %get-tuple-element.94, f32[1024,768]{0,1:T(8,128)} %get-tuple-element.86), kind=kOutput, calls=%fused_computation.22 | convolution fusion | flops 4834983936 | bytes 14155776 | tf_op jit(solution)/shard_map/dot_general | solution.py:33
  309.0 10.2 %convolution_convert_fusion.2 = bf16[3072,768]{1,0:T(8,128)(2,1)} fusion(bf16[1024,3072]{1,0:T(8,128)(2,1)} %get-tuple-element.116, f32[1024,768]{0,1:T(8,128)S(1)} %copy-done.5, f32[768]{0:T(1024)S(1)} %get-tuple-element.103, f32[768]{0:T(1024)S(1)} %get-tuple-element.104, f32[1024]{0:T(1024)S(1)} %add_rsqrt_fusion.1, f32[1024]{0:T(1024)S(1)} %broadcast_multiply_fusion.4), kind=kOutput, calls=%fused_computation.23 | convolution fusion | flops 4838129664 | bytes 14170112 | tf_op jit(solution)/shard_map/dot_general | solution.py:33
  319.3 39.4 %reduce-scatter.17.cloned.1.call-done = bf16[288,768]{1,0:T(8,128)(2,1)} async-done(((bf16[2304,768]{1,0:T(8,128)(2,1)}), bf16[288,768]{1,0:T(8,128)(2,1)}) %reduce-scatter.17.cloned.1.call-update) | async-done | bytes 442384 | tf_op jit(solution)/shard_map/reduce_scatter | solution.py:386
  358.7 57.3 %reduce-scatter.23.cloned.1.call-done = bf16[384,768]{1,0:T(8,128)(2,1)} async-done(((bf16[3072,768]{1,0:T(8,128)(2,1)}), bf16[384,768]{1,0:T(8,128)(2,1)}) %reduce-scatter.23.cloned.1.call-update) | async-done | bytes 589840 | tf_op jit(solution)/shard_map/reduce_scatter | solution.py:386
  415.9 57.3 %reduce-scatter.21.cloned.1.call-done = bf16[384,768]{1,0:T(8,128)(2,1)} async-done(((bf16[3072,768]{1,0:T(8,128)(2,1)}), bf16[384,768]{1,0:T(8,128)(2,1)}) %reduce-scatter.21.cloned.1.call-update) | async-done | bytes 589840 | tf_op jit(solution)/shard_map/reduce_scatter | solution.py:386
  476.0 9.0 convert.21
  485.0 6.3 convert_element_type.260
  491.3 59.4 %all-reduce.4.cloned.1.call-done = bf16[1152,768]{1,0:T(8,128)(2,1)} async-done(((bf16[1152,768]{1,0:T(8,128)(2,1)}), bf16[1152,768]{1,0:T(8,128)(2,1)}) %all-reduce.4.cloned.1.call-update) | async-done | bytes 1769488 | tf_op jit(solution)/shard_map/psum | solution.py:388
  554.3 4.5 fusion.6
  558.8 3.6 copy.103
  563.9 7.8 fusion.7
  571.7 6.6 copy.107
  578.4 7.8 fusion.8
  586.1 6.8 copy.109
  594.8 48.4 %reduce-scatter.25.cloned.1.call-done = bf16[288,768]{1,0:T(8,128)(2,1)} async-done(((bf16[2304,768]{1,0:T(8,128)(2,1)}), bf16[288,768]{1,0:T(8,128)(2,1)}) %reduce-scatter.25.cloned.1.call-update) | async-done | bytes 442384
  644.5 55.8 %reduce-scatter.29.cloned.1.call-done = bf16[384,768]{1,0:T(8,128)(2,1)} async-done(((bf16[3072,768]{1,0:T(8,128)(2,1)}), bf16[384,768]{1,0:T(8,128)(2,1)}) %reduce-scatter.29.cloned.1.call-update) | async-done | bytes 589840
  701.7 55.9 %reduce-scatter.31.cloned.1.call-done = bf16[384,768]{1,0:T(8,128)(2,1)} async-done(((bf16[3072,768]{1,0:T(8,128)(2,1)}), bf16[384,768]{1,0:T(8,128)(2,1)}) %reduce-scatter.31.cloned.1.call-update) | async-done | bytes 589840
  760.9 8.5 divide_convert_fusion
  781.0 7.2 copy.85
  788.7 11.4 %reduce.9 = bf16[1024,768]{1,0:T(8,128)(2,1)} reduce(bf16[1024,1,768]{2,1,0:T(2,128)(2,1)S(1)} %bitcast.131, bf16[]{:T(256)} %broadcast.535), dimensions={1}, to_apply=%bitcast.101.reduce_sub_computation | reduce | bytes 3145730
  800.1 3.7 reshape.477
  803.8 4.7 all-to-all-start.1
  808.5 3.4 fusion.22
  817.5 7.3 copy.91
  824.8 11.4 %reduce.10 = bf16[1024,768]{1,0:T(8,128)(2,1)} reduce(bf16[1024,1,768]{2,1,0:T(2,128)(2,1)S(1)} %bitcast.132, bf16[]{:T(256)} %broadcast.535), dimensions={1}, to_apply=%bitcast.103.reduce_sub_computation | reduce | bytes 3145730
  836.2 3.7 reshape.479
  839.9 5.1 all-to-all-done.1
  845.1 4.4 all-to-all-start.3
  852.0 54.8 %psum.15 = f32[9216]{0:T(1024)S(1)} all-reduce(f32[9216]{0:T(1024)S(1)} %constant_dynamic-update-slice_fusion), channel_id=1, replica_groups=mesh['dp'=8,'seq'=4] {'dp','seq'}, use_global_device_ids=true, to_apply=%region_28.29 | all-reduce | flops 9216 | bytes 73728 | tf_op jit(solution)/shard_map/psum | solution.py:382
  924.9 4.5 fusion.27
  929.4 6.1 fusion.13
  935.5 5.2 fusion.16
  943.6 5.3 copy.94
  (197 shorter events, 99.4 us)
Async XLA Ops:
  7.2 99.6 %all-gather.9.cloned.1.call-start = ((), (), s32[]{:S(2)}) async-start(), calls=%async_computation.12 | async-start | bytes 3981312 | tf_op jit(solution)/shard_map/all_gather | solution.py:300
  13.1 132.4 %all-gather.11.cloned.1.call-start = ((), (), s32[]{:S(2)}) async-start(), calls=%async_computation.13 | async-start | bytes 1327104 | tf_op jit(solution)/shard_map/all_gather | solution.py:300
  13.1 4.1 copy-start.16
  14.8 136.4 %all-gather.13.cloned.1.call-start = ((), (), s32[]{:S(2)}) async-start(), calls=%async_computation.14 | async-start | bytes 5308416 | tf_op jit(solution)/shard_map/all_gather | solution.py:300
  17.2 6.7 copy-start.17
  18.5 41.9 %all-to-all-start.2 = ((bf16[4,256,768]{2,1,0:T(8,128)(2,1)}), bf16[4,256,768]{2,1,0:T(8,128)(2,1)S(1)}, u32[]{:S(2)}, u32[]{:S(2)}) async-start(bf16[4,256,768]{2,1,0:T(8,128)(2,1)} %pad.8), calls=%async_computation.2 | async-start | bytes 3145728 | tf_op jit(solution)/shard_map/all_to_all | solution.py:288
  23.9 41.5 %copy-start.28 = (s32[3,1024]{1,0:T(4,128)S(1)}, s32[3,1024]{1,0:T(4,128)}, u32[]{:S(2)}) copy-start(s32[3,1024]{1,0:T(4,128)} %param.13) | copy-start | bytes 36868
  23.9 41.8 %copy-start.20 = (f32[9216]{0:T(1024)S(1)}, f32[9216]{0:T(1024)}, u32[]{:S(2)}) copy-start(f32[9216]{0:T(1024)} %param.20) | copy-start | bytes 110596
  23.9 42.1 %copy-start = (s32[5]{0:T(128)S(1)}, s32[5]{0:T(128)}, u32[]{:S(2)}) copy-start(s32[5]{0:T(128)} %constant.162.clone) | copy-start | bytes 64
  60.4 7.0 copy-start.3
  60.4 41.0 %all-to-all-start = ((bf16[4,256,768]{2,1,0:T(8,128)(2,1)}), bf16[4,256,768]{2,1,0:T(8,128)(2,1)}, u32[]{:S(2)}, u32[]{:S(2)}) async-start(bf16[4,256,768]{2,1,0:T(8,128)(2,1)} %pad.7), calls=%async_computation | async-start | bytes 3145728 | tf_op jit(solution)/shard_map/all_to_all | solution.py:288
  64.8 124.5 %all-gather.15.cloned.1.call-start = ((), (), s32[]{:S(2)}) async-start(), calls=%async_computation.15 | async-start | bytes 5308416 | tf_op jit(solution)/shard_map/all_gather | solution.py:300
  65.4 253.9 %reduce-scatter.19.cloned.1.call-start = ((), (), s32[]{:S(2)}) async-start(), calls=%async_computation.17 | async-start | bytes 1327104 | tf_op jit(solution)/shard_map/reduce_scatter | solution.py:386
  65.5 49.8 %copy-start.23 = (s32[1,1024]{1,0:T(1,128)}, s32[1,1024]{1,0:T(1,128)S(1)}, u32[]{:S(2)}) copy-start(s32[1,1024]{1,0:T(1,128)S(1)} %fusion.46) | copy-start | bytes 12292
  214.1 19.1 %copy-start.5 = (f32[1024,768]{0,1:T(8,128)S(1)}, f32[1024,768]{0,1:T(8,128)}, u32[]{:S(2)}) copy-start(f32[1024,768]{0,1:T(8,128)} %copy-done.4) | copy-start | bytes 9437188
  243.9 2.8 copy-start.32
  249.1 109.6 %reduce-scatter.17.cloned.1.call-start = ((), (), s32[]{:S(2)}) async-start(), calls=%async_computation.16 | async-start | bytes 3981312 | tf_op jit(solution)/shard_map/reduce_scatter | solution.py:386
  287.6 3.5 copy-start.11
  298.9 117.1 %reduce-scatter.23.cloned.1.call-start = ((), (), s32[]{:S(2)}) async-start(), calls=%async_computation.19 | async-start | bytes 5308416 | tf_op jit(solution)/shard_map/reduce_scatter | solution.py:386
  309.0 164.2 %reduce-scatter.21.cloned.1.call-start = ((), (), s32[]{:S(2)}) async-start(), calls=%async_computation.18 | async-start | bytes 5308416 | tf_op jit(solution)/shard_map/reduce_scatter | solution.py:386
  319.2 231.5 %all-reduce.4.cloned.1.call-start = ((), (), s32[]{:S(2)}) async-start(), calls=%async_computation.20 | async-start | bytes 3538944 | tf_op jit(solution)/shard_map/psum | solution.py:388
  476.0 117.1 %reduce-scatter.27.cloned.1.call-start = ((), (), s32[]{:S(2)}) async-start(), calls=%async_computation.26 | async-start | bytes 1327104
  554.3 88.9 %reduce-scatter.25.cloned.1.call-start = ((), (), s32[]{:S(2)}) async-start(), calls=%async_computation.25 | async-start | bytes 3981312
  562.4 137.9 %reduce-scatter.29.cloned.1.call-start = ((), (), s32[]{:S(2)}) async-start(), calls=%async_computation.27 | async-start | bytes 5308416
  578.3 179.2 %reduce-scatter.31.cloned.1.call-start = ((), (), s32[]{:S(2)}) async-start(), calls=%async_computation.28 | async-start | bytes 5308416
  593.0 329.5 %all-gather.19.cloned.1.call-start = ((), (), s32[]{:S(2)}) async-start(), calls=%async_computation.22 | async-start | bytes 1327104 | tf_op jit(solution)/shard_map/all_gather | solution.py:410
  772.0 152.9 %all-gather.17.cloned.1.call-start = ((), (), s32[]{:S(2)}) async-start(), calls=%async_computation.21 | async-start | bytes 3981312 | tf_op jit(solution)/shard_map/all_gather | solution.py:410
  775.2 154.2 %all-gather.23.cloned.1.call-start = ((), (), s32[]{:S(2)}) async-start(), calls=%async_computation.24 | async-start | bytes 5308416 | tf_op jit(solution)/shard_map/all_gather | solution.py:410
  778.1 157.4 %all-gather.21.cloned.1.call-start = ((), (), s32[]{:S(2)}) async-start(), calls=%async_computation.23 | async-start | bytes 5308416 | tf_op jit(solution)/shard_map/all_gather | solution.py:410
  803.8 8.1 slice-start
  803.8 41.3 %all-to-all-start.1 = ((bf16[4,2,98304]{2,1,0:T(2,128)(2,1)}), bf16[4,2,98304]{2,1,0:T(2,128)(2,1)}, u32[]{:S(2)}, u32[]{:S(2)}) async-start(bf16[4,2,98304]{2,1,0:T(2,128)(2,1)} %reshape.477), calls=%async_computation.1 | async-start | bytes 3145728 | tf_op jit(solution)/shard_map/all_to_all | solution.py:293
  808.5 3.4 slice-start.1
  808.5 4.1 copy-start.19
  836.2 13.3 %copy-start.31 = (f32[768]{0:T(1024)S(1)}, f32[768]{0:T(1024)}, u32[]{:S(2)}) copy-start(f32[768]{0:T(1024)} %get-tuple-element.72) | copy-start | bytes 9220
  836.2 13.3 %copy-start.29 = (f32[768]{0:T(1024)S(1)}, f32[768]{0:T(1024)}, u32[]{:S(2)}) copy-start(f32[768]{0:T(1024)} %get-tuple-element.70) | copy-start | bytes 9220
  836.2 13.3 %copy-start.30 = (f32[768]{0:T(1024)S(1)}, f32[768]{0:T(1024)}, u32[]{:S(2)}) copy-start(f32[768]{0:T(1024)} %get-tuple-element.77) | copy-start | bytes 9220
  836.2 13.3 %copy-start.26 = (f32[768]{0:T(1024)S(1)}, f32[768]{0:T(1024)}, u32[]{:S(2)}) copy-start(f32[768]{0:T(1024)} %get-tuple-element.78) | copy-start | bytes 9220
  839.9 12.0 %copy-start.27 = (f32[768]{0:T(1024)S(1)}, f32[768]{0:T(1024)}, u32[]{:S(2)}) copy-start(f32[768]{0:T(1024)} %get-tuple-element.85) | copy-start | bytes 9220
  839.9 67.5 %copy-start.21 = (f32[9216]{0:T(1024)S(1)}, f32[9216]{0:T(1024)}, u32[]{:S(2)}) copy-start(f32[9216]{0:T(1024)} %param.20) | copy-start | bytes 110596
  839.9 67.5 %copy-start.24 = (f32[9216]{0:T(1024)S(1)}, f32[9216]{0:T(1024)}, u32[]{:S(2)}) copy-start(f32[9216]{0:T(1024)} %param.22) | copy-start | bytes 110596
  839.9 67.5 %copy-start.25 = (f32[9216]{0:T(1024)S(1)}, f32[9216]{0:T(1024)}, u32[]{:S(2)}) copy-start(f32[9216]{0:T(1024)} %param.21) | copy-start | bytes 110596
  845.1 67.5 %all-to-all-start.3 = ((bf16[4,2,98304]{2,1,0:T(2,128)(2,1)}), bf16[4,2,98304]{2,1,0:T(2,128)(2,1)}, u32[]{:S(2)}, u32[]{:S(2)}) async-start(bf16[4,2,98304]{2,1,0:T(2,128)(2,1)} %reshape.479), calls=%async_computation.3 | async-start | bytes 3145728 | tf_op jit(solution)/shard_map/all_to_all | solution.py:293
  915.9 3.3 copy-start.13
  935.4 5.2 copy-start.2
  935.5 5.2 copy-start.14
  935.5 5.2 copy-start.15
  935.5 5.2 copy-start.18
  943.6 5.3 copy-start.8
  (8 other events, 12.7 us)
Sparse Core Ops, SparseCore 0:
  13.2 36.2 all-gather.8
  52.0 23.8 all-gather.10
  78.4 38.7 all-gather.12
  119.5 38.9 all-gather.14
  249.2 40.7 reduce-scatter.18
  299.0 59.6 reduce-scatter.16
  362.1 53.7 reduce-scatter.22
  419.4 53.7 reduce-scatter.20
  476.2 74.4 all-reduce.3
  554.4 36.5 reduce-scatter.26
  595.1 48.0 reduce-scatter.24
  646.5 53.7 reduce-scatter.28
  703.7 53.7 reduce-scatter.30
  772.1 24.4 all-gather.18
  798.3 33.8 all-gather.16
  834.0 39.4 all-gather.22
  875.2 39.2 all-gather.20

commit v2 on v1

--- a/solution.py
+++ b/solution.py
@@ -253,6 +253,493 @@
     )(table, project, project, project, grad, marks_col, marks_row, log_sum)
 
 
+MESH = pl.DeviceIdType.MESH
+ROWS = 48
+
+
+def partners(me):
+    core, along_x, along_y = me % 2, (me // 2) % 2, me // 4
+    side_x = me + 2 - 4 * along_x
+    return (me + 1 - 2 * core, side_x, me + 4 - 8 * along_y, side_x + 4 - 8 * along_y)
+
+
+def send(source, target, send_sem, recv_sem, axis, place):
+    return pltpu.make_async_remote_copy(
+        src_ref=source,
+        dst_ref=target,
+        send_sem=send_sem,
+        recv_sem=recv_sem,
+        device_id={axis: place},
+        device_id_type=MESH,
+    )
+
+
+def greet(peers):
+    barrier = pltpu.get_barrier_semaphore()
+    for axis, place in peers:
+        pl.semaphore_signal(barrier, inc=1, device_id={axis: place}, device_id_type=MESH)
+    pl.semaphore_wait(barrier, len(peers))
+
+
+def owner_rows(owner, width, part):
+    begin = pl.multiple_of(owner * width, 16)
+    if part is None:
+        return pl.ds(begin, width)
+    return pl.ds(pl.multiple_of(begin + part * (width // 2), 16), width // 2)
+
+
+def gather_kernel(widths, starts, shard_ref, *refs):
+    count = len(widths)
+    outs = refs[:count]
+    send_sem, recv_sem, own_sem = refs[count:]
+    me = lax.axis_index("dp")
+    sib, side_x, side_y, across = partners(me)
+    _, sib_x, sib_y, sib_across = partners(sib)
+    greet([("dp", sib), ("dp", side_x), ("dp", side_y)])
+    arrivals = [
+        (side_x, None),
+        (side_y, None),
+        (across, 0),
+        (across, 1),
+        (sib, None),
+        (sib_x, None),
+        (sib_y, None),
+        (sib_across, 0),
+        (sib_across, 1),
+    ]
+    sent = []
+
+    def put(block, kind, slot, source, owner, part, place):
+        copy = send(
+            source,
+            outs[block].at[owner_rows(owner, widths[block], part)],
+            send_sem.at[block, slot],
+            recv_sem.at[block, kind],
+            "dp",
+            place,
+        )
+        copy.start()
+        sent.append(copy)
+
+    def arrived(block, kind):
+        owner, part = arrivals[kind]
+        region = outs[block].at[owner_rows(owner, widths[block], part)]
+        send(region, region, send_sem.at[block, 0], recv_sem.at[block, kind], "dp", sib).wait_recv()
+
+    def forward(block, kind, slot, owner, part, place):
+        region = outs[block].at[owner_rows(owner, widths[block], part)]
+        put(block, kind, slot, region, owner, part, place)
+
+    kept = []
+    for block in range(count):
+        mine = shard_ref.at[pl.ds(starts[block], widths[block])]
+        put(block, 0, 0, mine, me, None, side_x)
+        put(block, 1, 1, mine, me, None, side_y)
+        put(block, 4, 2, mine, me, None, sib)
+        copy = pltpu.make_async_copy(
+            mine, outs[block].at[owner_rows(me, widths[block], None)], own_sem.at[block]
+        )
+        copy.start()
+        kept.append(copy)
+    for step in range(count + 1):
+        if step < count:
+            arrived(step, 0)
+            forward(step, 2, 3, side_x, 0, side_y)
+            forward(step, 5, 4, side_x, None, sib)
+            arrived(step, 1)
+            forward(step, 3, 5, side_y, 1, side_x)
+            forward(step, 6, 6, side_y, None, sib)
+        if step > 0:
+            arrived(step - 1, 2)
+            forward(step - 1, 7, 7, across, 0, sib)
+            arrived(step - 1, 3)
+            forward(step - 1, 8, 8, across, 1, sib)
+    for block in range(count):
+        for kind in range(4, 9):
+            arrived(block, kind)
+    for copy in sent:
+        copy.wait_send()
+    for copy in kept:
+        copy.wait()
+
+
+def plane_gather(shard, widths, starts):
+    count = len(widths)
+    depth = shard.shape[1]
+    return pl.pallas_call(
+        functools.partial(gather_kernel, widths, starts),
+        out_shape=tuple(jax.ShapeDtypeStruct((8 * width, depth), shard.dtype) for width in widths),
+        in_specs=[pl.BlockSpec(memory_space=pltpu.VMEM)],
+        out_specs=tuple(pl.BlockSpec(memory_space=pl.ANY) for _ in widths),
+        scratch_shapes=[
+            pltpu.SemaphoreType.DMA((count, 9)),
+            pltpu.SemaphoreType.DMA((count, 9)),
+            pltpu.SemaphoreType.DMA((count,)),
+        ],
+        compiler_params=pltpu.CompilerParams(
+            collective_id=1, has_side_effects=True, vmem_limit_bytes=16 * 1024 * 1024
+        ),
+        cost_estimate=pl.CostEstimate(
+            flops=0, bytes_accessed=8 * 16 * shard.shape[0] * depth, transcendentals=0
+        ),
+        name="plane_gather",
+    )(shard)
+
+
+def add_rows(target, target_at, terms, count):
+    def step(number, carry):
+        offset = pl.multiple_of(number * ROWS, 16)
+        total = None
+        for ref, begin in terms:
+            value = ref[pl.ds(begin + offset, ROWS), :].astype(jnp.float32)
+            total = value if total is None else total + value
+        target[pl.ds(target_at + offset, ROWS), :] = total.astype(target.dtype)
+        return carry
+
+    lax.fori_loop(0, count // ROWS, step, 0)
+
+
+def reduce_kernel(widths, starts, across_planes, *refs):
+    count = len(widths)
+    share = sum(widths)
+    blocks = refs[:count]
+    refs = refs[count:]
+    if across_planes:
+        small_ref, out_ref, small_out = refs[:3]
+        refs = refs[3:]
+    else:
+        out_ref = refs[0]
+        refs = refs[1:]
+    own, given, from_x, from_y, turn_x, turn_y, total = refs[:7]
+    load_sem, sib_send, sib_recv, link_send, link_recv, out_sem = refs[7:13]
+    refs = refs[13:]
+    if across_planes:
+        low_first, high_first, low_second, final, z_send, z_recv = refs[:6]
+        small_all, small_planes, small_sum, small_send, small_recv, wide_send, wide_recv = refs[6:]
+    me = lax.axis_index("dp")
+    plane = lax.axis_index("seq")
+    sib, side_x, side_y, across = partners(me)
+    _, sib_x, sib_y, sib_across = partners(sib)
+    owners = (me, side_x, side_y, across)
+    sib_owners = (sib, sib_x, sib_y, sib_across)
+    if across_planes:
+        others = [(me + step) % 8 for step in range(1, 8)]
+        planes = [(plane + step) % 4 for step in range(1, 4)]
+        greet([("dp", place) for place in others] + [("seq", place) for place in planes])
+    else:
+        greet([("dp", sib), ("dp", side_x), ("dp", side_y)])
+    order = (3, 1, 2, 0)
+    loads, sends = {}, []
+    for block in range(count):
+        width = widths[block]
+        here = pl.ds(starts[block], width)
+        for which in order:
+            copy = send(
+                blocks[block].at[owner_rows(sib_owners[which], width, None)],
+                given.at[which, here],
+                sib_send.at[block, which],
+                sib_recv.at[block, which],
+                "dp",
+                sib,
+            )
+            copy.start()
+            sends.append(copy)
+            load = pltpu.make_async_copy(
+                blocks[block].at[owner_rows(owners[which], width, None)],
+                own.at[which, here],
+                load_sem.at[block, which],
+            )
+            load.start()
+            loads[block, which] = (load, copy)
+    if across_planes:
+        small_all[me] = small_ref[...]
+        for number, place in enumerate(others):
+            copy = send(
+                small_ref, small_all.at[me], small_send.at[number], small_recv.at[me], "dp", place
+            )
+            copy.start()
+            sends.append(copy)
+
+    def link(block, slot, source, target, place):
+        copy = send(source, target, link_send.at[block, slot], link_recv.at[block, slot], "dp", place)
+        copy.start()
+        sends.append(copy)
+
+    def landed(block, slot, region):
+        send(region, region, link_send.at[block, slot], link_recv.at[block, slot], "dp", sib).wait_recv()
+
+    def upper(block):
+        return (starts[block], widths[block] // 2)
+
+    def lower(block):
+        return (starts[block] + widths[block] // 2, widths[block] // 2)
+
+    def rows_of(part):
+        return pl.ds(part[0], part[1])
+
+    def half_of(block):
+        return pl.ds(starts[block] // 2, widths[block] // 2)
+
+    def pair_sum(block, which):
+        load, copy = loads[block, which]
+        load.wait()
+        copy.wait_recv()
+        add_rows(
+            own.at[which],
+            starts[block],
+            [(own.at[which], starts[block]), (given.at[which], starts[block])],
+            widths[block],
+        )
+
+    def first_stage(block):
+        pair_sum(block, 3)
+        link(block, 0, own.at[3, rows_of(upper(block))], turn_x.at[half_of(block)], side_x)
+        link(block, 1, own.at[3, rows_of(lower(block))], turn_y.at[half_of(block)], side_y)
+        pair_sum(block, 1)
+        link(
+            block, 2, own.at[1, rows_of(upper(block))], from_x.at[rows_of(upper(block))], side_x
+        )
+        pair_sum(block, 2)
+        link(
+            block, 3, own.at[2, rows_of(lower(block))], from_y.at[rows_of(lower(block))], side_y
+        )
+        pair_sum(block, 0)
+
+    def second_stage(block):
+        landed(block, 0, turn_x.at[half_of(block)])
+        begin, size = upper(block)
+        add_rows(own.at[2], begin, [(own.at[2], begin), (turn_x, starts[block] // 2)], size)
+        link(block, 4, own.at[2, rows_of(upper(block))], from_y.at[rows_of(upper(block))], side_y)
+        landed(block, 1, turn_y.at[half_of(block)])
+        begin, size = lower(block)
+        add_rows(own.at[1], begin, [(own.at[1], begin), (turn_y, starts[block] // 2)], size)
+        link(block, 5, own.at[1, rows_of(lower(block))], from_x.at[rows_of(lower(block))], side_x)
+
+    def third_stage(block):
+        landed(block, 2, from_x.at[rows_of(upper(block))])
+        landed(block, 5, from_x.at[rows_of(lower(block))])
+        landed(block, 3, from_y.at[rows_of(lower(block))])
+        landed(block, 4, from_y.at[rows_of(upper(block))])
+        begin = starts[block]
+        add_rows(total, begin, [(own.at[0], begin), (from_x, begin), (from_y, begin)], widths[block])
+
+    stages = [first_stage, second_stage, third_stage]
+    results = total
+    if across_planes:
+        results = final
+
+        def z_copy(block, slot, source, target, place):
+            return send(source, target, z_send.at[block, slot], z_recv.at[block, slot], "seq", place)
+
+        def z_put(block, slot, source, target, place):
+            copy = z_copy(block, slot, source, target, place)
+            copy.start()
+            return copy
+
+        def z_landed(block, slot, region):
+            z_copy(block, slot, region, region, (plane + 1) % 4).wait_recv()
+
+        def fourth_stage(block):
+            up, down, half = rows_of(upper(block)), rows_of(lower(block)), half_of(block)
+
+            @pl.when(plane == 0)
+            def _():
+                z_put(block, 0, total.at[up], low_first.at[half], 1)
+                z_put(block, 1, total.at[down], low_second.at[half], 1)
+
+            @pl.when(plane == 2)
+            def _():
+                z_put(block, 2, total.at[up], high_first.at[half], 1)
+
+        def fifth_stage(block):
+            up, down, half = rows_of(upper(block)), rows_of(lower(block)), half_of(block)
+            middle = starts[block] // 2
+
+            @pl.when(plane == 1)
+            def _():
+                z_landed(block, 0, low_first.at[half])
+                z_landed(block, 2, high_first.at[half])
+                begin, size = upper(block)
+                add_rows(
+                    final, begin, [(total, begin), (low_first, middle), (high_first, middle)], size
+                )
+                z_put(block, 3, final.at[up], final.at[up], 0)
+                z_put(block, 4, final.at[up], final.at[up], 2)
+                z_landed(block, 1, low_second.at[half])
+                begin, size = lower(block)
+                add_rows(total, begin, [(total, begin), (low_second, middle)], size)
+                z_put(block, 5, total.at[down], low_second.at[half], 2)
+
+        def sixth_stage(block):
+            up, down, half = rows_of(upper(block)), rows_of(lower(block)), half_of(block)
+            middle = starts[block] // 2
+
+            @pl.when(plane == 2)
+            def _():
+                z_landed(block, 5, low_second.at[half])
+                begin, size = lower(block)
+                add_rows(final, begin, [(total, begin), (low_second, middle)], size)
+                z_put(block, 6, final.at[down], final.at[down], 1)
+                z_put(block, 7, final.at[down], final.at[down], 3)
+                z_landed(block, 4, final.at[up])
+                z_put(block, 8, final.at[up], final.at[up], 3)
+
+        def seventh_stage(block):
+            down = rows_of(lower(block))
+
+            @pl.when(plane == 1)
+            def _():
+                z_landed(block, 6, final.at[down])
+                z_put(block, 9, final.at[down], final.at[down], 0)
+
+        def eighth_stage(block):
+            up, down, half = rows_of(upper(block)), rows_of(lower(block)), half_of(block)
+
+            @pl.when(plane == 0)
+            def _():
+                z_landed(block, 3, final.at[up])
+                z_landed(block, 9, final.at[down])
+                z_copy(block, 0, total.at[up], low_first.at[half], 1).wait_send()
+                z_copy(block, 1, total.at[down], low_second.at[half], 1).wait_send()
+
+            @pl.when(plane == 1)
+            def _():
+                z_copy(block, 3, final.at[up], final.at[up], 0).wait_send()
+                z_copy(block, 4, final.at[up], final.at[up], 2).wait_send()
+                z_copy(block, 5, total.at[down], low_second.at[half], 2).wait_send()
+                z_copy(block, 9, final.at[down], final.at[down], 0).wait_send()
+
+            @pl.when(plane == 2)
+            def _():
+                z_copy(block, 2, total.at[up], high_first.at[half], 1).wait_send()
+                z_copy(block, 6, final.at[down], final.at[down], 1).wait_send()
+                z_copy(block, 7, final.at[down], final.at[down], 3).wait_send()
+                z_copy(block, 8, final.at[up], final.at[up], 3).wait_send()
+
+            @pl.when(plane == 3)
+            def _():
+                z_landed(block, 7, final.at[down])
+                z_landed(block, 8, final.at[up])
+
+        stages += [fourth_stage, fifth_stage, sixth_stage, seventh_stage, eighth_stage]
+
+    outgoing = []
+
+    def last_stage(block):
+        here = pl.ds(starts[block], widths[block])
+        copy = pltpu.make_async_copy(results.at[here], out_ref.at[here], out_sem.at[block])
+        copy.start()
+        outgoing.append(copy)
+
+    stages.append(last_stage)
+
+    def small_first():
+        for place in others:
+            send(
+                small_ref, small_all.at[place], small_send.at[0], small_recv.at[place], "dp", sib
+            ).wait_recv()
+        total_small = small_all[0]
+        for number in range(1, 8):
+            total_small = total_small + small_all[number]
+        small_sum[...] = total_small
+        small_planes[plane] = total_small
+        for number, place in enumerate(planes):
+            copy = send(
+                small_sum, small_planes.at[plane], wide_send.at[number], wide_recv.at[plane], "seq", place
+            )
+            copy.start()
+            sends.append(copy)
+
+    def small_second():
+        for place in planes:
+            send(
+                small_sum, small_planes.at[place], wide_send.at[0], wide_recv.at[place], "seq", place
+            ).wait_recv()
+        small_out[...] = (small_planes[0] + small_planes[1]) + (small_planes[2] + small_planes[3])
+
+    for tick in range(count + len(stages) - 1):
+        for number in range(len(stages) - 1, -1, -1):
+            block = tick - number
+            if 0 <= block < count:
+                stages[number](block)
+        if across_planes and tick == 1:
+            small_first()
+    if across_planes:
+        small_second()
+    for copy in sends:
+        copy.wait_send()
+    for copy in outgoing:
+        copy.wait()
+
+
+def plane_reduce(terms, widths, starts, small=None):
+    count = len(widths)
+    share = sum(widths)
+    depth = terms[0].shape[1]
+    across_planes = small is not None
+    low = terms[0].dtype
+    whole = pltpu.VMEM((share, depth), low)
+    half = pltpu.VMEM((share // 2, depth), low)
+    dma = pltpu.SemaphoreType.DMA
+    scratch = [
+        pltpu.VMEM((4, share, depth), low),
+        pltpu.VMEM((4, share, depth), low),
+        whole,
+        whole,
+        half,
+        half,
+        whole,
+        dma((count, 4)),
+        dma((count, 4)),
+        dma((count, 4)),
+        dma((count, 6)),
+        dma((count, 6)),
+        dma((count,)),
+    ]
+    any_spec = pl.BlockSpec(memory_space=pl.ANY)
+    vmem_spec = pl.BlockSpec(memory_space=pltpu.VMEM)
+    out_shape = [jax.ShapeDtypeStruct((share, depth), low)]
+    in_specs = [any_spec] * count
+    out_specs = [any_spec]
+    operands = list(terms)
+    if across_planes:
+        scratch += [
+            half,
+            half,
+            half,
+            whole,
+            dma((count, 10)),
+            dma((count, 10)),
+            pltpu.VMEM((8,) + small.shape, small.dtype),
+            pltpu.VMEM((4,) + small.shape, small.dtype),
+            pltpu.VMEM(small.shape, small.dtype),
+            dma((7,)),
+            dma((8,)),
+            dma((3,)),
+            dma((4,)),
+        ]
+        operands.append(small)
+        in_specs.append(vmem_spec)
+        out_specs.append(vmem_spec)
+        out_shape.append(jax.ShapeDtypeStruct(small.shape, small.dtype))
+    return pl.pallas_call(
+        functools.partial(reduce_kernel, widths, starts, across_planes),
+        out_shape=tuple(out_shape),
+        in_specs=in_specs,
+        out_specs=tuple(out_specs),
+        scratch_shapes=scratch,
+        compiler_params=pltpu.CompilerParams(
+            collective_id=2 if across_planes else 3,
+            has_side_effects=True,
+            vmem_limit_bytes=48 * 1024 * 1024,
+        ),
+        cost_estimate=pl.CostEstimate(
+            flops=0, bytes_accessed=8 * 20 * share * depth, transcendentals=0
+        ),
+        name="reduce_all" if across_planes else "plane_reduce",
+    )(*operands)
+
+
 def on_device(
     inputs,
     segments,
@@ -295,10 +782,21 @@
 
     x = to_rows(inputs)
     pull = to_rows(cotangent)
-    low = weights.astype(jnp.bfloat16).T
-    w_qkv, w_out, w_up, w_down = [
-        lax.all_gather(block, "dp", axis=0, tiled=True) for block in blocks_of(low)
-    ]
+    on_plane = owners == 8 and groups == 4 and number == 3
+
+    def gather_blocks(matrix):
+        if on_plane:
+            return plane_gather(matrix, block_widths, block_starts)
+        return [lax.all_gather(block, "dp", axis=0, tiled=True) for block in blocks_of(matrix)]
+
+    def scatter_blocks(terms):
+        if on_plane:
+            return plane_reduce(terms, block_widths, block_starts)[0]
+        return jnp.concatenate(
+            [lax.psum_scatter(term, "dp", scatter_dimension=0, tiled=True) for term in terms], axis=0
+        )
+
+    w_qkv, w_out, w_up, w_down = gather_blocks(weights.astype(jnp.bfloat16).T)
     pieces = [small[index * D : (index + 1) * D] for index in range(8)] + [small[8 * D :]]
     (
         gain_one,
@@ -379,13 +877,15 @@
             grad_bias_up,
         ]
     )
-    small_grad = lax.psum(small_local, ("dp", "seq"))
-
     grads = [grad_qkv, grad_outw, grad_up, grad_down]
-    mine = jnp.concatenate(
-        [lax.psum_scatter(grad, "dp", scatter_dimension=0, tiled=True) for grad in grads], axis=0
-    )
-    mine = lax.psum(mine, "seq")
+    if on_plane:
+        mine, small_grad = plane_reduce(
+            grads, block_widths, block_starts, small_local.reshape(-1, LANES)
+        )
+        small_grad = small_grad.reshape(-1)
+    else:
+        mine = lax.psum(scatter_blocks(grads), "seq")
+        small_grad = lax.psum(small_local, ("dp", "seq"))
     reduced = mine.T.astype(jnp.float32)
     bases_low = bases.astype(jnp.bfloat16)
     rights = [
@@ -395,20 +895,24 @@
         ].astype(jnp.bfloat16)
         for which in range(4)
     ]
-    rotated = []
+    terms = []
     for which, block in enumerate(blocks_of(mine)):
         turned = dot_dims(block, bases_low[which], 1, 0).astype(jnp.bfloat16)
-        term = dot_dims(rights[which], turned, 0, 0).astype(jnp.bfloat16)
-        rotated.append(lax.psum_scatter(term, "dp", scatter_dimension=0, tiled=True))
-    rotated = jnp.concatenate(rotated, axis=0).T.astype(jnp.float32)
+        terms.append(dot_dims(rights[which], turned, 0, 0).astype(jnp.bfloat16))
+    rotated = scatter_blocks(terms).T.astype(jnp.float32)
     first_new, second_new, heading = moments(rotated, first_moment, second_moment)
     heading = heading.astype(jnp.bfloat16)
-    update = []
-    for which in range(4):
-        block = heading[:, block_starts[which] : block_starts[which] + block_widths[which]]
-        step = dot_dims(block, bases_low[which], 0, 1).astype(jnp.bfloat16)
-        every = lax.all_gather(step, "dp", axis=0, tiled=True)
-        update.append(dot_dims(every, rights[which], 0, 1))
+    steps = [
+        dot_dims(
+            heading[:, block_starts[which] : block_starts[which] + block_widths[which]],
+            bases_low[which],
+            0,
+            1,
+        ).astype(jnp.bfloat16)
+        for which in range(4)
+    ]
+    every = gather_blocks(jnp.concatenate(steps, axis=0))
+    update = [dot_dims(every[which], rights[which], 0, 1) for which in range(4)]
     weights_new = weights - learn_rate * jnp.concatenate(update, axis=1)
     small_first_new, small_second_new, small_heading = moments(
         small_grad, small_first, small_second

time: 969 us -> 779 us (0.80)
  waiting for transfers between devices: 447 us -> 50.6 us
  Pallas kernels: 62.8 us -> 374 us
  blocking collectives: 54.8 us -> 0 us
  matrix products: 195 us -> 168 us
  between operations: 15 us -> 1.83 us
    pallas_call x0 -> x4, Pallas kernels: none -> 297 us  [the longest x2 171 us: plane_reduce(): pl.pallas_call(functools.partial(reduce_kernel, widths, starts, across_pl...]
    unnamed x21 -> x0, waiting for transfers between devices: 161 us -> none
    reduce_scatter x4 -> x0, waiting for transfers between devices: 154 us -> none  [on_device(): lax.psum_scatter(grad, 'dp', scatter_dimension=0, tiled=True)]
    psum x1 -> x0, waiting for transfers between devices: 59.4 us -> none  [on_device(): mine = lax.psum(mine, 'seq')]
    psum x1 -> x0, blocking collectives: 54.8 us -> none  [on_device(): small_grad = lax.psum(small_local, ('dp', 'seq'))]
    all_to_all x2, waiting for transfers between devices: 67.5 us -> 35.3 us  [to_rows(): lax.all_to_all(array, 'seq', split_axis=0, concat_axis=1, tiled=True)]
    dot_general x28, matrix products: 195 us -> 168 us  [dot_dims(): lax.dot_general(left, right, (((left_dim,), (right_dim,)), ((), ())), pre...]
    all_to_all x2, waiting for transfers between devices: 5.13 us -> 15.4 us  [to_quarters(): lax.all_to_all(array, 'seq', split_axis=1, concat_axis=0, tiled=True)]
  transfers between devices with their start and end apart: 21 -> 4, of which waited for: 10 -> 2; matrix products, arithmetic and copies ran while one was open for 26% -> 16% of each run, Pallas kernels for 7% -> 25%
where the time goes in v2:
time: 779 us; the launch traced here: 767 us
  Pallas kernels  374 us (48%)
  matrix products  168 us (22%)
  local copies, waits for them, and re-layouts  91.8 us (12%)
  other arithmetic  61 us (8%)
  waiting for transfers between devices  50.6 us (6%)
  starting transfers between devices  19.3 us (2%)
    pallas_call x2, Pallas kernels, plane_reduce(): pl.pallas_call(functools.partial(reduce_kernel, widths, starts, across_pl...  171 us
    dot_general x28, matrix products, dot_dims(): lax.dot_general(left, right, (((left_dim,), (right_dim,)), ((), ())), pre...  168 us
    pallas_call x2, Pallas kernels, plane_gather(): pl.pallas_call(functools.partial(gather_kernel, widths, starts), out_shap...  126 us
    unnamed x117, local copies, waits for them, and re-layouts  59.2 us
    pallas_call x1, Pallas kernels, attend_back(): pl.pallas_call(functools.partial(attend_back_kernel, sizes, tile), out_sh...  41.5 us
    pallas_call x1, Pallas kernels, attend(): pl.pallas_call(functools.partial(attend_kernel, sizes, tile), out_shape=(...  35.5 us
    all_to_all x2, waiting for transfers between devices, to_rows(): lax.all_to_all(array, 'seq', split_axis=0, concat_axis=1, tiled=True)  35.3 us
    unnamed x8, other arithmetic  22.5 us
  transfers between devices with their start and end apart: 4, of which 2 were waited for; matrix products, arithmetic and copies ran while one was open for 16% of the time, Pallas kernels for 25%

profile of v2, /device:TPU:1, one launch (start us, length us, event | category | flops | bytes accessed | tf_op | source)
XLA Modules:
  0.0 766.7 jit_solution(11241179586751196192)
XLA Ops:
  3.3 5.4 all-to-all-start.2
  9.9 35.3 %all-to-all-done.2 = bf16[4,256,768]{2,1,0:T(8,128)(2,1)S(1)} async-done(((bf16[4,256,768]{2,1,0:T(8,128)(2,1)}), bf16[4,256,768]{2,1,0:T(8,128)(2,1)S(1)}, u32[]{:S(2)}, u32[]{:S(2)}) %all-to-all-start.2) | async-done | bytes 1572896 | tf_op jit(solution)/shard_map/all_to_all | solution.py:775
  45.2 4.4 all-to-all-start
  52.2 3.3 copy.117
  57.4 63.6 %plane_gather.2 = (bf16[2304,768]{1,0:T(8,128)(2,1)S(1)}, bf16[768,768]{1,0:T(8,128)(2,1)S(1)}, bf16[3072,768]{1,0:T(8,128)(2,1)S(1)}, bf16[3072,768]{1,0:T(8,128)(2,1)S(1)}) custom-call(bf16[1152,768]{1,0:T(8,128)(2,1)S(1)} %convert_bitcast_fusion.1.shard_ref), custom_call_target="tpu_custom_call" | custom-call | bytes 113246208 | tf_op jit(solution)/shard_map/plane_gather/pallas_call | solution.py:369
  130.4 9.0 %convert.21 = bf16[1152,3072]{1,0:T(8,128)(2,1)} convert(f32[1152,3072]{1,0:T(8,128)} %param.19) | non-fusion elementwise | flops 3538944 | bytes 21233664 | tf_op jit(solution)/shard_map/convert.6
  139.5 6.3 convert_element_type.261
  145.7 5.1 copy.131
  150.9 5.2 copy.126
  158.1 3.1 copy.148
  163.7 7.4 add_convert_fusion.1.q_ref.k_ref.v_ref
  172.1 35.5 %attend.1 = (bf16[1024,768]{1,0:T(8,128)(2,1)}, f32[6,2,1024]{2,1,0:T(2,128)}) custom-call(s32[1,8]{1,0:T(1,128)} %reshape.460.table, bf16[1024,2304]{1,0:T(8,128)(2,1)} %add_convert_fusion.1.q_ref.k_ref.v_ref, bf16[1024,2304]{1,0:T(8,128)(2,1)} %add_convert_fusion.1.q_ref.k_ref.v_ref, bf16[1024,2304]{1,0:T(8,128)(2,1)} %add_convert_fusion.1.q_ref.k_ref.v_ref, ...), custom_call_target="tpu_custom_call" | custom-call | flops 3221225472 | bytes 6291456 | tf_op jit(solution)/shard_map/attend/pallas_call | solution.py:136
  207.6 3.8 fusion.67
  212.3 35.2 %multiply_convert_fusion = (bf16[1024,3072]{1,0:T(8,128)(2,1)S(1)}, f32[1024,3072]{1,0:T(8,128)}, f32[1024,3072]{1,0:T(8,128)}) fusion(f32[3072]{0:T(1024)S(1)} %copy-done.30, bf16[3072,768]{1,0:T(8,128)(2,1)S(1)} %bitcast.132, f32[1024,768]{0,1:T(8,128)S(1)} %get-tuple-element.128, f32[768]{0:T(1024)S(1)} %copy-done.31, f32[768]{0:T(1024)S(1)} %get-tuple-element.122, ...), kind=kOutput, calls=%fused_computation.5 | convolution fusion | flops 5043388416 | bytes 39348224 | tf_op jit(solution)/shard_map/dot_general | solution.py:33
  247.6 5.9 fusion.68
  257.5 3.0 convert_reduce_fusion.1
  260.6 19.0 %convert_reduce_fusion = (f32[3072]{0:T(1024)S(1)}, bf16[1024,3072]{1,0:T(8,128)(2,1)}) fusion(f32[1024,3072]{1,0:T(8,128)} %get-tuple-element.115, bf16[3072,768]{1,0:T(8,128)(2,1)} %copy-done.4, f32[1024,768]{0,1:T(8,128)} %get-tuple-element.111, f32[1024,3072]{1,0:T(8,128)} %get-tuple-element.129, f32[3072]{0:T(1024)S(1)} %copy-done.30), kind=kOutput, calls=%fused_computation.3 | convolution fusion | flops 4886098944 | bytes 39346176 | tf_op jit(solution)/shard_map/dot_general | solution.py:33
  279.6 10.2 %multiply_reduce_fusion.1 = (f32[768]{0:T(1024)S(1)}, f32[1024]{0:T(1024)S(1)}, f32[1024]{0:T(1024)S(1)}, f32[768]{0:T(1024)S(1)}, f32[1024,768]{0,1:T(8,128)S(1)}) fusion(f32[1024,768]{0,1:T(8,128)} %copy-done.16, f32[1024]{0:T(1024)S(1)} %add_rsqrt_fusion.1, f32[1024]{0:T(1024)S(1)} %broadcast_multiply_fusion.4, f32[768]{0:T(1024)S(1)} %get-tuple-element.122, ...), kind=kOutput, calls=%fused_computation.42 | convolution fusion | flops 4839698432 | bytes 20472832 | tf_op jit(solution)/shard_map/dot_general | solution.py:33
  293.8 41.5 %attend_back.1 = bf16[3,1024,768]{2,1,0:T(8,128)(2,1)} custom-call(s32[1,8]{1,0:T(1,128)} %reshape.460.table, bf16[1024,2304]{1,0:T(8,128)(2,1)} %add_convert_fusion.1.q_ref.k_ref.v_ref, bf16[1024,2304]{1,0:T(8,128)(2,1)} %add_convert_fusion.1.q_ref.k_ref.v_ref, bf16[1024,2304]{1,0:T(8,128)(2,1)} %add_convert_fusion.1.q_ref.k_ref.v_ref, ...), custom_call_target="tpu_custom_call" | custom-call | flops 8053063680 | bytes 11010048 | tf_op jit(solution)/shard_map/attend_back/pallas_call | solution.py:226
  335.3 4.6 fusion.22
  339.9 3.1 fusion.23
  348.7 3.0 convolution_convert_fusion.10
  354.5 7.5 convolution_convert_fusion.2.refs_2_
  362.0 7.2 convolution_convert_fusion.1.refs_3_
  372.1 103.8 %reduce_all.1 = (bf16[1152,768]{1,0:T(8,128)(2,1)S(1)}, f32[72,128]{1,0:T(8,128)S(1)}) custom-call(bf16[2304,768]{1,0:T(8,128)(2,1)} %pad_maximum_fusion.refs_0_, bf16[768,768]{1,0:T(8,128)(2,1)S(1)} %convolution_convert_fusion.7.refs_1_, bf16[3072,768]{1,0:T(8,128)(2,1)} %convolution_convert_fusion.2.refs_2_, ...), custom_call_target="tpu_custom_call" | custom-call | bytes 141557760 | tf_op jit(solution)/shard_map/reduce_all/pallas_call | solution.py:725
  478.0 6.0 fusion.6.refs_0_
  486.0 7.5 fusion.7.refs_2_
  493.5 7.4 fusion.8.refs_3_
  501.0 8.7 %copy.119 = bf16[1,1024,768]{2,0,1:T(2,128)(2,1)} copy(bf16[1,1024,768]{1,2,0:T(8,128)(2,1)} %get-tuple-element.118) | data formatting | bytes 3145728 | tf_op jit(solution)/shard_map/reshape | solution.py:779
  510.2 11.2 %reduce.9 = bf16[1024,768]{1,0:T(8,128)(2,1)S(1)} reduce(bf16[1024,1,768]{2,1,0:T(2,128)(2,1)} %bitcast.136, bf16[]{:T(256)} %broadcast.535), dimensions={1}, to_apply=%bitcast.99.reduce_sub_computation | reduce | bytes 3145730
  523.3 4.5 all-to-all-start.1
  527.8 6.2 fusion.20
  534.0 5.5 copy.125
  539.5 11.2 %reduce.10 = bf16[1024,768]{1,0:T(8,128)(2,1)S(1)} reduce(bf16[1024,1,768]{2,1,0:T(2,128)(2,1)} %bitcast.137, bf16[]{:T(256)} %broadcast.535), dimensions={1}, to_apply=%bitcast.101.reduce_sub_computation | reduce | bytes 3145730
  552.6 5.2 copy.133
  557.8 67.7 %plane_reduce.1 = bf16[1152,768]{1,0:T(8,128)(2,1)S(1)} custom-call(bf16[2304,768]{1,0:T(8,128)(2,1)} %fusion.6.refs_0_, bf16[768,768]{1,0:T(8,128)(2,1)S(1)} %fusion.21.refs_1_, bf16[3072,768]{1,0:T(8,128)(2,1)} %fusion.7.refs_2_, bf16[3072,768]{1,0:T(8,128)(2,1)} %fusion.8.refs_3_), custom_call_target="tpu_custom_call" | custom-call | bytes 141557760 | tf_op jit(solution)/shard_map/plane_reduce/pallas_call | solution.py:725
  625.5 5.5 divide_convert_fusion
  631.0 5.2 copy.134
  636.2 5.2 copy.135
  648.9 62.3 %plane_gather.3 = (bf16[2304,768]{1,0:T(8,128)(2,1)S(1)}, bf16[768,768]{1,0:T(8,128)(2,1)S(1)}, bf16[3072,768]{1,0:T(8,128)(2,1)S(1)}, bf16[3072,768]{1,0:T(8,128)(2,1)S(1)}) custom-call(bf16[1152,768]{1,0:T(8,128)(2,1)S(1)} %pad_maximum_fusion.1.shard_ref), custom_call_target="tpu_custom_call" | custom-call | bytes 113246208 | tf_op jit(solution)/shard_map/plane_gather/pallas_call | solution.py:369
  711.2 4.4 fusion.27
  715.6 3.7 fusion.13
  719.4 5.1 all-to-all-start.3
  725.7 5.2 fusion.16
  733.4 5.2 copy.136
  741.4 3.0 reshape.478
  745.8 15.4 %all-to-all-done.3 = bf16[4,2,98304]{2,1,0:T(2,128)(2,1)} async-done(((bf16[4,2,98304]{2,1,0:T(2,128)(2,1)}), bf16[4,2,98304]{2,1,0:T(2,128)(2,1)}, u32[]{:S(2)}, u32[]{:S(2)}) %all-to-all-start.3) | async-done | bytes 1572896 | tf_op jit(solution)/shard_map/all_to_all | solution.py:780
  761.2 3.1 reshape.480
  (167 shorter events, 69.3 us)
Async XLA Ops:
  0.6 8.0 %copy-start.23 = (bf16[3,256,768]{2,1,0:T(8,128)(2,1)S(1)}, bf16[3,256,768]{2,1,0:T(8,128)(2,1)}, u32[]{:S(2)}) copy-start(bf16[3,256,768]{2,1,0:T(8,128)(2,1)} %param.12) | copy-start | bytes 3538948
  3.3 41.9 %all-to-all-start.2 = ((bf16[4,256,768]{2,1,0:T(8,128)(2,1)}), bf16[4,256,768]{2,1,0:T(8,128)(2,1)S(1)}, u32[]{:S(2)}, u32[]{:S(2)}) async-start(bf16[4,256,768]{2,1,0:T(8,128)(2,1)} %pad.8), calls=%async_computation.2 | async-start | bytes 3145728 | tf_op jit(solution)/shard_map/all_to_all | solution.py:775
  8.7 40.9 %copy-start.29 = (s32[3,1024]{1,0:T(4,128)S(1)}, s32[3,1024]{1,0:T(4,128)}, u32[]{:S(2)}) copy-start(s32[3,1024]{1,0:T(4,128)} %param.13) | copy-start | bytes 36868
  45.2 5.7 copy-start.12
  45.2 116.0 %all-to-all-start = ((bf16[4,256,768]{2,1,0:T(8,128)(2,1)}), bf16[4,256,768]{2,1,0:T(8,128)(2,1)}, u32[]{:S(2)}, u32[]{:S(2)}) async-start(bf16[4,256,768]{2,1,0:T(8,128)(2,1)} %pad.7), calls=%async_computation | async-start | bytes 3145728 | tf_op jit(solution)/shard_map/all_to_all | solution.py:775
  49.6 121.5 %copy-start.26 = (s32[1,1024]{1,0:T(1,128)}, s32[1,1024]{1,0:T(1,128)S(1)}, u32[]{:S(2)}) copy-start(s32[1,1024]{1,0:T(1,128)S(1)} %fusion.46) | copy-start | bytes 12292
  55.5 1.7 copy-start.9
  57.2 69.1 %copy-start.34 = (s32[1,4]{1,0:T(1,128)S(1)}, s32[1,4]{1,0:T(1,128)}, u32[]{:S(2)}) copy-start(s32[1,4]{1,0:T(1,128)} %slice.128) | copy-start | bytes 52
  57.2 69.1 %copy-start.35 = (s32[1,4]{1,0:T(1,128)S(1)}, s32[1,4]{1,0:T(1,128)}, u32[]{:S(2)}) copy-start(s32[1,4]{1,0:T(1,128)} %slice.130) | copy-start | bytes 52
  57.2 70.1 %copy-start.8 = (s32[5]{0:T(128)S(1)}, s32[5]{0:T(128)}, u32[]{:S(2)}) copy-start(s32[5]{0:T(128)} %constant.162.clone) | copy-start | bytes 64
  121.0 2.2 copy-start.3
  123.1 2.2 copy-start.4
  125.3 1.0 copy-start.6
  126.3 37.4 %copy-start = (bf16[2304,768]{1,0:T(8,128)(2,1)}, bf16[2304,768]{1,0:T(8,128)(2,1)S(1)}, u32[]{:S(2)}) copy-start(bf16[2304,768]{1,0:T(8,128)(2,1)S(1)} %get-tuple-element.23) | copy-start | bytes 10616836
  172.1 35.5 %copy-start.33 = (f32[768]{0:T(1024)S(1)}, f32[768]{0:T(1024)}, u32[]{:S(2)}) copy-start(f32[768]{0:T(1024)} %get-tuple-element.123) | copy-start | bytes 9220
  207.6 4.3 slice-start
  207.6 4.3 slice-start.1
  207.6 39.9 %slice-start.2 = ((s8[4718592]{0:T(1024)(128)(4,1)}), s8[4194304]{0:T(1024)(128)(4,1)S(1)}, s32[]{:S(2)}) async-start(s8[4718592]{0:T(1024)(128)(4,1)} %bitcast.133), calls=%async_computation.6 | async-start | bytes 8388608
  211.5 36.1 %copy-start.16 = (f32[1024,768]{0,1:T(8,128)}, f32[1024,768]{0,1:T(8,128)S(1)}, u32[]{:S(2)}) copy-start(f32[1024,768]{0,1:T(8,128)S(1)} %get-tuple-element.128) | copy-start | bytes 9437188
  211.5 0.8 copy-start.31
  212.3 35.2 %slice-start.3 = ((s8[4718592]{0:T(1024)(128)(4,1)}), s8[524288]{0:T(1024)(128)(4,1)S(1)}, s32[]{:S(2)}) async-start(s8[4718592]{0:T(1024)(128)(4,1)} %bitcast.133), calls=%async_computation.7 | async-start | bytes 1048576
  212.3 35.2 %copy-start.32 = (f32[768]{0:T(1024)S(1)}, f32[768]{0:T(1024)}, u32[]{:S(2)}) copy-start(f32[768]{0:T(1024)} %get-tuple-element.120) | copy-start | bytes 9220
  247.5 5.9 copy-start.37
  253.5 1.9 copy-start.11
  255.4 1.4 copy-start.13
  279.6 10.2 %copy-start.17 = (f32[1024,768]{0,1:T(8,128)S(1)}, f32[1024,768]{0,1:T(8,128)}, u32[]{:S(2)}) copy-start(f32[1024,768]{0,1:T(8,128)} %copy-done.16) | copy-start | bytes 9437188
  289.8 1.3 copy-start.7
  291.0 2.8 copy-start.19
  293.8 41.5 %copy-start.1 = (bf16[2304,768]{1,0:T(8,128)(2,1)S(1)}, bf16[2304,768]{1,0:T(8,128)(2,1)}, u32[]{:S(2)}) copy-start(bf16[2304,768]{1,0:T(8,128)(2,1)} %copy-done) | copy-start | bytes 10616836
  335.2 4.6 copy-start.21
  348.7 3.1 copy-start.20
  348.7 3.1 copy-start.36
  348.7 4.5 slice-start.4
  351.7 2.1 copy-start.18
  351.7 2.7 slice-start.5
  351.8 10.3 %slice-start.6 = ((s8[6291456]{0:T(1024)(128)(4,1)}), s8[4194304]{0:T(1024)(128)(4,1)S(1)}, s32[]{:S(2)}) async-start(s8[6291456]{0:T(1024)(128)(4,1)} %bitcast.151), calls=%async_computation.10 | async-start | bytes 8388608
  354.5 7.5 copy-start.22
  354.5 7.5 slice-start.7
  523.3 196.1 %all-to-all-start.1 = ((bf16[4,2,98304]{2,1,0:T(2,128)(2,1)}), bf16[4,2,98304]{2,1,0:T(2,128)(2,1)}, u32[]{:S(2)}, u32[]{:S(2)}) async-start(bf16[4,2,98304]{2,1,0:T(2,128)(2,1)} %reshape.477), calls=%async_computation.1 | async-start | bytes 3145728 | tf_op jit(solution)/shard_map/all_to_all | solution.py:780
  557.8 67.7 %copy-start.14 = (f32[768,1152]{0,1:T(8,128)S(1)}, f32[768,1152]{0,1:T(8,128)}, u32[]{:S(2)}) copy-start(f32[768,1152]{0,1:T(8,128)} %copy.131) | copy-start | bytes 10616836
  557.8 67.7 %copy-start.15 = (f32[768,1152]{0,1:T(8,128)S(1)}, f32[768,1152]{0,1:T(8,128)}, u32[]{:S(2)}) copy-start(f32[768,1152]{0,1:T(8,128)} %copy.126) | copy-start | bytes 10616836
  711.2 4.4 copy-start.5
  719.4 41.9 %all-to-all-start.3 = ((bf16[4,2,98304]{2,1,0:T(2,128)(2,1)}), bf16[4,2,98304]{2,1,0:T(2,128)(2,1)}, u32[]{:S(2)}, u32[]{:S(2)}) async-start(bf16[4,2,98304]{2,1,0:T(2,128)(2,1)} %reshape.479), calls=%async_computation.3 | async-start | bytes 3145728 | tf_op jit(solution)/shard_map/all_to_all | solution.py:780
  725.7 5.2 copy-start.10
  725.7 5.2 copy-start.24
  738.6 2.2 copy-start.25
  738.6 2.2 copy-start.27
  738.6 2.2 copy-start.28
  (2 other events, 1.6 us)

commit v3 on v2

--- a/solution.py
+++ b/solution.py
@@ -281,21 +281,26 @@
     pl.semaphore_wait(barrier, len(peers))
 
 
-def owner_rows(owner, width, part):
-    begin = pl.multiple_of(owner * width, 16)
-    if part is None:
-        return pl.ds(begin, width)
-    return pl.ds(pl.multiple_of(begin + part * (width // 2), 16), width // 2)
-
-
-def gather_kernel(widths, starts, shard_ref, *refs):
+def gather_kernel(widths, starts, places, moves, shard_ref, *refs):
     count = len(widths)
-    outs = refs[:count]
-    send_sem, recv_sem, own_sem = refs[count:]
+    moved_in = refs[: len(moves)]
+    refs = refs[len(moves) :]
+    arrays = 1 + max(number for number, _ in places)
+    outs = refs[:arrays]
+    moved_out = refs[arrays : arrays + len(moves)]
+    refs = refs[arrays + len(moves) :]
+    send_sem, recv_sem, own_sem = refs[:3]
     me = lax.axis_index("dp")
     sib, side_x, side_y, across = partners(me)
     _, sib_x, sib_y, sib_across = partners(sib)
-    greet([("dp", sib), ("dp", side_x), ("dp", side_y)])
+    peers = [("dp", sib), ("dp", side_x), ("dp", side_y)]
+    if moves:
+        z_send, z_recv, z_own, zeros_ref = refs[3:]
+        plane = lax.axis_index("seq")
+        planes = [(plane + step) % 4 for step in range(1, 4)]
+        peers += [("seq", place) for place in planes]
+        zeros_ref[...] = jnp.zeros_like(zeros_ref)
+    greet(peers)
     arrivals = [
         (side_x, None),
         (side_y, None),
@@ -309,10 +314,20 @@
     ]
     sent = []
 
+    def rows_at(block, owner, part):
+        number, first = places[block]
+        width = widths[block]
+        begin = first + owner * width
+        size = width
+        if part is not None:
+            size = width // 2
+            begin = begin + part * size
+        return outs[number].at[pl.ds(pl.multiple_of(begin, 16), size)]
+
     def put(block, kind, slot, source, owner, part, place):
         copy = send(
             source,
-            outs[block].at[owner_rows(owner, widths[block], part)],
+            rows_at(block, owner, part),
             send_sem.at[block, slot],
             recv_sem.at[block, kind],
             "dp",
@@ -323,22 +338,95 @@
 
     def arrived(block, kind):
         owner, part = arrivals[kind]
-        region = outs[block].at[owner_rows(owner, widths[block], part)]
+        region = rows_at(block, owner, part)
         send(region, region, send_sem.at[block, 0], recv_sem.at[block, kind], "dp", sib).wait_recv()
 
     def forward(block, kind, slot, owner, part, place):
-        region = outs[block].at[owner_rows(owner, widths[block], part)]
-        put(block, kind, slot, region, owner, part, place)
-
+        put(block, kind, slot, rows_at(block, owner, part), owner, part, place)
+
+    def each_move(number, act_send, act_own, act_recv):
+        source, target = moved_in[number], moved_out[number]
+        if moves[number] == "in":
+            quarter = source.shape[1]
+            part = lambda place: target.at[pl.ds(pl.multiple_of(place * quarter, 16), quarter)]
+            for row in range(3):
+
+                @pl.when(plane != row)
+                def _(row=row):
+                    act_send(
+                        send(
+                            source.at[row],
+                            part(plane),
+                            z_send.at[number, row],
+                            z_recv.at[number, plane],
+                            "seq",
+                            row,
+                        )
+                    )
+
+                @pl.when(plane == row)
+                def _(row=row):
+                    act_own(pltpu.make_async_copy(source.at[row], part(plane), z_own.at[number, 0]))
+                    for place in planes if act_recv else ():
+                        act_recv(
+                            send(
+                                source.at[row],
+                                part(place),
+                                z_send.at[number, row],
+                                z_recv.at[number, place],
+                                "seq",
+                                place,
+                            )
+                        )
+
+            @pl.when(plane == 3)
+            def _():
+                for place in range(4):
+                    act_own(pltpu.make_async_copy(zeros_ref, part(place), z_own.at[number, place]))
+
+        else:
+            quarter = target.shape[1]
+            part = lambda place: source.at[pl.ds(pl.multiple_of(place * quarter, 16), quarter)]
+
+            @pl.when(plane < 3)
+            def _():
+                for step, place in enumerate(planes):
+                    act_send(
+                        send(
+                            part(place),
+                            target.at[plane],
+                            z_send.at[number, step],
+                            z_recv.at[number, plane],
+                            "seq",
+                            place,
+                        )
+                    )
+                act_own(pltpu.make_async_copy(part(plane), target.at[plane], z_own.at[number, 0]))
+
+            for row in range(3) if act_recv else ():
+
+                @pl.when(plane != row)
+                def _(row=row):
+                    act_recv(
+                        send(
+                            part(plane),
+                            target.at[row],
+                            z_send.at[number, 0],
+                            z_recv.at[number, row],
+                            "seq",
+                            row,
+                        )
+                    )
+
+    for number in range(len(moves)):
+        each_move(number, lambda copy: copy.start(), lambda copy: copy.start(), None)
     kept = []
     for block in range(count):
         mine = shard_ref.at[pl.ds(starts[block], widths[block])]
         put(block, 0, 0, mine, me, None, side_x)
         put(block, 1, 1, mine, me, None, side_y)
         put(block, 4, 2, mine, me, None, sib)
-        copy = pltpu.make_async_copy(
-            mine, outs[block].at[owner_rows(me, widths[block], None)], own_sem.at[block]
-        )
+        copy = pltpu.make_async_copy(mine, rows_at(block, me, None), own_sem.at[block])
         copy.start()
         kept.append(copy)
     for step in range(count + 1):
@@ -361,29 +449,54 @@
         copy.wait_send()
     for copy in kept:
         copy.wait()
-
-
-def plane_gather(shard, widths, starts):
+    for number in range(len(moves)):
+        each_move(
+            number,
+            lambda copy: copy.wait_send(),
+            lambda copy: copy.wait(),
+            lambda copy: copy.wait_recv(),
+        )
+
+
+def plane_gather(shard, widths, starts, joined, moves=(), arrays=(), length=0):
     count = len(widths)
     depth = shard.shape[1]
+    if joined:
+        places = [(0, 8 * start) for start in starts]
+        out_shape = [jax.ShapeDtypeStruct((8 * sum(widths), depth), shard.dtype)]
+    else:
+        places = [(number, 0) for number in range(count)]
+        out_shape = [jax.ShapeDtypeStruct((8 * width, depth), shard.dtype) for width in widths]
+    scratch = [
+        pltpu.SemaphoreType.DMA((count, 9)),
+        pltpu.SemaphoreType.DMA((count, 9)),
+        pltpu.SemaphoreType.DMA((count,)),
+    ]
+    if moves:
+        quarter = length // 4
+        for kind in moves:
+            shape = (length, depth) if kind == "in" else (3, quarter, depth)
+            out_shape.append(jax.ShapeDtypeStruct(shape, shard.dtype))
+        scratch += [
+            pltpu.SemaphoreType.DMA((len(moves), 3)),
+            pltpu.SemaphoreType.DMA((len(moves), 4)),
+            pltpu.SemaphoreType.DMA((len(moves), 4)),
+            pltpu.VMEM((quarter, depth), shard.dtype),
+        ]
     return pl.pallas_call(
-        functools.partial(gather_kernel, widths, starts),
-        out_shape=tuple(jax.ShapeDtypeStruct((8 * width, depth), shard.dtype) for width in widths),
-        in_specs=[pl.BlockSpec(memory_space=pltpu.VMEM)],
-        out_specs=tuple(pl.BlockSpec(memory_space=pl.ANY) for _ in widths),
-        scratch_shapes=[
-            pltpu.SemaphoreType.DMA((count, 9)),
-            pltpu.SemaphoreType.DMA((count, 9)),
-            pltpu.SemaphoreType.DMA((count,)),
-        ],
+        functools.partial(gather_kernel, widths, starts, places, moves),
+        out_shape=tuple(out_shape),
+        in_specs=[pl.BlockSpec(memory_space=pltpu.VMEM)] * (1 + len(moves)),
+        out_specs=tuple(pl.BlockSpec(memory_space=pl.ANY) for _ in out_shape),
+        scratch_shapes=scratch,
         compiler_params=pltpu.CompilerParams(
-            collective_id=1, has_side_effects=True, vmem_limit_bytes=16 * 1024 * 1024
+            collective_id=4 if joined else 1, has_side_effects=True, vmem_limit_bytes=16 * 1024 * 1024
         ),
         cost_estimate=pl.CostEstimate(
             flops=0, bytes_accessed=8 * 16 * shard.shape[0] * depth, transcendentals=0
         ),
-        name="plane_gather",
-    )(shard)
+        name="gather_steps" if joined else "gather_weights",
+    )(shard, *arrays)
 
 
 def add_rows(target, target_at, terms, count):
@@ -399,11 +512,11 @@
     lax.fori_loop(0, count // ROWS, step, 0)
 
 
-def reduce_kernel(widths, starts, across_planes, *refs):
+def reduce_kernel(widths, starts, places, across_planes, *refs):
     count = len(widths)
-    share = sum(widths)
-    blocks = refs[:count]
-    refs = refs[count:]
+    arrays = 1 + max(number for number, _ in places)
+    blocks = refs[:arrays]
+    refs = refs[arrays:]
     if across_planes:
         small_ref, out_ref, small_out = refs[:3]
         refs = refs[3:]
@@ -430,12 +543,18 @@
         greet([("dp", sib), ("dp", side_x), ("dp", side_y)])
     order = (3, 1, 2, 0)
     loads, sends = {}, []
+
+    def block_rows(block, owner):
+        number, first = places[block]
+        begin = pl.multiple_of(first + owner * widths[block], 16)
+        return blocks[number].at[pl.ds(begin, widths[block])]
+
     for block in range(count):
         width = widths[block]
         here = pl.ds(starts[block], width)
         for which in order:
             copy = send(
-                blocks[block].at[owner_rows(sib_owners[which], width, None)],
+                block_rows(block, sib_owners[which]),
                 given.at[which, here],
                 sib_send.at[block, which],
                 sib_recv.at[block, which],
@@ -445,7 +564,7 @@
             copy.start()
             sends.append(copy)
             load = pltpu.make_async_copy(
-                blocks[block].at[owner_rows(owners[which], width, None)],
+                block_rows(block, owners[which]),
                 own.at[which, here],
                 load_sem.at[block, which],
             )
@@ -677,6 +796,10 @@
     share = sum(widths)
     depth = terms[0].shape[1]
     across_planes = small is not None
+    if len(terms) == 1:
+        places = [(0, 8 * start) for start in starts]
+    else:
+        places = [(number, 0) for number in range(count)]
     low = terms[0].dtype
     whole = pltpu.VMEM((share, depth), low)
     half = pltpu.VMEM((share // 2, depth), low)
@@ -699,7 +822,7 @@
     any_spec = pl.BlockSpec(memory_space=pl.ANY)
     vmem_spec = pl.BlockSpec(memory_space=pltpu.VMEM)
     out_shape = [jax.ShapeDtypeStruct((share, depth), low)]
-    in_specs = [any_spec] * count
+    in_specs = [any_spec] * len(terms)
     out_specs = [any_spec]
     operands = list(terms)
     if across_planes:
@@ -723,7 +846,7 @@
         out_specs.append(vmem_spec)
         out_shape.append(jax.ShapeDtypeStruct(small.shape, small.dtype))
     return pl.pallas_call(
-        functools.partial(reduce_kernel, widths, starts, across_planes),
+        functools.partial(reduce_kernel, widths, starts, places, across_planes),
         out_shape=tuple(out_shape),
         in_specs=in_specs,
         out_specs=tuple(out_specs),
@@ -738,6 +861,159 @@
         ),
         name="reduce_all" if across_planes else "plane_reduce",
     )(*operands)
+
+
+def basis_specs():
+    return [
+        pl.BlockSpec((1, D, D), lambda g: (g + jnp.minimum(g, 1), 0, 0)),
+        pl.BlockSpec((1, D, D), lambda g: (1, 0, 0)),
+    ]
+
+
+def low_of(value):
+    return value.astype(jnp.bfloat16)
+
+
+def turn_kernel(joint, grad_ref, basis_ref, basis_out_ref, right_ref, reduced_ref, term_ref):
+    group = pl.program_id(0)
+    grad = grad_ref[...]
+    reduced_ref[...] = grad.astype(jnp.float32).T
+    basis = low_of(basis_ref[0])
+
+    def spread(rows, turned, begin, columns):
+        for step in range(columns // D):
+            right = low_of(right_ref[rows, step * D : (step + 1) * D].T)
+            term_ref[begin + step * D : begin + (step + 1) * D, :] = low_of(
+                jnp.dot(right, turned, preferred_element_type=jnp.float32)
+            )
+
+    @pl.when(group == 0)
+    def _():
+        turned = low_of(jnp.dot(grad[:joint], basis, preferred_element_type=jnp.float32))
+        spread(slice(0, joint), turned, 0, 3 * D)
+        other = low_of(basis_out_ref[0])
+        turned = low_of(jnp.dot(grad[joint:], other, preferred_element_type=jnp.float32))
+        spread(slice(joint, grad.shape[0]), turned, 3 * D, D)
+
+    @pl.when(group != 0)
+    def _():
+        turned = low_of(jnp.dot(grad, basis, preferred_element_type=jnp.float32))
+        spread(slice(None), turned, 0, FF)
+
+
+def turn(grad, bases, right_bases, joint):
+    share = grad.shape[0]
+    part = share // 3
+    return pl.pallas_call(
+        functools.partial(turn_kernel, joint),
+        grid=(3,),
+        out_shape=(
+            jax.ShapeDtypeStruct((D, share), jnp.float32),
+            jax.ShapeDtypeStruct((3 * FF, D), jnp.bfloat16),
+        ),
+        in_specs=[pl.BlockSpec((part, D), lambda g: (g, 0))]
+        + basis_specs()
+        + [pl.BlockSpec((part, FF), lambda g: (g, 0))],
+        out_specs=(
+            pl.BlockSpec((D, part), lambda g: (0, g)),
+            pl.BlockSpec((FF, D), lambda g: (g, 0)),
+        ),
+        compiler_params=pltpu.CompilerParams(vmem_limit_bytes=VMEM_LIMIT),
+        cost_estimate=pl.CostEstimate(
+            flops=2 * share * D * (D + FF), bytes_accessed=4 * share * (FF + D) + 6 * FF * D, transcendentals=0
+        ),
+        name="turn",
+    )(grad, bases, bases, right_bases)
+
+
+def adam_kernel(
+    joint, rotated_ref, first_ref, second_ref, basis_ref, basis_out_ref, first_out, second_out, step_ref
+):
+    group = pl.program_id(0)
+    rotated = rotated_ref[...].astype(jnp.float32).T
+    first, second, heading = moments(rotated, first_ref[...], second_ref[...])
+    first_out[...] = first
+    second_out[...] = second
+    heading = low_of(heading.T)
+    basis = low_of(basis_ref[0])
+
+    @pl.when(group == 0)
+    def _():
+        other = low_of(basis_out_ref[0])
+        step_ref[:joint, :] = low_of(dot_dims(heading[:joint], basis, 1, 1))
+        step_ref[joint:, :] = low_of(dot_dims(heading[joint:], other, 1, 1))
+
+    @pl.when(group != 0)
+    def _():
+        step_ref[...] = low_of(dot_dims(heading, basis, 1, 1))
+
+
+def adam(rotated, first_moment, second_moment, bases, joint):
+    share = rotated.shape[0]
+    part = share // 3
+    rows = pl.BlockSpec((part, D), lambda g: (g, 0))
+    columns = pl.BlockSpec((D, part), lambda g: (0, g))
+    wide = jax.ShapeDtypeStruct((D, share), jnp.float32)
+    return pl.pallas_call(
+        functools.partial(adam_kernel, joint),
+        grid=(3,),
+        out_shape=(wide, wide, jax.ShapeDtypeStruct((share, D), jnp.bfloat16)),
+        in_specs=[rows, columns, columns] + basis_specs(),
+        out_specs=(columns, columns, rows),
+        compiler_params=pltpu.CompilerParams(vmem_limit_bytes=VMEM_LIMIT),
+        cost_estimate=pl.CostEstimate(
+            flops=2 * share * D * D, bytes_accessed=20 * share * D, transcendentals=share * D
+        ),
+        name="adam",
+    )(rotated, first_moment, second_moment, bases, bases)
+
+
+def update_kernel(joint, every_ref, right_ref, weights_ref, new_ref, low_ref):
+    group = pl.program_id(0)
+
+    def finish(update):
+        new = weights_ref[...] - learn_rate * update.T
+        new_ref[...] = new
+        low_ref[...] = low_of(new)
+
+    @pl.when(group == 0)
+    def _():
+        upper = jnp.dot(
+            low_of(right_ref[:joint, : 3 * D]), every_ref[: 3 * D, :], preferred_element_type=jnp.float32
+        )
+        lower = jnp.dot(
+            low_of(right_ref[joint:, :D]), every_ref[3 * D :, :], preferred_element_type=jnp.float32
+        )
+        finish(jnp.concatenate([upper, lower], axis=0))
+
+    @pl.when(group != 0)
+    def _():
+        finish(jnp.dot(low_of(right_ref[...]), every_ref[...], preferred_element_type=jnp.float32))
+
+
+def apply_update(every, right_bases, weights, joint):
+    share = weights.shape[1]
+    part = share // 3
+    columns = pl.BlockSpec((D, part), lambda g: (0, g))
+    return pl.pallas_call(
+        functools.partial(update_kernel, joint),
+        grid=(3,),
+        out_shape=(
+            jax.ShapeDtypeStruct((D, share), jnp.float32),
+            jax.ShapeDtypeStruct((D, share), jnp.bfloat16),
+        ),
+        in_specs=[
+            pl.BlockSpec((FF, D), lambda g: (g, 0)),
+            pl.BlockSpec((part, FF), lambda g: (g, 0)),
+            columns,
+        ],
+        out_specs=(columns, columns),
+        compiler_params=pltpu.CompilerParams(vmem_limit_bytes=VMEM_LIMIT),
+        cost_estimate=pl.CostEstimate(
+            flops=2 * share * D * FF, bytes_accessed=4 * share * FF + 16 * share * D, transcendentals=0
+        ),
+        name="apply_update",
+    )(every, right_bases, weights)
 
 
 def on_device(
@@ -780,23 +1056,18 @@
         moved = lax.all_to_all(array, "seq", split_axis=1, concat_axis=0, tiled=True)
         return moved[:number]
 
-    x = to_rows(inputs)
-    pull = to_rows(cotangent)
     on_plane = owners == 8 and groups == 4 and number == 3
-
-    def gather_blocks(matrix):
-        if on_plane:
-            return plane_gather(matrix, block_widths, block_starts)
-        return [lax.all_gather(block, "dp", axis=0, tiled=True) for block in blocks_of(matrix)]
-
-    def scatter_blocks(terms):
-        if on_plane:
-            return plane_reduce(terms, block_widths, block_starts)[0]
-        return jnp.concatenate(
-            [lax.psum_scatter(term, "dp", scatter_dimension=0, tiled=True) for term in terms], axis=0
+    shard = weights.astype(jnp.bfloat16).T
+    if on_plane:
+        w_qkv, w_out, w_up, w_down, x, pull = plane_gather(
+            shard, block_widths, block_starts, False, ("in", "in"), (inputs, cotangent), length
         )
-
-    w_qkv, w_out, w_up, w_down = gather_blocks(weights.astype(jnp.bfloat16).T)
+    else:
+        x = to_rows(inputs)
+        pull = to_rows(cotangent)
+        w_qkv, w_out, w_up, w_down = [
+            lax.all_gather(block, "dp", axis=0, tiled=True) for block in blocks_of(shard)
+        ]
     pieces = [small[index * D : (index + 1) * D] for index in range(8)] + [small[8 * D :]]
     (
         gain_one,
@@ -861,8 +1132,8 @@
     input_grad = d_one
     for part in range(3):
         input_grad = input_grad + dot_dims(d_qkv[part], w_qkv[part * D : (part + 1) * D], 1, 0)
-    input_grad = to_quarters(input_grad.astype(jnp.bfloat16))
-    output = to_quarters(output.astype(jnp.bfloat16))
+    input_grad = input_grad.astype(jnp.bfloat16)
+    output = output.astype(jnp.bfloat16)
 
     small_local = jnp.concatenate(
         [
@@ -879,41 +1150,48 @@
     )
     grads = [grad_qkv, grad_outw, grad_up, grad_down]
     if on_plane:
+        joint = block_widths[0]
         mine, small_grad = plane_reduce(
             grads, block_widths, block_starts, small_local.reshape(-1, LANES)
         )
         small_grad = small_grad.reshape(-1)
+        reduced, term = turn(mine, bases, right_bases, joint)
+        (rotated,) = plane_reduce([term], block_widths, block_starts)
+        first_new, second_new, step = adam(rotated, first_moment, second_moment, bases, joint)
+        every, output, input_grad = plane_gather(
+            step, block_widths, block_starts, True, ("out", "out"), (output, input_grad), length
+        )
+        weights_new, weights_low = apply_update(every, right_bases, weights, joint)
     else:
-        mine = lax.psum(scatter_blocks(grads), "seq")
+        output = to_quarters(output)
+        input_grad = to_quarters(input_grad)
+        scatter = lambda array: lax.psum_scatter(array, "dp", scatter_dimension=0, tiled=True)
+        mine = lax.psum(jnp.concatenate([scatter(grad) for grad in grads], axis=0), "seq")
         small_grad = lax.psum(small_local, ("dp", "seq"))
-    reduced = mine.T.astype(jnp.float32)
-    bases_low = bases.astype(jnp.bfloat16)
-    rights = [
-        right_bases[
-            block_starts[which] : block_starts[which] + block_widths[which],
-            : owners * block_widths[which],
-        ].astype(jnp.bfloat16)
-        for which in range(4)
-    ]
-    terms = []
-    for which, block in enumerate(blocks_of(mine)):
-        turned = dot_dims(block, bases_low[which], 1, 0).astype(jnp.bfloat16)
-        terms.append(dot_dims(rights[which], turned, 0, 0).astype(jnp.bfloat16))
-    rotated = scatter_blocks(terms).T.astype(jnp.float32)
-    first_new, second_new, heading = moments(rotated, first_moment, second_moment)
-    heading = heading.astype(jnp.bfloat16)
-    steps = [
-        dot_dims(
-            heading[:, block_starts[which] : block_starts[which] + block_widths[which]],
-            bases_low[which],
-            0,
-            1,
-        ).astype(jnp.bfloat16)
-        for which in range(4)
-    ]
-    every = gather_blocks(jnp.concatenate(steps, axis=0))
-    update = [dot_dims(every[which], rights[which], 0, 1) for which in range(4)]
-    weights_new = weights - learn_rate * jnp.concatenate(update, axis=1)
+        reduced = mine.T.astype(jnp.float32)
+        bases_low = bases.astype(jnp.bfloat16)
+        rights = [
+            right_bases[
+                block_starts[which] : block_starts[which] + block_widths[which],
+                : owners * block_widths[which],
+            ].astype(jnp.bfloat16)
+            for which in range(4)
+        ]
+        rotated = []
+        for which, block in enumerate(blocks_of(mine)):
+            turned = low_of(dot_dims(block, bases_low[which], 1, 0))
+            rotated.append(scatter(low_of(dot_dims(rights[which], turned, 0, 0))))
+        rotated = jnp.concatenate(rotated, axis=0).T.astype(jnp.float32)
+        first_new, second_new, heading = moments(rotated, first_moment, second_moment)
+        heading = low_of(heading)
+        update = []
+        for which in range(4):
+            block = heading[:, block_starts[which] : block_starts[which] + block_widths[which]]
+            step = low_of(dot_dims(block, bases_low[which], 0, 1))
+            every = lax.all_gather(step, "dp", axis=0, tiled=True)
+            update.append(dot_dims(every, rights[which], 0, 1))
+        weights_new = weights - learn_rate * jnp.concatenate(update, axis=1)
+        weights_low = low_of(weights_new)
     small_first_new, small_second_new, small_heading = moments(
         small_grad, small_first, small_second
     )
@@ -925,7 +1203,7 @@
         first_new,
         second_new,
         weights_new,
-        weights_new.astype(jnp.bfloat16),
+        weights_low,
         small_grad,
         small_first_new,
         small_second_new,

time: 779 us -> 606 us (0.78)
  the two profiles are of different devices: /device:TPU:1 before, /device:TPU:24 now
where the time goes in v3:
time: 606 us; the launch traced here: 599 us
  Pallas kernels  439 us (72%)
  matrix products  115 us (19%)
  local copies, waits for them, and re-layouts  30.6 us (5%)
  other arithmetic  12.8 us (2%)
    pallas_call x2, Pallas kernels, plane_reduce(): pl.pallas_call(functools.partial(reduce_kernel, widths, starts, places, a...  205 us
    pallas_call x2, Pallas kernels, plane_gather(): pl.pallas_call(functools.partial(gather_kernel, widths, starts, places, m...  136 us
    dot_general x16, matrix products, dot_dims(): lax.dot_general(left, right, (((left_dim,), (right_dim,)), ((), ())), pre...  115 us
    unnamed x94, local copies, waits for them, and re-layouts  25.9 us
    pallas_call x1, Pallas kernels, attend_back(): pl.pallas_call(functools.partial(attend_back_kernel, sizes, tile), out_sh...  24.7 us
    pallas_call x1, Pallas kernels, attend(): pl.pallas_call(functools.partial(attend_kernel, sizes, tile), out_shape=(...  23.3 us
    pallas_call x1, Pallas kernels, turn(): pl.pallas_call(functools.partial(turn_kernel, joint), grid=(3,), out_shap...  21.5 us
    pallas_call x1, Pallas kernels, apply_update(): pl.pallas_call(functools.partial(update_kernel, joint), grid=(3,), out_sh...  14.3 us

profile of v3, /device:TPU:24, one launch (start us, length us, event | category | flops | bytes accessed | tf_op | source)
XLA Modules:
  0.0 599.0 jit_solution(6775631627908119200)
XLA Ops:
  0.7 0.7 fusion.20
  1.9 1.3 gather_fusion
  3.9 0.8 fusion.37
  4.7 3.1 copy.30
  7.8 1.3 copy-done.8
  9.1 1.3 copy-done.9
  10.3 64.4 %gather_weights.1 = (bf16[2304,768]{1,0:T(8,128)(2,1)S(1)}, bf16[768,768]{1,0:T(8,128)(2,1)S(1)}, bf16[3072,768]{1,0:T(8,128)(2,1)S(1)}, bf16[3072,768]{1,0:T(8,...) custom-call(bf16[1152,768]{1,0:T(8,128)(2,1)S(1)} %bitcast.67, ...), custom_call_target="tpu_custom_call" | custom-call | bytes 113246208 | tf_op jit(solution)/shard_map/gather_weights/pallas_call | solution.py:486
  74.8 2.2 copy-done.12
  77.0 2.1 copy-done.13
  79.6 5.5 add_convert_fusion.1.q_ref.k_ref.v_ref
  85.1 1.0 broadcast_in_dim.7.col_ref
  86.1 23.3 %attend.1 = (bf16[1024,768]{1,0:T(8,128)(2,1)}, f32[6,2,1024]{2,1,0:T(2,128)}) custom-call(s32[1,8]{1,0:T(1,128)} %reshape.417.table, bf16[1024,2304]{1,0:T(8,128)(2,1)} %add_convert_fusion.1.q_ref.k_ref.v_ref, bf16[1024,2304]{1,0:T(8,128)(2,1)} %add_convert_fusion.1.q_ref.k_ref.v_ref, bf16[1024,2304]{1,0:T(8,128)(2,1)} %add_convert_fusion.1.q_ref.k_ref.v_ref, ...), custom_call_target="tpu_custom_call" | custom-call | flops 3221225472 | bytes 6291456 | tf_op jit(solution)/shard_map/attend/pallas_call | solution.py:136
  109.4 3.4 fusion.38
  114.2 37.7 %multiply_convert_fusion = (bf16[1024,3072]{1,0:T(8,128)(2,1)S(1)}, f32[1024,3072]{1,0:T(8,128)}, f32[1024,3072]{1,0:T(8,128)}) fusion(f32[3072]{0:T(1024)S(1)} %slice.69, bf16[3072,768]{1,0:T(8,128)(2,1)S(1)} %bitcast.71, f32[1024,768]{1,0:T(8,128)S(1)} %get-tuple-element.84, f32[768]{0:T(1024)S(1)} %get-tuple-element.78, f32[768]{0:T(1024)S(1)} %get-tuple-element.79, ...), kind=kOutput, calls=%fused_computation.5 | convolution fusion | flops 5043388416 | bytes 39348224 | tf_op jit(solution)/shard_map/dot_general | solution.py:33
  151.9 5.5 fusion.39
  157.9 2.1 fusion.12
  160.1 2.3 convert_reduce_fusion.2
  162.4 19.3 %convert_reduce_fusion = (f32[3072]{0:T(1024)S(1)}, bf16[1024,3072]{1,0:T(8,128)(2,1)}) fusion(f32[1024,3072]{1,0:T(8,128)} %get-tuple-element.71, bf16[3072,768]{1,0:T(8,128)(2,1)} %copy-done.13, f32[1024,768]{1,0:T(8,128)} %get-tuple-element.67, f32[1024,3072]{1,0:T(8,128)} %get-tuple-element.85, f32[3072]{0:T(1024)S(1)} %slice.69), kind=kOutput, calls=%fused_computation.3 | convolution fusion | flops 4886098944 | bytes 39346176 | tf_op jit(solution)/shard_map/dot_general | solution.py:33
  181.7 10.9 %multiply_reduce_fusion = (f32[768]{0:T(1024)S(1)}, f32[1024]{0:T(1024)S(1)}, f32[1024]{0:T(1024)S(1)}, f32[768]{0:T(1024)S(1)}, f32[1024,768]{1,0:T(8,128)S(1)}) fusion(f32[1024,768]{1,0:T(8,128)} %copy-done.19, f32[1024]{0:T(1024)S(1)} %add_rsqrt_fusion.1, f32[1024]{0:T(1024)S(1)} %broadcast_multiply_fusion.5, f32[768]{0:T(1024)S(1)} %get-tuple-element.79, ...), kind=kOutput, calls=%fused_computation.39 | convolution fusion | flops 4839698432 | bytes 20472832 | tf_op jit(solution)/shard_map/dot_general | solution.py:33
  192.6 1.1 convert_reduce_fusion.3
  193.9 2.6 convolution_convert_fusion.2.g_ref
  196.5 24.7 %attend_back.1 = bf16[3,1024,768]{2,1,0:T(8,128)(2,1)} custom-call(s32[1,8]{1,0:T(1,128)} %reshape.417.table, bf16[1024,2304]{1,0:T(8,128)(2,1)} %add_convert_fusion.1.q_ref.k_ref.v_ref, bf16[1024,2304]{1,0:T(8,128)(2,1)} %add_convert_fusion.1.q_ref.k_ref.v_ref, bf16[1024,2304]{1,0:T(8,128)(2,1)} %add_convert_fusion.1.q_ref.k_ref.v_ref, ...), custom_call_target="tpu_custom_call" | custom-call | flops 8053063680 | bytes 11010048 | tf_op jit(solution)/shard_map/attend_back/pallas_call | solution.py:226
  221.2 3.3 fusion.14
  224.5 0.9 copy-done.25
  225.4 1.4 fusion.15
  227.3 1.4 add_convert_fusion.2.refs_1_
  228.8 2.5 convert_reduce_fusion.4
  231.6 10.1 %convolution_convert_fusion.refs_3_ = bf16[3072,768]{1,0:T(8,128)(2,1)} fusion(bf16[1024,3072]{1,0:T(8,128)(2,1)} %copy-done.32, f32[1024,768]{1,0:T(8,128)S(1)} %copy-done.26), kind=kOutput, calls=%fused_computation.20 | convolution fusion | flops 4834983936 | bytes 14155776 | tf_op jit(solution)/shard_map/dot_general | solution.py:33
  241.8 8.0 %convolution_convert_fusion.1.refs_2_ = bf16[3072,768]{1,0:T(8,128)(2,1)} fusion(bf16[1024,3072]{1,0:T(8,128)(2,1)S(1)} %bitcast.83, f32[1024,768]{1,0:T(8,128)S(1)} %copy-done.21, f32[768]{0:T(1024)S(1)} %get-tuple-element.78, f32[768]{0:T(1024)S(1)} %get-tuple-element.79, f32[1024]{0:T(1024)S(1)} %add_rsqrt_fusion.1, f32[1024]{0:T(1024)S(1)} %broadcast_multiply_fusion.5), kind=kOutput, calls=%fused_computation.21 | convolution fusion | flops 4838129664 | bytes 14170112 | tf_op jit(solution)/shard_map/dot_general | solution.py:33
  249.8 1.4 convolution_convert_fusion.3.refs_1_
  251.3 1.4 convolution_convert_fusion.6
  252.7 1.4 convolution_convert_fusion.5
  254.2 1.4 convolution_convert_fusion.4
  255.6 2.0 pad_maximum_fusion.refs_0_
  257.6 140.2 %reduce_all.1 = (bf16[1152,768]{1,0:T(8,128)(2,1)S(1)}, f32[72,128]{1,0:T(8,128)S(1)}) custom-call(bf16[2304,768]{1,0:T(8,128)(2,1)} %pad_maximum_fusion.refs_0_, bf16[768,768]{1,0:T(8,128)(2,1)S(1)} %convolution_convert_fusion.3.refs_1_, bf16[3072,768]{1,0:T(8,128)(2,1)} %convolution_convert_fusion.1.refs_2_, ...), custom_call_target="tpu_custom_call" | custom-call | bytes 141557760 | tf_op jit(solution)/shard_map/reduce_all/pallas_call | solution.py:848
  397.8 1.2 copy-done.3
  399.0 21.5 %turn.1 = (f32[768,1152]{1,0:T(8,128)}, bf16[9216,768]{1,0:T(8,128)(2,1)}) custom-call(bf16[1152,768]{1,0:T(8,128)(2,1)} %copy-done.3, f32[4,768,768]{2,1,0:T(8,128)} %basis_out_ref.3, f32[4,768,768]{2,1,0:T(8,128)} %basis_out_ref.3, f32[1152,3072]{1,0:T(8,128)} %right_ref.3), custom_call_target="tpu_custom_call" | custom-call | flops 6794772480 | bytes 31850496 | tf_op jit(solution)/shard_map/turn/pallas_call | solution.py:907
  420.5 64.9 %plane_reduce.1.rotated_ref = bf16[1152,768]{1,0:T(8,128)(2,1)S(1)} custom-call(bf16[9216,768]{1,0:T(8,128)(2,1)} %get-tuple-element.40.refs_0_), custom_call_target="tpu_custom_call" | custom-call | bytes 141557760 | tf_op jit(solution)/shard_map/plane_reduce/pallas_call | solution.py:848
  485.4 1.2 copy-done.1
  486.6 14.1 %adam.1 = (f32[768,1152]{1,0:T(8,128)}, f32[768,1152]{1,0:T(8,128)}, bf16[1152,768]{1,0:T(8,128)(2,1)}) custom-call(bf16[1152,768]{1,0:T(8,128)(2,1)} %copy-done.1, f32[768,1152]{1,0:T(8,128)} %first_ref.1, f32[768,1152]{1,0:T(8,128)} %second_ref.1, f32[4,768,768]{2,1,0:T(8,128)} %basis_out_ref.3, f32[4,768,768]{2,1,0:T(8,128)} %basis_out_ref.3), custom_call_target="tpu_custom_call" | custom-call | flops 1358954496 | bytes 17694720 | tf_op jit(solution)/shard_map/adam/pallas_call | solution.py:957
  500.7 1.5 copy-done.2
  502.2 71.9 %gather_steps.1 = (bf16[9216,768]{1,0:T(8,128)(2,1)S(1)}, bf16[3,256,768]{2,1,0:T(8,128)(2,1)S(1)}, bf16[3,256,768]{2,1,0:T(8,128)(2,1)S(1)}) custom-call(bf16[1152,768]{1,0:T(8,128)(2,1)S(1)} %copy-done.2, bf16[1024,768]{1,0:T(8,128)(2,1)S(1)} %get-tuple-element.74.refs_0_, bf16[1024,768]{1,0:T(8,128)(2,1)S(1)} %add_convert_fusion.2.refs_1_), custom_call_target="tpu_custom_call" | custom-call | bytes 113246208 | tf_op jit(solution)/shard_map/gather_steps/pallas_call | solution.py:486
  574.1 5.0 copy-done
  579.1 1.0 copy-done.4
  580.2 1.0 copy-done.6
  581.2 14.3 %apply_update.1 = (f32[768,1152]{1,0:T(8,128)}, bf16[768,1152]{1,0:T(8,128)(2,1)}) custom-call(bf16[9216,768]{1,0:T(8,128)(2,1)} %copy-done, f32[1152,3072]{1,0:T(8,128)} %right_ref.3, f32[768,1152]{1,0:T(8,128)} %weights_ref.1), custom_call_target="tpu_custom_call" | custom-call | flops 5435817984 | bytes 28311552 | tf_op jit(solution)/shard_map/apply_update/pallas_call | solution.py:998
  596.2 1.0 copy.45
  597.2 1.0 copy.46
  (109 shorter events, 5.7 us)
Async XLA Ops:
  1.4 83.7 %copy-start.28 = (s32[1,1024]{1,0:T(1,128)}, s32[1,1024]{1,0:T(1,128)S(1)}, u32[]{:S(2)}) copy-start(s32[1,1024]{1,0:T(1,128)S(1)} %fusion.20) | copy-start | bytes 12292
  7.8 1.3 copy-start.8
  9.1 1.3 copy-start.9
  74.8 2.2 copy-start.12
  77.0 2.1 copy-start.13
  77.0 2.6 copy-start.17
  77.0 8.1 %copy-start.10 = (bf16[2304,768]{1,0:T(8,128)(2,1)}, bf16[2304,768]{1,0:T(8,128)(2,1)S(1)}, u32[]{:S(2)}) copy-start(bf16[2304,768]{1,0:T(8,128)(2,1)S(1)} %get-tuple-element.32) | copy-start | bytes 10616836
  77.0 8.1 %copy-start.14 = (bf16[1024,768]{1,0:T(8,128)(2,1)}, bf16[1024,768]{1,0:T(8,128)(2,1)S(1)}, u32[]{:S(2)}) copy-start(bf16[1024,768]{1,0:T(8,128)(2,1)S(1)} %get-tuple-element.31) | copy-start | bytes 4718596
  86.1 23.3 %copy-start.15 = (bf16[1024,768]{1,0:T(8,128)(2,1)S(1)}, bf16[1024,768]{1,0:T(8,128)(2,1)}, u32[]{:S(2)}) copy-start(bf16[1024,768]{1,0:T(8,128)(2,1)} %copy-done.14) | copy-start | bytes 4718596
  109.4 4.8 slice-start
  109.4 4.8 slice-start.1
  109.4 42.5 %slice-start.2 = ((s8[4718592]{0:T(1024)(128)(4,1)}), s8[4194304]{0:T(1024)(128)(4,1)S(1)}, s32[]{:S(2)}) async-start(s8[4718592]{0:T(1024)(128)(4,1)} %bitcast.72), calls=%async_computation.2 | async-start | bytes 8388608
  112.9 39.0 %copy-start.19 = (f32[1024,768]{1,0:T(8,128)}, f32[1024,768]{1,0:T(8,128)S(1)}, u32[]{:S(2)}) copy-start(f32[1024,768]{1,0:T(8,128)S(1)} %get-tuple-element.84) | copy-start | bytes 9437188
  114.2 37.7 %slice-start.3 = ((s8[4718592]{0:T(1024)(128)(4,1)}), s8[524288]{0:T(1024)(128)(4,1)S(1)}, s32[]{:S(2)}) async-start(s8[4718592]{0:T(1024)(128)(4,1)} %bitcast.72), calls=%async_computation.3 | async-start | bytes 1048576
  151.9 5.5 copy-start.32
  181.7 10.9 %copy-start.20 = (f32[1024,768]{1,0:T(8,128)S(1)}, f32[1024,768]{1,0:T(8,128)}, u32[]{:S(2)}) copy-start(f32[1024,768]{1,0:T(8,128)} %copy-done.19) | copy-start | bytes 9437188
  192.6 1.3 copy-start.18
  193.7 2.8 copy-start.22
  221.2 3.3 copy-start.11
  221.2 4.2 copy-start.25
  225.4 1.9 copy-start.23
  228.7 2.8 copy-start.26
  228.8 12.9 %slice-start.6 = ((s8[6291456]{0:T(1024)(128)(4,1)}), s8[4194304]{0:T(1024)(128)(4,1)S(1)}, s32[]{:S(2)}) async-start(s8[6291456]{0:T(1024)(128)(4,1)} %bitcast.82), calls=%async_computation.6 | async-start | bytes 8388608
  231.6 10.1 %copy-start.21 = (f32[1024,768]{1,0:T(8,128)S(1)}, f32[1024,768]{1,0:T(8,128)}, u32[]{:S(2)}) copy-start(f32[1024,768]{1,0:T(8,128)} %copy-done.19) | copy-start | bytes 9437188
  231.6 10.1 %slice-start.7 = ((s8[6291456]{0:T(1024)(128)(4,1)}), s8[2097152]{0:T(1024)(128)(4,1)S(1)}, s32[]{:S(2)}) async-start(s8[6291456]{0:T(1024)(128)(4,1)} %bitcast.82), calls=%async_computation.7 | async-start | bytes 4194304
  231.6 19.6 %slice-start.4 = ((s8[4718592]{0:T(1024)(128)(4,1)}), s8[4194304]{0:T(1024)(128)(4,1)S(1)}, s32[]{:S(2)}) async-start(s8[4718592]{0:T(1024)(128)(4,1)} %bitcast.74), calls=%async_computation.4 | async-start | bytes 8388608
  241.7 8.0 %copy-start.24 = (f32[1024,768]{1,0:T(8,128)S(1)}, f32[1024,768]{1,0:T(8,128)}, u32[]{:S(2)}) copy-start(f32[1024,768]{1,0:T(8,128)} %copy-done.22) | copy-start | bytes 9437188
  241.7 8.0 %copy-start.31 = (bf16[1024,768]{1,0:T(8,128)(2,1)S(1)}, bf16[1024,768]{1,0:T(8,128)(2,1)}, u32[]{:S(2)}) copy-start(bf16[1024,768]{1,0:T(8,128)(2,1)} %get-tuple-element.33) | copy-start | bytes 4718596
  241.7 9.5 %slice-start.5 = ((s8[4718592]{0:T(1024)(128)(4,1)}), s8[524288]{0:T(1024)(128)(4,1)S(1)}, s32[]{:S(2)}) async-start(s8[4718592]{0:T(1024)(128)(4,1)} %bitcast.74), calls=%async_computation.5 | async-start | bytes 1048576
  249.8 1.5 copy-start.16
  397.8 1.2 copy-start.3
  485.4 1.2 copy-start.1
  500.7 1.5 copy-start.2
  574.1 5.0 copy-start
  579.1 1.0 copy-start.4
  580.2 1.0 copy-start.6
  581.2 14.3 %copy-start.27 = (f32[9216]{0:T(1024)S(1)}, f32[9216]{0:T(1024)}, u32[]{:S(2)}) copy-start(f32[9216]{0:T(1024)} %param.20) | copy-start | bytes 110596
  581.2 14.3 %copy-start.29 = (f32[9216]{0:T(1024)S(1)}, f32[9216]{0:T(1024)}, u32[]{:S(2)}) copy-start(f32[9216]{0:T(1024)} %param.22) | copy-start | bytes 110596
  581.2 14.3 %copy-start.30 = (f32[9216]{0:T(1024)S(1)}, f32[9216]{0:T(1024)}, u32[]{:S(2)}) copy-start(f32[9216]{0:T(1024)} %param.21) | copy-start | bytes 110596
  581.2 15.0 %copy-start.7 = (bf16[3,256,768]{2,1,0:T(8,128)(2,1)S(1)}, bf16[3,256,768]{2,1,0:T(8,128)(2,1)}, u32[]{:S(2)}) copy-start(bf16[3,256,768]{2,1,0:T(8,128)(2,1)} %copy-done.6) | copy-start | bytes 3538948
  595.5 1.7 copy-start.5

commit v4 on v3

--- a/solution.py
+++ b/solution.py
@@ -33,6 +33,10 @@
     return lax.dot_general(
         left, right, (((left_dim,), (right_dim,)), ((), ())), preferred_element_type=jnp.float32
     )
+
+
+def low_of(value):
+    return value.astype(jnp.bfloat16)
 
 
 def normalize(resid, gain, shift):
@@ -251,6 +255,167 @@
         ),
         name="attend_back",
     )(table, project, project, project, grad, marks_col, marks_row, log_sum)
+
+
+TOKENS = 256
+PIECE = 768
+
+
+def gelu_and_slope(value):
+    size = jnp.abs(value)
+    turn_at = 1.0 / (1.0 + size * (0.3275911 * 0.5**0.5))
+    bell = jnp.exp(value * value * -0.5)
+    tail = turn_at * (
+        0.5 * 0.254829592
+        + turn_at
+        * (
+            0.5 * -0.284496736
+            + turn_at
+            * (0.5 * 1.421413741 + turn_at * (0.5 * -1.453152027 + turn_at * (0.5 * 1.061405429)))
+        )
+    )
+    tail = tail * bell
+    chance = jnp.where(value >= 0.0, 1.0 - tail, tail)
+    return (value * chance, chance + value * bell * (2.0 * math.pi) ** (-0.5))
+
+
+def layer_kernel(
+    context_ref,
+    x_ref,
+    pull_ref,
+    out_w,
+    up_w,
+    down_w,
+    small_ref,
+    bias_up_ref,
+    output_ref,
+    first_ref,
+    active_ref,
+    d_down_ref,
+    d_up_ref,
+    d_att_ref,
+    d_context_ref,
+    sums_ref,
+    up_sums_ref,
+    slope_ref,
+):
+    parameter = lambda row: small_ref[row : row + 1, :]
+    gain_one, gain_two, shift_one, shift_two = [parameter(row) for row in range(4)]
+    bias_out, bias_down = parameter(6), parameter(7)
+    attended = dot_dims(context_ref[...], out_w[...], 1, 1) + bias_out
+    first, scaled_one, inv_one = normalize(
+        x_ref[...].astype(jnp.float32) + attended, gain_one, shift_one
+    )
+    first_low = low_of(first)
+    first_ref[...] = first_low
+    downward = bias_down
+    for begin in range(0, FF, PIECE):
+        units = slice(begin, begin + PIECE)
+        upward = dot_dims(first_low, up_w[units, :], 1, 1) + bias_up_ref[:, units]
+        active, slope = gelu_and_slope(upward)
+        active = low_of(active)
+        active_ref[:, units] = active
+        slope_ref[:, units] = slope
+        downward = downward + jnp.dot(active, down_w[units, :], preferred_element_type=jnp.float32)
+    output, scaled_two, inv_two = normalize(first + downward, gain_two, shift_two)
+    output_ref[...] = low_of(output)
+    grad_out = pull_ref[...].astype(jnp.float32)
+    d_two = norm_back(grad_out, scaled_two, inv_two, gain_two)
+    d_down = low_of(d_two)
+    d_down_ref[...] = d_down
+    d_first = d_two
+    up_sums = []
+    for begin in range(0, FF, PIECE):
+        units = slice(begin, begin + PIECE)
+        d_active = dot_dims(d_down, down_w[units, :], 1, 1)
+        d_up = low_of(d_active * slope_ref[:, units])
+        d_up_ref[:, units] = d_up
+        up_sums.append(jnp.sum(d_up.astype(jnp.float32), axis=0, keepdims=True))
+        d_first = d_first + jnp.dot(d_up, up_w[units, :], preferred_element_type=jnp.float32)
+    d_one = norm_back(d_first, scaled_one, inv_one, gain_one)
+    d_att = low_of(d_one)
+    d_att_ref[...] = d_att
+    d_context_ref[...] = low_of(jnp.dot(d_att, out_w[...], preferred_element_type=jnp.float32))
+    total = lambda value: jnp.sum(value, axis=0, keepdims=True)
+    nothing = jnp.zeros_like(gain_one)
+    sums = jnp.concatenate(
+        [
+            total(d_first * scaled_one),
+            total(grad_out * scaled_two),
+            total(d_first),
+            total(grad_out),
+            nothing,
+            nothing,
+            total(d_att.astype(jnp.float32)),
+            total(d_down.astype(jnp.float32)),
+        ],
+        axis=0,
+    )
+    up_sums = jnp.concatenate(up_sums, axis=1)
+
+    @pl.when(pl.program_id(0) == 0)
+    def _():
+        sums_ref[...] = sums
+        up_sums_ref[...] = up_sums
+
+    @pl.when(pl.program_id(0) != 0)
+    def _():
+        sums_ref[...] += sums
+        up_sums_ref[...] += up_sums
+
+
+def layer(context, x, pull, w_out, w_up, w_down, small):
+    tokens = context.shape[0]
+    tile = min(TOKENS, tokens)
+    narrow = pl.BlockSpec((tile, D), lambda i: (i, 0))
+    broad = pl.BlockSpec((tile, FF), lambda i: (i, 0))
+    fixed = lambda shape: pl.BlockSpec(shape, lambda i: (0, 0), pipeline_mode=pl.Buffered(1))
+    low_narrow = jax.ShapeDtypeStruct((tokens, D), jnp.bfloat16)
+    low_broad = jax.ShapeDtypeStruct((tokens, FF), jnp.bfloat16)
+    return pl.pallas_call(
+        layer_kernel,
+        grid=(tokens // tile,),
+        out_shape=(
+            low_narrow,
+            low_narrow,
+            low_broad,
+            low_narrow,
+            low_broad,
+            low_narrow,
+            low_narrow,
+            jax.ShapeDtypeStruct((8, D), jnp.float32),
+            jax.ShapeDtypeStruct((1, FF), jnp.float32),
+        ),
+        in_specs=[
+            narrow,
+            narrow,
+            narrow,
+            fixed((D, D)),
+            fixed((FF, D)),
+            fixed((FF, D)),
+            fixed((8, D)),
+            fixed((1, FF)),
+        ],
+        out_specs=(
+            narrow,
+            narrow,
+            broad,
+            narrow,
+            broad,
+            narrow,
+            narrow,
+            pl.BlockSpec((8, D), lambda i: (0, 0)),
+            pl.BlockSpec((1, FF), lambda i: (0, 0)),
+        ),
+        scratch_shapes=[pltpu.VMEM((tile, FF), jnp.float32)],
+        compiler_params=pltpu.CompilerParams(vmem_limit_bytes=VMEM_LIMIT),
+        cost_estimate=pl.CostEstimate(
+            flops=4 * tokens * D * (D + 2 * FF),
+            bytes_accessed=2 * (tokens * (7 * D + 2 * FF) + D * (D + 2 * FF)),
+            transcendentals=2 * tokens * FF,
+        ),
+        name="layer",
+    )(context, x, pull, w_out, w_up, w_down, small[: 8 * D].reshape(8, D), small[8 * D :].reshape(1, FF))
 
 
 MESH = pl.DeviceIdType.MESH
@@ -514,7 +679,7 @@
 
 def reduce_kernel(widths, starts, places, across_planes, *refs):
     count = len(widths)
-    arrays = 1 + max(number for number, _ in places)
+    arrays = 1 + max(place[0] for place in places)
     blocks = refs[:arrays]
     refs = refs[arrays:]
     if across_planes:
@@ -545,8 +710,8 @@
     loads, sends = {}, []
 
     def block_rows(block, owner):
-        number, first = places[block]
-        begin = pl.multiple_of(first + owner * widths[block], 16)
+        number, first, stride = places[block]
+        begin = pl.multiple_of(first + owner * stride, 16)
         return blocks[number].at[pl.ds(begin, widths[block])]
 
     for block in range(count):
@@ -792,14 +957,17 @@
 
 
 def plane_reduce(terms, widths, starts, small=None):
-    count = len(widths)
     share = sum(widths)
     depth = terms[0].shape[1]
     across_planes = small is not None
-    if len(terms) == 1:
-        places = [(0, 8 * start) for start in starts]
-    else:
-        places = [(number, 0) for number in range(count)]
+    pieces = []
+    for which in (2, 3, 0, 1):
+        width, start = widths[which], starts[which]
+        number, first = (0, 8 * start) if len(terms) == 1 else (which, 0)
+        size = next(size for size in (192, 96, width) if width % size == 0)
+        pieces += [(size, start + cut, (number, first + cut, width)) for cut in range(0, width, size)]
+    widths, starts, places = [list(part) for part in zip(*pieces)]
+    count = len(pieces)
     low = terms[0].dtype
     whole = pltpu.VMEM((share, depth), low)
     half = pltpu.VMEM((share // 2, depth), low)
@@ -870,10 +1038,6 @@
     ]
 
 
-def low_of(value):
-    return value.astype(jnp.bfloat16)
-
-
 def turn_kernel(joint, grad_ref, basis_ref, basis_out_ref, right_ref, reduced_ref, term_ref):
     group = pl.program_id(0)
     grad = grad_ref[...]
@@ -1068,19 +1232,7 @@
         w_qkv, w_out, w_up, w_down = [
             lax.all_gather(block, "dp", axis=0, tiled=True) for block in blocks_of(shard)
         ]
-    pieces = [small[index * D : (index + 1) * D] for index in range(8)] + [small[8 * D :]]
-    (
-        gain_one,
-        gain_two,
-        shift_one,
-        shift_two,
-        bias_query,
-        bias_value,
-        bias_out,
-        bias_down,
-        bias_up,
-    ) = pieces
-
+    bias_query, bias_value = small[4 * D : 5 * D], small[5 * D : 6 * D]
     filler = jnp.broadcast_to(
         (jnp.arange(length, dtype=jnp.int32) // TILE)[None], (padded - number, length)
     )
@@ -1091,61 +1243,33 @@
     marks_col = jnp.broadcast_to(marks.reshape(tokens, 1), (tokens, LANES))
     marks_row = marks.reshape(rows, 1, length)
 
-    acts = x.astype(jnp.float32)
     bias_qkv = jnp.concatenate([bias_query, jnp.zeros_like(bias_query), bias_value])
     project = (dot_dims(x, w_qkv, 1, 1) + bias_qkv).astype(jnp.bfloat16)
     context, log_sum = attend(table, project, marks_col, marks_row, rows, length)
-    attended = dot_dims(context, w_out, 1, 1) + bias_out
-    first, scaled_one, inv_one = normalize(acts + attended, gain_one, shift_one)
-    first_low = first.astype(jnp.bfloat16)
-    upward = dot_dims(first_low, w_up, 1, 1) + bias_up
-    active_full, gelu_pull = jax.vjp(lambda value: jax.nn.gelu(value, approximate=False), upward)
-    active = active_full.astype(jnp.bfloat16)
-    downward = dot_dims(active, w_down, 1, 0) + bias_down
-    output, scaled_two, inv_two = normalize(first + downward, gain_two, shift_two)
-    grad_out = pull.astype(jnp.float32)
-    d_two = norm_back(grad_out, scaled_two, inv_two, gain_two)
-    grad_gain_two = jnp.sum(grad_out * scaled_two, axis=0)
-    grad_shift_two = jnp.sum(grad_out, axis=0)
-    d_down = d_two.astype(jnp.bfloat16)
-    grad_bias_down = jnp.sum(d_down.astype(jnp.float32), axis=0)
-    grad_down = dot_dims(active, d_down, 0, 0).astype(jnp.bfloat16)
-    d_active = dot_dims(d_down, w_down, 1, 1)
-    (d_up_full,) = gelu_pull(d_active)
-    d_up = d_up_full.astype(jnp.bfloat16)
-    grad_bias_up = jnp.sum(d_up.astype(jnp.float32), axis=0)
-    grad_up = dot_dims(d_up, first_low, 0, 0).astype(jnp.bfloat16)
-    d_first = d_two + dot_dims(d_up, w_up, 1, 0)
-    d_one = norm_back(d_first, scaled_one, inv_one, gain_one)
-    grad_gain_one = jnp.sum(d_first * scaled_one, axis=0)
-    grad_shift_one = jnp.sum(d_first, axis=0)
-    d_att = d_one.astype(jnp.bfloat16)
-    grad_bias_out = jnp.sum(d_att.astype(jnp.float32), axis=0)
-    grad_outw = dot_dims(d_att, context, 0, 0).astype(jnp.bfloat16)
-    d_context = dot_dims(d_att, w_out, 1, 0).astype(jnp.bfloat16)
+    output, first_low, active, d_down, d_up, d_att, d_context, sums, up_sums = layer(
+        context, x, pull, w_out, w_up, w_down, small
+    )
+    grad_down = low_of(dot_dims(active, d_down, 0, 0))
+    grad_up = low_of(dot_dims(d_up, first_low, 0, 0))
+    grad_outw = low_of(dot_dims(d_att, context, 0, 0))
     d_qkv = attend_back(table, project, d_context, marks_col, marks_row, log_sum, rows, length)
     grad_bias_query = jnp.sum(d_qkv[0].astype(jnp.float32), axis=0)
     grad_bias_value = jnp.sum(d_qkv[2].astype(jnp.float32), axis=0)
     grad_qkv = jnp.concatenate([dot_dims(d_qkv[part], x, 0, 0) for part in range(3)], axis=0).astype(
         jnp.bfloat16
     )
-    input_grad = d_one
+    input_grad = d_att.astype(jnp.float32)
     for part in range(3):
         input_grad = input_grad + dot_dims(d_qkv[part], w_qkv[part * D : (part + 1) * D], 1, 0)
     input_grad = input_grad.astype(jnp.bfloat16)
-    output = output.astype(jnp.bfloat16)
 
     small_local = jnp.concatenate(
         [
-            grad_gain_one,
-            grad_gain_two,
-            grad_shift_one,
-            grad_shift_two,
+            sums[:4].reshape(-1),
             grad_bias_query,
             grad_bias_value,
-            grad_bias_out,
-            grad_bias_down,
-            grad_bias_up,
+            sums[6:].reshape(-1),
+            up_sums.reshape(-1),
         ]
     )
     grads = [grad_qkv, grad_outw, grad_up, grad_down]

time: 606 us -> 557 us (0.919)
  the two profiles are of different devices: /device:TPU:24 before, /device:TPU:1 now
where the time goes in v4:
time: 557 us; the launch traced here: 547 us
  Pallas kernels  466 us (84%)
  matrix products  37.3 us (7%)
  local copies, waits for them, and re-layouts  35.9 us (6%)
  other arithmetic  6.41 us (1%)
    pallas_call x2, Pallas kernels, plane_reduce(): pl.pallas_call(functools.partial(reduce_kernel, widths, starts, places, a...  178 us
    pallas_call x2, Pallas kernels, plane_gather(): pl.pallas_call(functools.partial(gather_kernel, widths, starts, places, m...  132 us
    pallas_call x1, Pallas kernels, layer(): pl.pallas_call(layer_kernel, grid=(tokens // tile,), out_shape=(low_narro...  43.5 us
    dot_general x10, matrix products, dot_dims(): lax.dot_general(left, right, (((left_dim,), (right_dim,)), ((), ())), pre...  37.3 us
    pallas_call x1, Pallas kernels, attend_back(): pl.pallas_call(functools.partial(attend_back_kernel, sizes, tile), out_sh...  33.7 us
    unnamed x74, local copies, waits for them, and re-layouts  29.2 us
    pallas_call x1, Pallas kernels, attend(): pl.pallas_call(functools.partial(attend_kernel, sizes, tile), out_shape=(...  29.1 us
    pallas_call x1, Pallas kernels, turn(): pl.pallas_call(functools.partial(turn_kernel, joint), grid=(3,), out_shap...  21.5 us

profile of v4, /device:TPU:1, one launch (start us, length us, event | category | flops | bytes accessed | tf_op | source)
XLA Modules:
  0.0 547.3 jit_solution(7097954091034501139)
XLA Ops:
  0.7 0.7 fusion.6
  1.9 1.3 gather_fusion
  3.3 0.6 reshape.391.table
  3.9 0.8 fusion.14
  4.7 1.3 slice.69
  6.0 0.7 slice.67
  7.4 1.0 broadcast_in_dim.7.col_ref
  8.4 3.2 copy.28
  11.6 1.3 copy-done.10
  12.8 66.7 %gather_weights.1 = (bf16[2304,768]{1,0:T(8,128)(2,1)S(1)}, bf16[768,768]{1,0:T(8,128)(2,1)S(1)}, bf16[3072,768]{1,0:T(8,128)(2,1)S(1)}, bf16[3072,768]{1,0:T(8,...) custom-call(bf16[1152,768]{1,0:T(8,128)(2,1)S(1)} %bitcast.63, ...), custom_call_target="tpu_custom_call" | custom-call | bytes 113246208 | tf_op jit(solution)/shard_map/gather_weights/pallas_call | solution.py:651
  79.5 2.1 copy-done.13
  81.7 2.2 copy-done.14
  83.8 1.1 copy-done.15
  85.0 1.0 copy-done.16
  86.0 1.8 copy-done.11
  87.8 7.3 %add_convert_fusion.q_ref.k_ref.v_ref = bf16[1024,2304]{1,0:T(8,128)(2,1)} fusion(bf16[1024,768]{1,0:T(8,128)(2,1)} %get-tuple-element.40.x_ref, bf16[2304,768]{1,0:T(8,128)(2,1)S(1)} %get-tuple-element.41, f32[2304]{0:T(1024)S(1)} %pad_maximum_fusion.1), kind=kOutput, calls=%fused_computation.1 | convolution fusion | flops 3628597248 | bytes 9839616 | tf_op jit(solution)/shard_map/dot_general | solution.py:33
  95.1 29.1 %attend.1 = (bf16[1024,768]{1,0:T(8,128)(2,1)}, f32[6,2,1024]{2,1,0:T(2,128)}) custom-call(s32[1,8]{1,0:T(1,128)} %reshape.391.table, bf16[1024,2304]{1,0:T(8,128)(2,1)} %add_convert_fusion.q_ref.k_ref.v_ref, bf16[1024,2304]{1,0:T(8,128)(2,1)} %add_convert_fusion.q_ref.k_ref.v_ref, bf16[1024,2304]{1,0:T(8,128)(2,1)} %add_convert_fusion.q_ref.k_ref.v_ref, ...), custom_call_target="tpu_custom_call" | custom-call | flops 3221225472 | bytes 6291456 | tf_op jit(solution)/shard_map/attend/pallas_call | solution.py:140
  124.3 43.5 %layer.1 = (bf16[1024,768]{1,0:T(8,128)(2,1)}, bf16[1024,768]{1,0:T(8,128)(2,1)}, bf16[1024,3072]{1,0:T(8,128)(2,1)}, bf16[1024,768]{1,0:T(8,128)(2,1)}, bf16[10...) custom-call(bf16[1024,768]{1,0:T(8,128)(2,1)} %get-tuple-element.42., ...), custom_call_target="tpu_custom_call" | custom-call | flops 21743271936 | bytes 34209792 | tf_op jit(solution)/shard_map/layer/pallas_call | solution.py:375
  167.8 2.8 convolution_convert_fusion.2.refs_1_
  170.7 33.7 %attend_back.1 = bf16[3,1024,768]{2,1,0:T(8,128)(2,1)} custom-call(s32[1,8]{1,0:T(1,128)} %reshape.391.table, bf16[1024,2304]{1,0:T(8,128)(2,1)} %add_convert_fusion.q_ref.k_ref.v_ref, bf16[1024,2304]{1,0:T(8,128)(2,1)} %add_convert_fusion.q_ref.k_ref.v_ref, bf16[1024,2304]{1,0:T(8,128)(2,1)} %add_convert_fusion.q_ref.k_ref.v_ref, ...), custom_call_target="tpu_custom_call" | custom-call | flops 8053063680 | bytes 11010048 | tf_op jit(solution)/shard_map/attend_back/pallas_call | solution.py:230
  204.4 2.5 convert_reduce_fusion
  207.0 3.4 convolution_convert_fusion.3
  210.4 2.8 convolution_convert_fusion.4
  213.3 2.8 convolution_convert_fusion.5
  216.2 2.2 pad_maximum_fusion.refs_0_
  218.4 1.1 copy-done.12
  219.4 1.4 fusion.1
  220.9 1.4 fusion
  222.3 1.4 add_convert_fusion.1.refs_1_
  223.7 0.7 slice-done.5
  224.8 6.9 %convolution_convert_fusion.1.refs_2_ = bf16[3072,768]{1,0:T(8,128)(2,1)} fusion(bf16[1024,3072]{1,0:T(8,128)(2,1)S(1)} %bitcast.79, bf16[1024,768]{1,0:T(8,128)(2,1)S(1)} %copy-done.26), kind=kOutput, calls=%fused_computation.3 | convolution fusion | flops 4834197504 | bytes 12582912 | tf_op jit(solution)/shard_map/dot_general | solution.py:33
  231.7 6.9 %convolution_convert_fusion.refs_3_ = bf16[3072,768]{1,0:T(8,128)(2,1)} fusion(bf16[1024,3072]{1,0:T(8,128)(2,1)S(1)} %bitcast.77, bf16[1024,768]{1,0:T(8,128)(2,1)S(1)} %copy-done.25), kind=kOutput, calls=%fused_computation.2 | convolution fusion | flops 4834197504 | bytes 12582912 | tf_op jit(solution)/shard_map/dot_general | solution.py:33
  238.6 107.0 %reduce_all.1 = (bf16[1152,768]{1,0:T(8,128)(2,1)S(1)}, f32[72,128]{1,0:T(8,128)S(1)}) custom-call(bf16[2304,768]{1,0:T(8,128)(2,1)} %pad_maximum_fusion.refs_0_, bf16[768,768]{1,0:T(8,128)(2,1)S(1)} %convolution_convert_fusion.2.refs_1_, bf16[3072,768]{1,0:T(8,128)(2,1)} %convolution_convert_fusion.1.refs_2_, ...), custom_call_target="tpu_custom_call" | custom-call | bytes 141557760 | tf_op jit(solution)/shard_map/reduce_all/pallas_call | solution.py:1016
  345.6 1.2 copy-done.3
  346.8 0.7 multiply_subtract_fusion
  347.5 21.5 %turn.1 = (f32[768,1152]{1,0:T(8,128)}, bf16[9216,768]{1,0:T(8,128)(2,1)}) custom-call(bf16[1152,768]{1,0:T(8,128)(2,1)} %copy-done.3, f32[4,768,768]{2,1,0:T(8,128)} %basis_out_ref.3, f32[4,768,768]{2,1,0:T(8,128)} %basis_out_ref.3, f32[1152,3072]{1,0:T(8,128)} %right_ref.3), custom_call_target="tpu_custom_call" | custom-call | flops 6794772480 | bytes 31850496 | tf_op jit(solution)/shard_map/turn/pallas_call | solution.py:1071
  369.0 71.0 %plane_reduce.1.rotated_ref = bf16[1152,768]{1,0:T(8,128)(2,1)S(1)} custom-call(bf16[9216,768]{1,0:T(8,128)(2,1)} %get-tuple-element.57.refs_0_), custom_call_target="tpu_custom_call" | custom-call | bytes 141557760 | tf_op jit(solution)/shard_map/plane_reduce/pallas_call | solution.py:1016
  439.9 1.2 copy-done.1
  441.1 14.4 %adam.1 = (f32[768,1152]{1,0:T(8,128)}, f32[768,1152]{1,0:T(8,128)}, bf16[1152,768]{1,0:T(8,128)(2,1)}) custom-call(bf16[1152,768]{1,0:T(8,128)(2,1)} %copy-done.1, f32[768,1152]{1,0:T(8,128)} %first_ref.1, f32[768,1152]{1,0:T(8,128)} %second_ref.1, f32[4,768,768]{2,1,0:T(8,128)} %basis_out_ref.3, f32[4,768,768]{2,1,0:T(8,128)} %basis_out_ref.3), custom_call_target="tpu_custom_call" | custom-call | flops 1358954496 | bytes 17694720 | tf_op jit(solution)/shard_map/adam/pallas_call | solution.py:1121
  455.6 1.5 copy-done.2
  457.0 65.4 %gather_steps.1 = (bf16[9216,768]{1,0:T(8,128)(2,1)S(1)}, bf16[3,256,768]{2,1,0:T(8,128)(2,1)S(1)}, bf16[3,256,768]{2,1,0:T(8,128)(2,1)S(1)}) custom-call(bf16[1152,768]{1,0:T(8,128)(2,1)S(1)} %copy-done.2, bf16[1024,768]{1,0:T(8,128)(2,1)S(1)} %copy-done.4, bf16[1024,768]{1,0:T(8,128)(2,1)S(1)} %add_convert_fusion.1.refs_1_), custom_call_target="tpu_custom_call" | custom-call | bytes 113246208 | tf_op jit(solution)/shard_map/gather_steps/pallas_call | solution.py:651
  522.4 5.0 copy-done
  527.4 1.0 copy-done.5
  528.5 1.0 copy-done.7
  529.5 14.3 %apply_update.1 = (f32[768,1152]{1,0:T(8,128)}, bf16[768,1152]{1,0:T(8,128)(2,1)}) custom-call(bf16[9216,768]{1,0:T(8,128)(2,1)} %copy-done, f32[1152,3072]{1,0:T(8,128)} %right_ref.3, f32[768,1152]{1,0:T(8,128)} %weights_ref.1), custom_call_target="tpu_custom_call" | custom-call | flops 5435817984 | bytes 28311552 | tf_op jit(solution)/shard_map/apply_update/pallas_call | solution.py:1162
  543.8 1.0 copy.36
  544.8 0.7 copy-done.6
  545.5 1.0 copy.37
  (76 shorter events, 2.4 us)
Async XLA Ops:
  1.4 10.1 %copy-start.19 = (s32[1,1024]{1,0:T(1,128)}, s32[1,1024]{1,0:T(1,128)S(1)}, u32[]{:S(2)}) copy-start(s32[1,1024]{1,0:T(1,128)S(1)} %fusion.6) | copy-start | bytes 12292
  8.4 3.2 copy-start.9
  11.6 1.3 copy-start.10
  79.5 2.2 copy-start.13
  81.7 2.2 copy-start.14
  83.8 1.1 copy-start.15
  85.0 1.0 copy-start.16
  86.0 1.8 copy-start.11
  124.3 43.5 %copy-start.24 = (bf16[1024,768]{1,0:T(8,128)(2,1)S(1)}, bf16[1024,768]{1,0:T(8,128)(2,1)}, u32[]{:S(2)}) copy-start(bf16[1024,768]{1,0:T(8,128)(2,1)} %get-tuple-element.42.context_ref) | copy-start | bytes 4718596
  170.6 33.7 %copy-start.22 = (f32[8,768]{1,0:T(8,128)S(1)}, f32[8,768]{1,0:T(8,128)}, u32[]{:S(2)}) copy-start(f32[8,768]{1,0:T(8,128)} %get-tuple-element.54) | copy-start | bytes 73732
  204.4 2.6 copy-start.23
  204.4 6.0 %slice-start = ((s8[4718592]{0:T(1024)(128)(4,1)}), s8[4194304]{0:T(1024)(128)(4,1)S(1)}, s32[]{:S(2)}) async-start(s8[4718592]{0:T(1024)(128)(4,1)} %bitcast.66), calls=%async_computation | async-start | bytes 8388608
  207.0 3.4 slice-start.1
  216.2 3.3 copy-start.12
  220.8 1.4 copy-start.17
  220.8 2.9 slice-start.4
  222.3 2.1 slice-start.5
  222.3 2.5 copy-start.26
  222.3 9.4 %slice-start.2 = ((s8[6291456]{0:T(1024)(128)(4,1)}), s8[2097152]{0:T(1024)(128)(4,1)S(1)}, s32[]{:S(2)}) async-start(s8[6291456]{0:T(1024)(128)(4,1)} %bitcast.76), calls=%async_computation.2 | async-start | bytes 4194304
  224.8 6.9 %slice-start.3 = ((s8[6291456]{0:T(1024)(128)(4,1)}), s8[4194304]{0:T(1024)(128)(4,1)S(1)}, s32[]{:S(2)}) async-start(s8[6291456]{0:T(1024)(128)(4,1)} %bitcast.76), calls=%async_computation.3 | async-start | bytes 8388608
  224.8 6.9 %copy-start.25 = (bf16[1024,768]{1,0:T(8,128)(2,1)S(1)}, bf16[1024,768]{1,0:T(8,128)(2,1)}, u32[]{:S(2)}) copy-start(bf16[1024,768]{1,0:T(8,128)(2,1)} %get-tuple-element.53) | copy-start | bytes 4718596
  238.6 108.2 %copy-start.18 = (f32[9216]{0:T(1024)S(1)}, f32[9216]{0:T(1024)}, u32[]{:S(2)}) copy-start(f32[9216]{0:T(1024)} %param.20) | copy-start | bytes 110596
  238.6 108.2 %copy-start.20 = (f32[9216]{0:T(1024)S(1)}, f32[9216]{0:T(1024)}, u32[]{:S(2)}) copy-start(f32[9216]{0:T(1024)} %param.22) | copy-start | bytes 110596
  238.6 108.2 %copy-start.21 = (f32[9216]{0:T(1024)S(1)}, f32[9216]{0:T(1024)}, u32[]{:S(2)}) copy-start(f32[9216]{0:T(1024)} %param.21) | copy-start | bytes 110596
  345.6 1.2 copy-start.3
  439.9 1.2 copy-start.1
  441.1 14.4 %copy-start.4 = (bf16[1024,768]{1,0:T(8,128)(2,1)S(1)}, bf16[1024,768]{1,0:T(8,128)(2,1)}, u32[]{:S(2)}) copy-start(bf16[1024,768]{1,0:T(8,128)(2,1)} %get-tuple-element.59.refs_0_) | copy-start | bytes 4718596
  455.6 1.5 copy-start.2
  522.4 5.0 copy-start
  527.4 1.0 copy-start.5
  528.5 1.0 copy-start.7
  529.5 14.3 %copy-start.8 = (bf16[3,256,768]{2,1,0:T(8,128)(2,1)S(1)}, bf16[3,256,768]{2,1,0:T(8,128)(2,1)}, u32[]{:S(2)}) copy-start(bf16[3,256,768]{2,1,0:T(8,128)(2,1)} %copy-done.7) | copy-start | bytes 3538948
  543.8 1.7 copy-start.6

commit v5 on v4

--- a/solution.py
+++ b/solution.py
@@ -24,6 +24,7 @@
 
 TILE = 256
 LANES = 128
+SIDE = 4
 WINDOWS = (256, 512, 640, 768, 1024)
 NEG = -1e30
 VMEM_LIMIT = 60 * 1024 * 1024
@@ -113,7 +114,7 @@
                 same = jnp.concatenate([marks] * (tile // LANES), axis=1) == row_ref[0, :, rows]
                 here = q_ref[rows, :]
                 done = []
-                for half in range(2):
+                for half in range(SIDE):
                     mine = jnp.where(head_lanes(half, here.shape), here * HD ** (-0.5), 0.0).astype(
                         jnp.bfloat16
                     )
@@ -132,16 +133,16 @@
 
 
 def attend(table, project, marks_col, marks_row, rows, length):
-    pairs = HEADS * HD // LANES
+    pairs = HEADS // SIDE
     tile = min(TILE, length)
     sizes = windows_of(length)
-    columns = lambda part: pl.BlockSpec((length, LANES), lambda i, j, t: (i, part * pairs + j))
+    columns = lambda part: pl.BlockSpec((length, SIDE * HD), lambda i, j, t: (i, part * pairs + j))
     flops = 4 * rows * HEADS * length * length * HD
     return pl.pallas_call(
         functools.partial(attend_kernel, sizes, tile),
         out_shape=(
             jax.ShapeDtypeStruct((rows * length, D), jnp.bfloat16),
-            jax.ShapeDtypeStruct((rows * pairs, 2, length), jnp.float32),
+            jax.ShapeDtypeStruct((rows * pairs, SIDE, length), jnp.float32),
         ),
         grid_spec=pltpu.PrefetchScalarGridSpec(
             num_scalar_prefetch=1,
@@ -154,10 +155,10 @@
                 pl.BlockSpec((1, 1, length), lambda i, j, t: (i, 0, 0)),
             ],
             out_specs=[
-                pl.BlockSpec((length, LANES), lambda i, j, t: (i, j)),
-                pl.BlockSpec((1, 2, length), lambda i, j, t: (i * pairs + j, 0, 0)),
+                pl.BlockSpec((length, SIDE * HD), lambda i, j, t: (i, j)),
+                pl.BlockSpec((1, SIDE, length), lambda i, j, t: (i * pairs + j, 0, 0)),
             ],
-            scratch_shapes=[pltpu.VMEM((LANES, length), jnp.bfloat16)],
+            scratch_shapes=[pltpu.VMEM((SIDE * HD, length), jnp.bfloat16)],
         ),
         compiler_params=pltpu.CompilerParams(vmem_limit_bytes=VMEM_LIMIT),
         cost_estimate=pl.CostEstimate(
@@ -194,7 +195,7 @@
                 here = q_ref[rows, :]
                 grad = g_ref[rows, :]
                 done = []
-                for half in range(2):
+                for half in range(SIDE):
                     lanes = head_lanes(half, here.shape)
                     mine = jnp.where(lanes, here * scale, 0.0).astype(jnp.bfloat16)
                     own = jnp.where(lanes, grad, 0.0).astype(jnp.bfloat16)
@@ -222,10 +223,10 @@
 
 
 def attend_back(table, project, grad, marks_col, marks_row, log_sum, rows, length):
-    pairs = HEADS * HD // LANES
+    pairs = HEADS // SIDE
     tile = min(TILE, length)
     sizes = windows_of(length)
-    columns = lambda part: pl.BlockSpec((length, LANES), lambda i, j, t: (i, part * pairs + j))
+    columns = lambda part: pl.BlockSpec((length, SIDE * HD), lambda i, j, t: (i, part * pairs + j))
     flops = 10 * rows * HEADS * length * length * HD
     return pl.pallas_call(
         functools.partial(attend_back_kernel, sizes, tile),
@@ -240,13 +241,13 @@
                 columns(0),
                 pl.BlockSpec((length, LANES), lambda i, j, t: (i, 0)),
                 pl.BlockSpec((1, 1, length), lambda i, j, t: (i, 0, 0)),
-                pl.BlockSpec((1, 2, length), lambda i, j, t: (i * pairs + j, 0, 0)),
+                pl.BlockSpec((1, SIDE, length), lambda i, j, t: (i * pairs + j, 0, 0)),
             ],
-            out_specs=pl.BlockSpec((3, length, LANES), lambda i, j, t: (0, i, j)),
+            out_specs=pl.BlockSpec((3, length, SIDE * HD), lambda i, j, t: (0, i, j)),
             scratch_shapes=[
-                pltpu.VMEM((LANES, length), jnp.bfloat16),
-                pltpu.VMEM((length, LANES), jnp.float32),
-                pltpu.VMEM((length, LANES), jnp.float32),
+                pltpu.VMEM((SIDE * HD, length), jnp.bfloat16),
+                pltpu.VMEM((length, SIDE * HD), jnp.float32),
+                pltpu.VMEM((length, SIDE * HD), jnp.float32),
             ],
         ),
         compiler_params=pltpu.CompilerParams(vmem_limit_bytes=VMEM_LIMIT),
@@ -446,26 +447,10 @@
     pl.semaphore_wait(barrier, len(peers))
 
 
-def gather_kernel(widths, starts, places, moves, shard_ref, *refs):
-    count = len(widths)
-    moved_in = refs[: len(moves)]
-    refs = refs[len(moves) :]
-    arrays = 1 + max(number for number, _ in places)
-    outs = refs[:arrays]
-    moved_out = refs[arrays : arrays + len(moves)]
-    refs = refs[arrays + len(moves) :]
-    send_sem, recv_sem, own_sem = refs[:3]
+def gather_tasks(widths, starts, places, shard_ref, outs, send_sem, recv_sem, own_sem):
     me = lax.axis_index("dp")
     sib, side_x, side_y, across = partners(me)
     _, sib_x, sib_y, sib_across = partners(sib)
-    peers = [("dp", sib), ("dp", side_x), ("dp", side_y)]
-    if moves:
-        z_send, z_recv, z_own, zeros_ref = refs[3:]
-        plane = lax.axis_index("seq")
-        planes = [(plane + step) % 4 for step in range(1, 4)]
-        peers += [("seq", place) for place in planes]
-        zeros_ref[...] = jnp.zeros_like(zeros_ref)
-    greet(peers)
     arrivals = [
         (side_x, None),
         (side_y, None),
@@ -477,7 +462,7 @@
         (sib_across, 0),
         (sib_across, 1),
     ]
-    sent = []
+    sent, kept = [], {}
 
     def rows_at(block, owner, part):
         number, first = places[block]
@@ -508,6 +493,41 @@
 
     def forward(block, kind, slot, owner, part, place):
         put(block, kind, slot, rows_at(block, owner, part), owner, part, place)
+
+    def begin(block):
+        mine = shard_ref.at[pl.ds(starts[block], widths[block])]
+        put(block, 0, 0, mine, me, None, side_x)
+        put(block, 1, 1, mine, me, None, side_y)
+        put(block, 4, 2, mine, me, None, sib)
+        copy = pltpu.make_async_copy(mine, rows_at(block, me, None), own_sem.at[block])
+        copy.start()
+        kept[block] = copy
+
+    def go_on(block):
+        arrived(block, 0)
+        forward(block, 2, 3, side_x, 0, side_y)
+        forward(block, 5, 4, side_x, None, sib)
+        arrived(block, 1)
+        forward(block, 3, 5, side_y, 1, side_x)
+        forward(block, 6, 6, side_y, None, sib)
+
+    def share(block):
+        arrived(block, 2)
+        forward(block, 7, 7, across, 0, sib)
+        arrived(block, 3)
+        forward(block, 8, 8, across, 1, sib)
+
+    def finish(block):
+        for kind in range(4, 9):
+            arrived(block, kind)
+        kept[block].wait()
+
+    return (begin, go_on, share, finish, sent)
+
+
+def move_task(moves, moved_in, moved_out, z_send, z_recv, z_own, zeros_ref):
+    plane = lax.axis_index("seq")
+    planes = [(plane + step) % 4 for step in range(1, 4)]
 
     def each_move(number, act_send, act_own, act_recv):
         source, target = moved_in[number], moved_out[number]
@@ -583,84 +603,89 @@
                         )
                     )
 
-    for number in range(len(moves)):
-        each_move(number, lambda copy: copy.start(), lambda copy: copy.start(), None)
-    kept = []
+    def start():
+        for number in range(len(moves)):
+            each_move(number, lambda copy: copy.start(), lambda copy: copy.start(), None)
+
+    def finish():
+        for number in range(len(moves)):
+            each_move(
+                number,
+                lambda copy: copy.wait_send(),
+                lambda copy: copy.wait(),
+                lambda copy: copy.wait_recv(),
+            )
+
+    return (start, finish)
+
+
+def greet_plane(with_planes):
+    me, plane = lax.axis_index("dp"), lax.axis_index("seq")
+    peers = [("dp", place) for place in partners(me)[:3]]
+    if with_planes:
+        peers += [("seq", (plane + step) % 4) for step in range(1, 4)]
+    greet(peers)
+
+
+def gather_kernel(widths, starts, places, moves, shard_ref, *refs):
+    count = len(widths)
+    moved_in = refs[: len(moves)]
+    refs = refs[len(moves) :]
+    arrays = 1 + max(number for number, _ in places)
+    outs = refs[:arrays]
+    moved_out = refs[arrays : arrays + len(moves)]
+    send_sem, recv_sem, own_sem, z_send, z_recv, z_own, zeros_ref = refs[arrays + len(moves) :]
+    zeros_ref[...] = jnp.zeros_like(zeros_ref)
+    greet_plane(True)
+    start, settle = move_task(moves, moved_in, moved_out, z_send, z_recv, z_own, zeros_ref)
+    begin, go_on, share, finish, sent = gather_tasks(
+        widths, starts, places, shard_ref, outs, send_sem, recv_sem, own_sem
+    )
+    start()
     for block in range(count):
-        mine = shard_ref.at[pl.ds(starts[block], widths[block])]
-        put(block, 0, 0, mine, me, None, side_x)
-        put(block, 1, 1, mine, me, None, side_y)
-        put(block, 4, 2, mine, me, None, sib)
-        copy = pltpu.make_async_copy(mine, rows_at(block, me, None), own_sem.at[block])
-        copy.start()
-        kept.append(copy)
+        begin(block)
     for step in range(count + 1):
         if step < count:
-            arrived(step, 0)
-            forward(step, 2, 3, side_x, 0, side_y)
-            forward(step, 5, 4, side_x, None, sib)
-            arrived(step, 1)
-            forward(step, 3, 5, side_y, 1, side_x)
-            forward(step, 6, 6, side_y, None, sib)
+            go_on(step)
         if step > 0:
-            arrived(step - 1, 2)
-            forward(step - 1, 7, 7, across, 0, sib)
-            arrived(step - 1, 3)
-            forward(step - 1, 8, 8, across, 1, sib)
+            share(step - 1)
     for block in range(count):
-        for kind in range(4, 9):
-            arrived(block, kind)
+        finish(block)
     for copy in sent:
         copy.wait_send()
-    for copy in kept:
-        copy.wait()
-    for number in range(len(moves)):
-        each_move(
-            number,
-            lambda copy: copy.wait_send(),
-            lambda copy: copy.wait(),
-            lambda copy: copy.wait_recv(),
-        )
-
-
-def plane_gather(shard, widths, starts, joined, moves=(), arrays=(), length=0):
+    settle()
+
+
+def gather_weights(shard, widths, starts, arrays, length):
     count = len(widths)
     depth = shard.shape[1]
-    if joined:
-        places = [(0, 8 * start) for start in starts]
-        out_shape = [jax.ShapeDtypeStruct((8 * sum(widths), depth), shard.dtype)]
-    else:
-        places = [(number, 0) for number in range(count)]
-        out_shape = [jax.ShapeDtypeStruct((8 * width, depth), shard.dtype) for width in widths]
-    scratch = [
-        pltpu.SemaphoreType.DMA((count, 9)),
-        pltpu.SemaphoreType.DMA((count, 9)),
-        pltpu.SemaphoreType.DMA((count,)),
-    ]
-    if moves:
-        quarter = length // 4
-        for kind in moves:
-            shape = (length, depth) if kind == "in" else (3, quarter, depth)
-            out_shape.append(jax.ShapeDtypeStruct(shape, shard.dtype))
-        scratch += [
-            pltpu.SemaphoreType.DMA((len(moves), 3)),
-            pltpu.SemaphoreType.DMA((len(moves), 4)),
-            pltpu.SemaphoreType.DMA((len(moves), 4)),
-            pltpu.VMEM((quarter, depth), shard.dtype),
-        ]
+    moves = ("in",) * len(arrays)
+    out_shape = [jax.ShapeDtypeStruct((8 * width, depth), shard.dtype) for width in widths]
+    out_shape += [jax.ShapeDtypeStruct((length, depth), shard.dtype) for _ in moves]
+    dma = pltpu.SemaphoreType.DMA
     return pl.pallas_call(
-        functools.partial(gather_kernel, widths, starts, places, moves),
+        functools.partial(
+            gather_kernel, widths, starts, [(number, 0) for number in range(count)], moves
+        ),
         out_shape=tuple(out_shape),
         in_specs=[pl.BlockSpec(memory_space=pltpu.VMEM)] * (1 + len(moves)),
         out_specs=tuple(pl.BlockSpec(memory_space=pl.ANY) for _ in out_shape),
-        scratch_shapes=scratch,
+        scratch_shapes=[
+            dma((count, 9)),
+            dma((count, 9)),
+            dma((count,)),
+            dma((len(moves), 3)),
+            dma((len(moves), 4)),
+            dma((len(moves), 4)),
+            pltpu.VMEM((length // 4, depth), shard.dtype),
+        ],
         compiler_params=pltpu.CompilerParams(
-            collective_id=4 if joined else 1, has_side_effects=True, vmem_limit_bytes=16 * 1024 * 1024
+            collective_id=1, has_side_effects=True, vmem_limit_bytes=16 * 1024 * 1024
         ),
         cost_estimate=pl.CostEstimate(
             flops=0, bytes_accessed=8 * 16 * shard.shape[0] * depth, transcendentals=0
         ),
-        name="gather_steps" if joined else "gather_weights",
+        name="gather_weights",
     )(shard, *arrays)
 
 
@@ -956,18 +981,22 @@
         copy.wait()
 
 
+def pieces_of(widths, starts, joined):
+    pieces = []
+    for which in (2, 3, 0, 1):
+        width, start = widths[which], starts[which]
+        number, first = (0, 8 * start) if joined else (which, 0)
+        size = next(size for size in (192, 96, width) if width % size == 0)
+        pieces += [(size, start + cut, (number, first + cut, width)) for cut in range(0, width, size)]
+    return [list(part) for part in zip(*pieces)]
+
+
 def plane_reduce(terms, widths, starts, small=None):
     share = sum(widths)
     depth = terms[0].shape[1]
     across_planes = small is not None
-    pieces = []
-    for which in (2, 3, 0, 1):
-        width, start = widths[which], starts[which]
-        number, first = (0, 8 * start) if len(terms) == 1 else (which, 0)
-        size = next(size for size in (192, 96, width) if width % size == 0)
-        pieces += [(size, start + cut, (number, first + cut, width)) for cut in range(0, width, size)]
-    widths, starts, places = [list(part) for part in zip(*pieces)]
-    count = len(pieces)
+    widths, starts, places = pieces_of(widths, starts, len(terms) == 1)
+    count = len(widths)
     low = terms[0].dtype
     whole = pltpu.VMEM((share, depth), low)
     half = pltpu.VMEM((share // 2, depth), low)
@@ -1031,153 +1060,470 @@
     )(*operands)
 
 
-def basis_specs():
-    return [
-        pl.BlockSpec((1, D, D), lambda g: (g + jnp.minimum(g, 1), 0, 0)),
-        pl.BlockSpec((1, D, D), lambda g: (1, 0, 0)),
-    ]
-
-
-def turn_kernel(joint, grad_ref, basis_ref, basis_out_ref, right_ref, reduced_ref, term_ref):
-    group = pl.program_id(0)
-    grad = grad_ref[...]
-    reduced_ref[...] = grad.astype(jnp.float32).T
-    basis = low_of(basis_ref[0])
-
-    def spread(rows, turned, begin, columns):
-        for step in range(columns // D):
-            right = low_of(right_ref[rows, step * D : (step + 1) * D].T)
-            term_ref[begin + step * D : begin + (step + 1) * D, :] = low_of(
-                jnp.dot(right, turned, preferred_element_type=jnp.float32)
+GROUPS = (1, 2, 0)
+PART = 384
+
+
+def group_parts(group, joint):
+    if group == 0:
+        return [(0, joint, 0), (joint, PART, 1)]
+    return [(0, PART, group + 1)]
+
+
+def group_chunks(group, joint):
+    if group == 0:
+        return [(0, step * D) for step in range(3)] + [(1, 0)]
+    return [(0, step * D) for step in range(4)]
+
+
+class Stream:
+    def __init__(self, copies):
+        self.copies, self.next = copies, 0
+        for copy in copies[:2]:
+            copy.start()
+
+    def take(self):
+        self.copies[self.next].wait()
+        self.next += 1
+        return (self.next - 1) % 2
+
+    def free(self):
+        if self.next + 1 < len(self.copies):
+            self.copies[self.next + 1].start()
+
+
+def optimize_kernel(
+    block_widths,
+    block_starts,
+    grad_ref,
+    output_ref,
+    input_grad_ref,
+    right_ref,
+    bases_ref,
+    first_ref,
+    second_ref,
+    weights_ref,
+    reduced_out,
+    first_out,
+    second_out,
+    new_out,
+    low_out,
+    every_out,
+    output_out,
+    input_grad_out,
+    term,
+    given,
+    from_x,
+    from_y,
+    turn_x,
+    turn_y,
+    total,
+    shard,
+    right_buf,
+    basis_buf,
+    first_buf,
+    second_buf,
+    wide_buf,
+    low_buf,
+    every_buf,
+    sib_send,
+    sib_recv,
+    link_send,
+    link_recv,
+    gather_send,
+    gather_recv,
+    gather_own,
+    z_send,
+    z_recv,
+    z_own,
+    right_sem,
+    basis_sem,
+    in_sem,
+    out_sem,
+    every_sem,
+):
+    joint = block_widths[0]
+    me = lax.axis_index("dp")
+    sib, side_x, side_y, across = partners(me)
+    _, sib_x, sib_y, sib_across = partners(sib)
+    owners = (me, side_x, side_y, across)
+    sib_owners = (sib, sib_x, sib_y, sib_across)
+    widths, starts, places = pieces_of(block_widths, block_starts, True)
+
+    right_loads, basis_loads = [], []
+    for group in GROUPS + GROUPS:
+        parts = group_parts(group, joint)
+        for part, column in group_chunks(group, joint):
+            low, high, _ = parts[part]
+            slot = len(right_loads) % 2
+            right_loads.append(
+                pltpu.make_async_copy(
+                    right_ref.at[pl.ds(PART * group + low, high - low), pl.ds(column, D)],
+                    right_buf.at[slot, pl.ds(0, high - low)],
+                    right_sem.at[slot],
+                )
             )
-
-    @pl.when(group == 0)
-    def _():
-        turned = low_of(jnp.dot(grad[:joint], basis, preferred_element_type=jnp.float32))
-        spread(slice(0, joint), turned, 0, 3 * D)
-        other = low_of(basis_out_ref[0])
-        turned = low_of(jnp.dot(grad[joint:], other, preferred_element_type=jnp.float32))
-        spread(slice(joint, grad.shape[0]), turned, 3 * D, D)
-
-    @pl.when(group != 0)
-    def _():
-        turned = low_of(jnp.dot(grad, basis, preferred_element_type=jnp.float32))
-        spread(slice(None), turned, 0, FF)
-
-
-def turn(grad, bases, right_bases, joint):
+        for _, _, basis in parts:
+            slot = len(basis_loads) % 2
+            basis_loads.append(
+                pltpu.make_async_copy(bases_ref.at[basis], basis_buf.at[slot], basis_sem.at[slot])
+            )
+
+    def columns(ref, group):
+        return ref.at[:, pl.ds(PART * group, PART)]
+
+    def load_moments(turn):
+        for number, (ref, buf) in enumerate(((first_ref, first_buf), (second_ref, second_buf))):
+            copy = pltpu.make_async_copy(
+                columns(ref, GROUPS[turn]), buf.at[turn % 2], in_sem.at[number, turn % 2]
+            )
+            copy.start()
+            moment_loads[number, turn] = copy
+
+    def put_out(number, buf, ref, turn):
+        copy = pltpu.make_async_copy(
+            buf.at[turn % 2], columns(ref, GROUPS[turn]), out_sem.at[number, turn % 2]
+        )
+        copy.start()
+        outgoing[number, turn] = copy
+
+    moment_loads, outgoing, sends, kept = {}, {}, [], {}
+    greet_plane(True)
+    move_start, move_finish = move_task(
+        ("out", "out"),
+        (output_ref, input_grad_ref),
+        (output_out, input_grad_out),
+        z_send,
+        z_recv,
+        z_own,
+        None,
+    )
+    rights, bases = Stream(right_loads), Stream(basis_loads)
+    move_start()
+    for turn in range(2):
+        load_moments(turn)
+
+
+    def turn_group(turn, between):
+        group = GROUPS[turn]
+        parts = group_parts(group, joint)
+        rows = slice(PART * group, PART * (group + 1))
+        grad = grad_ref[rows, :]
+        if turn >= 2:
+            outgoing[0, turn - 2].wait()
+        wide_buf[turn % 2] = grad.astype(jnp.float32).T
+        put_out(0, wide_buf, reduced_out, turn)
+        turned = []
+        for low, high, _ in parts:
+            slot = bases.take()
+            turned.append(
+                low_of(
+                    jnp.dot(
+                        grad[low:high], low_of(basis_buf[slot]), preferred_element_type=jnp.float32
+                    )
+                )
+            )
+            bases.free()
+        for number, (part, _) in enumerate(group_chunks(group, joint)):
+            low, high, _ = parts[part]
+            slot = rights.take()
+            right = low_of(right_buf[slot, 0 : high - low, :].T)
+            begin = FF * group + D * number
+            term[begin : begin + D, :] = low_of(
+                jnp.dot(right, turned[part], preferred_element_type=jnp.float32)
+            )
+            rights.free()
+            for task in between[number]:
+                task()
+
+    def place_of(piece, owner):
+        _, first, stride = places[piece]
+        return pl.multiple_of(first + owner * stride, 16)
+
+    def begin(piece):
+        size = widths[piece]
+        for which in (3, 1, 2, 0):
+            copy = send(
+                term.at[pl.ds(place_of(piece, sib_owners[which]), size)],
+                given.at[which, pl.ds(starts[piece], size)],
+                sib_send.at[piece, which],
+                sib_recv.at[piece, which],
+                "dp",
+                sib,
+            )
+            copy.start()
+            sends.append(copy)
+            kept[piece, which] = copy
+
+    def link(piece, slot, source, target, place):
+        copy = send(source, target, link_send.at[piece, slot], link_recv.at[piece, slot], "dp", place)
+        copy.start()
+        sends.append(copy)
+
+    def landed(piece, slot, region):
+        send(region, region, link_send.at[piece, slot], link_recv.at[piece, slot], "dp", sib).wait_recv()
+
+    def own_half(piece, which, part):
+        half = widths[piece] // 2
+        return pl.multiple_of(place_of(piece, owners[which]) + part * half, 16)
+
+    def own_rows(piece, which, part):
+        return term.at[pl.ds(own_half(piece, which, part), widths[piece] // 2)]
+
+    def share_rows(ref, piece, part):
+        half = widths[piece] // 2
+        return ref.at[pl.ds(starts[piece] + part * half, half)]
+
+    def turn_rows(ref, piece):
+        return ref.at[pl.ds(starts[piece] // 2, widths[piece] // 2)]
+
+    def pair_sum(piece, which):
+        kept[piece, which].wait_recv()
+        here = place_of(piece, owners[which])
+        add_rows(term, here, [(term, here), (given.at[which], starts[piece])], widths[piece])
+
+    def first_stage(piece):
+        pair_sum(piece, 3)
+        link(piece, 0, own_rows(piece, 3, 0), turn_rows(turn_x, piece), side_x)
+        link(piece, 1, own_rows(piece, 3, 1), turn_rows(turn_y, piece), side_y)
+        pair_sum(piece, 1)
+        link(piece, 2, own_rows(piece, 1, 0), share_rows(from_x, piece, 0), side_x)
+        pair_sum(piece, 2)
+        link(piece, 3, own_rows(piece, 2, 1), share_rows(from_y, piece, 1), side_y)
+        pair_sum(piece, 0)
+
+    def second_stage(piece):
+        half = widths[piece] // 2
+        landed(piece, 0, turn_rows(turn_x, piece))
+        here = own_half(piece, 2, 0)
+        add_rows(term, here, [(term, here), (turn_x, starts[piece] // 2)], half)
+        link(piece, 4, own_rows(piece, 2, 0), share_rows(from_y, piece, 0), side_y)
+        landed(piece, 1, turn_rows(turn_y, piece))
+        here = own_half(piece, 1, 1)
+        add_rows(term, here, [(term, here), (turn_y, starts[piece] // 2)], half)
+        link(piece, 5, own_rows(piece, 1, 1), share_rows(from_x, piece, 1), side_x)
+
+    def third_stage(piece):
+        landed(piece, 2, share_rows(from_x, piece, 0))
+        landed(piece, 5, share_rows(from_x, piece, 1))
+        landed(piece, 3, share_rows(from_y, piece, 1))
+        landed(piece, 4, share_rows(from_y, piece, 0))
+        here = starts[piece]
+        add_rows(
+            total,
+            here,
+            [(term, place_of(piece, me)), (from_x, here), (from_y, here)],
+            widths[piece],
+        )
+
+
+    def adam_group(turn):
+        group = GROUPS[turn]
+        slot = turn % 2
+        for number in range(2):
+            moment_loads[number, turn].wait()
+        rows = slice(PART * group, PART * (group + 1))
+        rotated = total[rows, :].astype(jnp.float32).T
+        first, second, heading = moments(rotated, first_buf[slot], second_buf[slot])
+        first_buf[slot] = first
+        second_buf[slot] = second
+        put_out(1, first_buf, first_out, turn)
+        put_out(2, second_buf, second_out, turn)
+        heading = low_of(heading.T)
+        for low, high, _ in group_parts(group, joint):
+            basis = bases.take()
+            shard[PART * group + low : PART * group + high, :] = low_of(
+                dot_dims(heading[low:high], low_of(basis_buf[basis]), 1, 1)
+            )
+            bases.free()
+        if turn == 1:
+            for number in (1, 2):
+                outgoing[number, 0].wait()
+            load_moments(2)
+
+    every_places = [(0, 8 * start) for start in block_starts]
+    g_begin, g_go_on, g_share, g_finish, g_sent = gather_tasks(
+        block_widths, block_starts, every_places, shard, [every_out], gather_send, gather_recv, gather_own
+    )
+
+
+    def load_weights(turn):
+        copy = pltpu.make_async_copy(
+            columns(weights_ref, GROUPS[turn]), wide_buf.at[turn % 2], in_sem.at[2, turn % 2]
+        )
+        copy.start()
+        moment_loads[2, turn] = copy
+
+    def update_group(turn):
+        group = GROUPS[turn]
+        slot = turn % 2
+        parts = group_parts(group, joint)
+        chunks = group_chunks(group, joint)
+        loads = Stream(
+            [
+                pltpu.make_async_copy(
+                    every_out.at[pl.ds(FF * group + D * number, D)],
+                    every_buf.at[number % 2],
+                    every_sem.at[number % 2],
+                )
+                for number in range(4)
+            ]
+        )
+        sums = [None] * len(parts)
+        for number, (part, _) in enumerate(chunks):
+            low, high, _ = parts[part]
+            right = rights.take()
+            here = loads.take()
+            piece = jnp.dot(
+                low_of(right_buf[right, 0 : high - low, :]),
+                every_buf[here],
+                preferred_element_type=jnp.float32,
+            )
+            sums[part] = piece if sums[part] is None else sums[part] + piece
+            rights.free()
+            loads.free()
+        update = sums[0] if len(sums) == 1 else jnp.concatenate(sums, axis=0)
+        moment_loads[2, turn].wait()
+        new = wide_buf[slot] - learn_rate * update.T
+        if turn >= 2:
+            outgoing[4, turn - 2].wait()
+        wide_buf[slot] = new
+        low_buf[slot] = low_of(new)
+        put_out(3, wide_buf, new_out, turn)
+        put_out(4, low_buf, low_out, turn)
+
+    turn_group(0, [[], [], [], []])
+    for piece in (0, 1):
+        begin(piece)
+    do = lambda act, piece: lambda: act(piece)
+    turn_group(
+        1, [[do(first_stage, 0)], [do(first_stage, 1)], [do(second_stage, 0)], [do(second_stage, 1)]]
+    )
+    for piece in (2, 3):
+        begin(piece)
+    turn_group(
+        2,
+        [[do(first_stage, 2)], [do(first_stage, 3)], [do(third_stage, 0)], [do(second_stage, 2)]],
+    )
+    for piece in (4, 5, 6, 7):
+        begin(piece)
+    third_stage(1)
+    first_stage(4)
+    first_stage(5)
+    adam_group(0)
+    g_begin(2)
+    second_stage(3)
+    first_stage(6)
+    first_stage(7)
+    third_stage(2)
+    third_stage(3)
+    second_stage(4)
+    second_stage(5)
+    adam_group(1)
+    g_begin(3)
+    second_stage(6)
+    second_stage(7)
+    outgoing[0, 1].wait()
+    outgoing[0, 2].wait()
+    load_weights(0)
+    load_weights(1)
+    for piece in (4, 5, 6, 7):
+        third_stage(piece)
+    adam_group(2)
+    g_begin(0)
+    g_begin(1)
+    g_go_on(2)
+    g_go_on(3)
+    g_share(2)
+    g_finish(2)
+    update_group(0)
+    g_go_on(0)
+    g_go_on(1)
+    g_share(3)
+    g_finish(3)
+    update_group(1)
+    g_share(0)
+    g_share(1)
+    outgoing[3, 0].wait()
+    load_weights(2)
+    g_finish(0)
+    g_finish(1)
+    update_group(2)
+    for copy in sends + g_sent:
+        copy.wait_send()
+    for number, turn in ((1, 1), (1, 2), (2, 1), (2, 2), (3, 1), (3, 2), (4, 1), (4, 2)):
+        outgoing[number, turn].wait()
+    move_finish()
+
+
+def optimize(
+    grad, output, input_grad, right_bases, bases, first_moment, second_moment, weights, widths, starts
+):
     share = grad.shape[0]
-    part = share // 3
+    length = output.shape[0]
+    low = grad.dtype
+    pieces = len(pieces_of(widths, starts, True)[0])
+    any_spec = pl.BlockSpec(memory_space=pl.ANY)
+    vmem_spec = pl.BlockSpec(memory_space=pltpu.VMEM)
+    wide = jax.ShapeDtypeStruct((D, share), jnp.float32)
+    moved = jax.ShapeDtypeStruct((3, length // 4, D), low)
+    dma = pltpu.SemaphoreType.DMA
+    whole = pltpu.VMEM((share, D), low)
+    half = pltpu.VMEM((share // 2, D), low)
     return pl.pallas_call(
-        functools.partial(turn_kernel, joint),
-        grid=(3,),
+        functools.partial(optimize_kernel, widths, starts),
         out_shape=(
-            jax.ShapeDtypeStruct((D, share), jnp.float32),
-            jax.ShapeDtypeStruct((3 * FF, D), jnp.bfloat16),
+            wide,
+            wide,
+            wide,
+            wide,
+            jax.ShapeDtypeStruct((D, share), low),
+            jax.ShapeDtypeStruct((8 * share, D), low),
+            moved,
+            moved,
         ),
-        in_specs=[pl.BlockSpec((part, D), lambda g: (g, 0))]
-        + basis_specs()
-        + [pl.BlockSpec((part, FF), lambda g: (g, 0))],
-        out_specs=(
-            pl.BlockSpec((D, part), lambda g: (0, g)),
-            pl.BlockSpec((FF, D), lambda g: (g, 0)),
+        in_specs=[vmem_spec] * 3 + [any_spec] * 5,
+        out_specs=(any_spec,) * 8,
+        scratch_shapes=[
+            pltpu.VMEM((8 * share, D), low),
+            pltpu.VMEM((4, share, D), low),
+            whole,
+            whole,
+            half,
+            half,
+            whole,
+            whole,
+            pltpu.VMEM((2, PART, D), jnp.float32),
+            pltpu.VMEM((2, D, D), jnp.float32),
+            pltpu.VMEM((2, D, PART), jnp.float32),
+            pltpu.VMEM((2, D, PART), jnp.float32),
+            pltpu.VMEM((2, D, PART), jnp.float32),
+            pltpu.VMEM((2, D, PART), low),
+            pltpu.VMEM((2, D, D), low),
+            dma((pieces, 4)),
+            dma((pieces, 4)),
+            dma((pieces, 6)),
+            dma((pieces, 6)),
+            dma((4, 9)),
+            dma((4, 9)),
+            dma((4,)),
+            dma((2, 3)),
+            dma((2, 4)),
+            dma((2, 4)),
+            dma((2,)),
+            dma((2,)),
+            dma((3, 2)),
+            dma((5, 2)),
+            dma((2,)),
+        ],
+        compiler_params=pltpu.CompilerParams(
+            collective_id=4, has_side_effects=True, vmem_limit_bytes=67043328
         ),
-        compiler_params=pltpu.CompilerParams(vmem_limit_bytes=VMEM_LIMIT),
         cost_estimate=pl.CostEstimate(
-            flops=2 * share * D * (D + FF), bytes_accessed=4 * share * (FF + D) + 6 * FF * D, transcendentals=0
+            flops=4 * share * D * (D + FF), bytes_accessed=8 * 40 * share * D, transcendentals=0
         ),
-        name="turn",
-    )(grad, bases, bases, right_bases)
-
-
-def adam_kernel(
-    joint, rotated_ref, first_ref, second_ref, basis_ref, basis_out_ref, first_out, second_out, step_ref
-):
-    group = pl.program_id(0)
-    rotated = rotated_ref[...].astype(jnp.float32).T
-    first, second, heading = moments(rotated, first_ref[...], second_ref[...])
-    first_out[...] = first
-    second_out[...] = second
-    heading = low_of(heading.T)
-    basis = low_of(basis_ref[0])
-
-    @pl.when(group == 0)
-    def _():
-        other = low_of(basis_out_ref[0])
-        step_ref[:joint, :] = low_of(dot_dims(heading[:joint], basis, 1, 1))
-        step_ref[joint:, :] = low_of(dot_dims(heading[joint:], other, 1, 1))
-
-    @pl.when(group != 0)
-    def _():
-        step_ref[...] = low_of(dot_dims(heading, basis, 1, 1))
-
-
-def adam(rotated, first_moment, second_moment, bases, joint):
-    share = rotated.shape[0]
-    part = share // 3
-    rows = pl.BlockSpec((part, D), lambda g: (g, 0))
-    columns = pl.BlockSpec((D, part), lambda g: (0, g))
-    wide = jax.ShapeDtypeStruct((D, share), jnp.float32)
-    return pl.pallas_call(
-        functools.partial(adam_kernel, joint),
-        grid=(3,),
-        out_shape=(wide, wide, jax.ShapeDtypeStruct((share, D), jnp.bfloat16)),
-        in_specs=[rows, columns, columns] + basis_specs(),
-        out_specs=(columns, columns, rows),
-        compiler_params=pltpu.CompilerParams(vmem_limit_bytes=VMEM_LIMIT),
-        cost_estimate=pl.CostEstimate(
-            flops=2 * share * D * D, bytes_accessed=20 * share * D, transcendentals=share * D
-        ),
-        name="adam",
-    )(rotated, first_moment, second_moment, bases, bases)
-
-
-def update_kernel(joint, every_ref, right_ref, weights_ref, new_ref, low_ref):
-    group = pl.program_id(0)
-
-    def finish(update):
-        new = weights_ref[...] - learn_rate * update.T
-        new_ref[...] = new
-        low_ref[...] = low_of(new)
-
-    @pl.when(group == 0)
-    def _():
-        upper = jnp.dot(
-            low_of(right_ref[:joint, : 3 * D]), every_ref[: 3 * D, :], preferred_element_type=jnp.float32
-        )
-        lower = jnp.dot(
-            low_of(right_ref[joint:, :D]), every_ref[3 * D :, :], preferred_element_type=jnp.float32
-        )
-        finish(jnp.concatenate([upper, lower], axis=0))
-
-    @pl.when(group != 0)
-    def _():
-        finish(jnp.dot(low_of(right_ref[...]), every_ref[...], preferred_element_type=jnp.float32))
-
-
-def apply_update(every, right_bases, weights, joint):
-    share = weights.shape[1]
-    part = share // 3
-    columns = pl.BlockSpec((D, part), lambda g: (0, g))
-    return pl.pallas_call(
-        functools.partial(update_kernel, joint),
-        grid=(3,),
-        out_shape=(
-            jax.ShapeDtypeStruct((D, share), jnp.float32),
-            jax.ShapeDtypeStruct((D, share), jnp.bfloat16),
-        ),
-        in_specs=[
-            pl.BlockSpec((FF, D), lambda g: (g, 0)),
-            pl.BlockSpec((part, FF), lambda g: (g, 0)),
-            columns,
-        ],
-        out_specs=(columns, columns),
-        compiler_params=pltpu.CompilerParams(vmem_limit_bytes=VMEM_LIMIT),
-        cost_estimate=pl.CostEstimate(
-            flops=2 * share * D * FF, bytes_accessed=4 * share * FF + 16 * share * D, transcendentals=0
-        ),
-        name="apply_update",
-    )(every, right_bases, weights)
+        name="optimize",
+    )(grad, output, input_grad, right_bases, bases, first_moment, second_moment, weights)
 
 
 def on_device(
@@ -1223,8 +1569,8 @@
     on_plane = owners == 8 and groups == 4 and number == 3
     shard = weights.astype(jnp.bfloat16).T
     if on_plane:
-        w_qkv, w_out, w_up, w_down, x, pull = plane_gather(
-            shard, block_widths, block_starts, False, ("in", "in"), (inputs, cotangent), length
+        w_qkv, w_out, w_up, w_down, x, pull = gather_weights(
+            shard, block_widths, block_starts, (inputs, cotangent), length
         )
     else:
         x = to_rows(inputs)
@@ -1274,18 +1620,22 @@
     )
     grads = [grad_qkv, grad_outw, grad_up, grad_down]
     if on_plane:
-        joint = block_widths[0]
         mine, small_grad = plane_reduce(
             grads, block_widths, block_starts, small_local.reshape(-1, LANES)
         )
         small_grad = small_grad.reshape(-1)
-        reduced, term = turn(mine, bases, right_bases, joint)
-        (rotated,) = plane_reduce([term], block_widths, block_starts)
-        first_new, second_new, step = adam(rotated, first_moment, second_moment, bases, joint)
-        every, output, input_grad = plane_gather(
-            step, block_widths, block_starts, True, ("out", "out"), (output, input_grad), length
+        reduced, first_new, second_new, weights_new, weights_low, _, output, input_grad = optimize(
+            mine,
+            output,
+            input_grad,
+            right_bases,
+            bases,
+            first_moment,
+            second_moment,
+            weights,
+            block_widths,
+            block_starts,
         )
-        weights_new, weights_low = apply_update(every, right_bases, weights, joint)
     else:
         output = to_quarters(output)
         input_grad = to_quarters(input_grad)

time: 557 us -> 522 us (0.937)
  Pallas kernels: 466 us -> 430 us
  local copies, waits for them, and re-layouts: 35.9 us -> 42.4 us
    pallas_call x2 -> x1, Pallas kernels: 178 us -> 92.8 us  [plane_reduce(): pl.pallas_call(functools.partial(reduce_kernel, widths, starts, places, a...]
    pallas_call x5 -> x2, Pallas kernels: 182 us -> 224 us  [the longest x1 158 us: optimize(): pl.pallas_call(functools.partial(optimize_kernel, widths, starts), out_sh...]
    unnamed x74 -> x81, local copies, waits for them, and re-layouts: 29.2 us -> 35.6 us
    pallas_call x1, Pallas kernels: 33.7 us -> 39.5 us  [attend_back(): pl.pallas_call(functools.partial(attend_back_kernel, sizes, tile), out_sh...]
where the time goes in v5:
time: 522 us; the launch traced here: 514 us
  Pallas kernels  430 us (82%)
  local copies, waits for them, and re-layouts  42.4 us (8%)
  matrix products  33.6 us (6%)
  other arithmetic  6.22 us (1%)
    pallas_call x1, Pallas kernels, optimize(): pl.pallas_call(functools.partial(optimize_kernel, widths, starts), out_sh...  158 us
    pallas_call x1, Pallas kernels, plane_reduce(): pl.pallas_call(functools.partial(reduce_kernel, widths, starts, places, a...  92.8 us
    pallas_call x1, Pallas kernels, gather_weights(): pl.pallas_call(functools.partial(gather_kernel, widths, starts, [(number,...  66.9 us
    pallas_call x1, Pallas kernels, layer(): pl.pallas_call(layer_kernel, grid=(tokens // tile,), out_shape=(low_narro...  43.2 us
    pallas_call x1, Pallas kernels, attend_back(): pl.pallas_call(functools.partial(attend_back_kernel, sizes, tile), out_sh...  39.5 us
    unnamed x81, local copies, waits for them, and re-layouts  35.6 us
    dot_general x10, matrix products, dot_dims(): lax.dot_general(left, right, (((left_dim,), (right_dim,)), ((), ())), pre...  33.6 us
    pallas_call x1, Pallas kernels, attend(): pl.pallas_call(functools.partial(attend_kernel, sizes, tile), out_shape=(...  30.4 us

profile of v5, /device:TPU:1, one launch (start us, length us, event | category | flops | bytes accessed | tf_op | source)
XLA Modules:
  0.0 514.0 jit_solution(1388227547179462280)
XLA Ops:
  0.7 0.7 fusion.6
  1.9 1.4 gather_fusion
  3.4 0.6 reshape.391.table
  4.0 0.8 fusion.14
  4.8 1.3 slice.69
  6.1 0.7 slice.67
  6.9 0.6 slice.68.small_ref
  7.5 1.0 broadcast_in_dim.7.col_ref
  8.5 3.1 copy.28
  11.6 1.3 copy-done.1
  12.8 66.9 %gather_weights.1 = (bf16[2304,768]{1,0:T(8,128)(2,1)S(1)}, bf16[768,768]{1,0:T(8,128)(2,1)S(1)}, bf16[3072,768]{1,0:T(8,128)(2,1)S(1)}, bf16[3072,768]{1,0:T(8,...) custom-call(bf16[1152,768]{1,0:T(8,128)(2,1)S(1)} %bitcast.63, ...), custom_call_target="tpu_custom_call" | custom-call | bytes 113246208 | tf_op jit(solution)/shard_map/gather_weights/pallas_call | solution.py:666
  79.7 2.2 copy-done.6
  81.9 2.2 copy-done.7
  84.1 1.1 copy-done.11
  85.2 1.0 copy-done.12
  86.2 1.8 copy-done.2
  88.5 5.4 %add_convert_fusion.q_ref.k_ref.v_ref = bf16[1024,2304]{1,0:T(8,128)(2,1)} fusion(bf16[1024,768]{1,0:T(8,128)(2,1)S(1)} %get-tuple-element.37.x_ref, bf16[2304,768]{1,0:T(8,128)(2,1)S(1)} %get-tuple-element.38, f32[2304]{0:T(1024)S(1)} %pad_maximum_fusion.1), kind=kOutput, calls=%fused_computation.1 | convolution fusion | flops 3628597248 | bytes 9839616 | tf_op jit(solution)/shard_map/dot_general | solution.py:34
  94.0 30.4 %attend.1 = (bf16[1024,768]{1,0:T(8,128)(2,1)}, f32[3,4,1024]{2,1,0:T(4,128)}) custom-call(s32[1,8]{1,0:T(1,128)} %reshape.391.table, bf16[1024,2304]{1,0:T(8,128)(2,1)} %add_convert_fusion.q_ref.k_ref.v_ref, bf16[1024,2304]{1,0:T(8,128)(2,1)} %add_convert_fusion.q_ref.k_ref.v_ref, bf16[1024,2304]{1,0:T(8,128)(2,1)} %add_convert_fusion.q_ref.k_ref.v_ref, ...), custom_call_target="tpu_custom_call" | custom-call | flops 3221225472 | bytes 6291456 | tf_op jit(solution)/shard_map/attend/pallas_call | solution.py:141
  124.3 43.2 %layer.1 = (bf16[1024,768]{1,0:T(8,128)(2,1)}, bf16[1024,768]{1,0:T(8,128)(2,1)}, bf16[1024,3072]{1,0:T(8,128)(2,1)}, bf16[1024,768]{1,0:T(8,128)(2,1)}, bf16[10...) custom-call(bf16[1024,768]{1,0:T(8,128)(2,1)} %get-tuple-element.39., ...), custom_call_target="tpu_custom_call" | custom-call | flops 21743271936 | bytes 34209792 | tf_op jit(solution)/shard_map/layer/pallas_call | solution.py:376
  167.6 2.8 convolution_convert_fusion.2.refs_1_
  170.4 39.5 %attend_back.1 = bf16[3,1024,768]{2,1,0:T(8,128)(2,1)} custom-call(s32[1,8]{1,0:T(1,128)} %reshape.391.table, bf16[1024,2304]{1,0:T(8,128)(2,1)} %add_convert_fusion.q_ref.k_ref.v_ref, bf16[1024,2304]{1,0:T(8,128)(2,1)} %add_convert_fusion.q_ref.k_ref.v_ref, bf16[1024,2304]{1,0:T(8,128)(2,1)} %add_convert_fusion.q_ref.k_ref.v_ref, ...), custom_call_target="tpu_custom_call" | custom-call | flops 8053063680 | bytes 11010048 | tf_op jit(solution)/shard_map/attend_back/pallas_call | solution.py:231
  210.1 2.5 convert_reduce_fusion
  212.7 2.9 convolution_convert_fusion.3
  215.6 1.4 convolution_convert_fusion.4
  217.1 1.4 convolution_convert_fusion.5
  218.5 2.0 pad_maximum_fusion.refs_0_
  220.5 1.3 copy-done.3
  221.8 1.4 fusion.1
  223.2 1.4 fusion
  224.7 2.7 add_convert_fusion.1.input_grad_ref
  227.4 6.9 %convolution_convert_fusion.1.refs_2_ = bf16[3072,768]{1,0:T(8,128)(2,1)} fusion(bf16[1024,3072]{1,0:T(8,128)(2,1)S(1)} %bitcast.79, bf16[1024,768]{1,0:T(8,128)(2,1)S(1)} %copy-done.27), kind=kOutput, calls=%fused_computation.3 | convolution fusion | flops 4834197504 | bytes 12582912 | tf_op jit(solution)/shard_map/dot_general | solution.py:34
  234.3 7.1 %convolution_convert_fusion.refs_3_ = bf16[3072,768]{1,0:T(8,128)(2,1)} fusion(bf16[1024,3072]{1,0:T(8,128)(2,1)S(1)} %bitcast.77, bf16[1024,768]{1,0:T(8,128)(2,1)S(1)} %copy-done.26), kind=kOutput, calls=%fused_computation.2 | convolution fusion | flops 4834197504 | bytes 12582912 | tf_op jit(solution)/shard_map/dot_general | solution.py:34
  241.4 92.8 %reduce_all.1 = (bf16[1152,768]{1,0:T(8,128)(2,1)S(1)}, f32[72,128]{1,0:T(8,128)S(1)}) custom-call(bf16[2304,768]{1,0:T(8,128)(2,1)} %pad_maximum_fusion.refs_0_, bf16[768,768]{1,0:T(8,128)(2,1)S(1)} %convolution_convert_fusion.2.refs_1_, bf16[3072,768]{1,0:T(8,128)(2,1)} %convolution_convert_fusion.1.refs_2_, ...), custom_call_target="tpu_custom_call" | custom-call | bytes 141557760 | tf_op jit(solution)/shard_map/reduce_all/pallas_call | solution.py:1045
  334.2 1.2 copy-done.8
  336.0 0.7 multiply_subtract_fusion
  336.7 157.6 %optimize.1 = (f32[768,1152]{1,0:T(8,128)}, f32[768,1152]{1,0:T(8,128)}, f32[768,1152]{1,0:T(8,128)}, f32[768,1152]{1,0:T(8,128)}, bf16[768,1152]{1,0:T(8,128)(2...) custom-call(bf16[1152,768]{1,0:T(8,128)(2,1)} %copy-done.8, ...), custom_call_target="tpu_custom_call" | custom-call | flops 13589544960 | bytes 283115520 | tf_op jit(solution)/shard_map/optimize/pallas_call | solution.py:1473
  494.3 2.5 copy.41
  496.8 2.4 copy.42
  499.2 1.8 copy.43
  501.0 1.5 copy-done.15
  502.5 1.8 copy.44
  504.3 1.5 copy-done.14
  505.7 1.8 copy.45
  507.5 1.5 copy-done.13
  509.0 1.8 copy.46
  510.8 0.9 copy-done.17
  511.8 1.2 copy.47
  513.0 0.6 copy.48
  (79 shorter events, 1.9 us)
Async XLA Ops:
  1.4 10.1 %copy-start.20 = (s32[1,1024]{1,0:T(1,128)}, s32[1,1024]{1,0:T(1,128)S(1)}, u32[]{:S(2)}) copy-start(s32[1,1024]{1,0:T(1,128)S(1)} %fusion.6) | copy-start | bytes 12292
  1.9 9.7 %copy-start = (bf16[3,256,768]{2,1,0:T(8,128)(2,1)S(1)}, bf16[3,256,768]{2,1,0:T(8,128)(2,1)}, u32[]{:S(2)}) copy-start(bf16[3,256,768]{2,1,0:T(8,128)(2,1)} %refs_0_.1) | copy-start | bytes 3538948
  11.6 1.3 copy-start.1
  79.7 2.2 copy-start.6
  81.9 2.2 copy-start.7
  84.1 1.1 copy-start.11
  85.2 1.0 copy-start.12
  86.2 1.8 copy-start.2
  86.2 2.3 copy-start.9
  124.3 43.2 %copy-start.25 = (bf16[1024,768]{1,0:T(8,128)(2,1)S(1)}, bf16[1024,768]{1,0:T(8,128)(2,1)}, u32[]{:S(2)}) copy-start(bf16[1024,768]{1,0:T(8,128)(2,1)} %get-tuple-element.39.context_ref) | copy-start | bytes 4718596
  170.4 39.6 %copy-start.23 = (f32[8,768]{1,0:T(8,128)S(1)}, f32[8,768]{1,0:T(8,128)}, u32[]{:S(2)}) copy-start(f32[8,768]{1,0:T(8,128)} %get-tuple-element.51) | copy-start | bytes 73732
  210.0 2.7 copy-start.24
  210.0 2.7 copy-start.10
  210.1 5.5 %slice-start = ((s8[4718592]{0:T(1024)(128)(4,1)}), s8[4194304]{0:T(1024)(128)(4,1)S(1)}, s32[]{:S(2)}) async-start(s8[4718592]{0:T(1024)(128)(4,1)} %bitcast.66), calls=%async_computation | async-start | bytes 8388608
  212.7 2.9 slice-start.1
  218.5 3.3 copy-start.3
  223.2 1.4 copy-start.18
  223.2 4.1 slice-start.4
  224.6 2.7 slice-start.5
  224.6 2.7 copy-start.27
  224.6 9.6 %slice-start.2 = ((s8[6291456]{0:T(1024)(128)(4,1)}), s8[2097152]{0:T(1024)(128)(4,1)S(1)}, s32[]{:S(2)}) async-start(s8[6291456]{0:T(1024)(128)(4,1)} %bitcast.76), calls=%async_computation.2 | async-start | bytes 4194304
  227.3 7.0 %slice-start.3 = ((s8[6291456]{0:T(1024)(128)(4,1)}), s8[4194304]{0:T(1024)(128)(4,1)S(1)}, s32[]{:S(2)}) async-start(s8[6291456]{0:T(1024)(128)(4,1)} %bitcast.76), calls=%async_computation.3 | async-start | bytes 8388608
  227.3 7.0 %copy-start.26 = (bf16[1024,768]{1,0:T(8,128)(2,1)S(1)}, bf16[1024,768]{1,0:T(8,128)(2,1)}, u32[]{:S(2)}) copy-start(bf16[1024,768]{1,0:T(8,128)(2,1)} %get-tuple-element.50) | copy-start | bytes 4718596
  241.4 94.6 %copy-start.19 = (f32[9216]{0:T(1024)S(1)}, f32[9216]{0:T(1024)}, u32[]{:S(2)}) copy-start(f32[9216]{0:T(1024)} %param.20) | copy-start | bytes 110596
  241.4 94.6 %copy-start.21 = (f32[9216]{0:T(1024)S(1)}, f32[9216]{0:T(1024)}, u32[]{:S(2)}) copy-start(f32[9216]{0:T(1024)} %param.22) | copy-start | bytes 110596
  241.4 94.6 %copy-start.22 = (f32[9216]{0:T(1024)S(1)}, f32[9216]{0:T(1024)}, u32[]{:S(2)}) copy-start(f32[9216]{0:T(1024)} %param.21) | copy-start | bytes 110596
  334.2 1.2 copy-start.8
  335.4 0.6 copy-start.4
  494.3 4.9 copy-start.16
  499.2 3.3 copy-start.15
  502.5 3.3 copy-start.14
  505.7 3.3 copy-start.13
  509.0 2.8 copy-start.17
  511.8 1.2 copy-start.5

commit v6 on v5

--- a/solution.py
+++ b/solution.py
@@ -95,6 +95,20 @@
     return (lane >= half * HD) & (lane < (half + 1) * HD)
 
 
+def attend_tile(here, keys, values_of, same):
+    done, logs = [], []
+    for half in range(SIDE):
+        mine = jnp.where(head_lanes(half, here.shape), here * HD ** (-0.5), 0.0).astype(jnp.bfloat16)
+        raw = jnp.where(same, dot_dims(keys, mine, 1, 1), NEG)
+        peak = jnp.max(raw, axis=0, keepdims=True)
+        expo = jnp.exp(raw - peak)
+        sums = jnp.sum(expo, axis=0, keepdims=True)
+        mixed = jnp.dot(values_of(half), expo.astype(jnp.bfloat16), preferred_element_type=jnp.float32)
+        done.append(mixed * (1.0 / sums))
+        logs.append(peak + jnp.log(sums))
+    return (low_of(jnp.concatenate(done, axis=0).T), jnp.concatenate(logs, axis=0))
+
+
 def attend_kernel(sizes, tile, table, q_ref, k_ref, v_ref, col_ref, row_ref, ctx_ref, log_ref, vt_ref):
     length = k_ref.shape[0]
     row = pl.program_id(0)
@@ -112,24 +126,12 @@
                 keys = k_ref[pl.ds(begin, size), :]
                 marks = col_ref[pl.ds(begin, size), :]
                 same = jnp.concatenate([marks] * (tile // LANES), axis=1) == row_ref[0, :, rows]
-                here = q_ref[rows, :]
-                done = []
-                for half in range(SIDE):
-                    mine = jnp.where(head_lanes(half, here.shape), here * HD ** (-0.5), 0.0).astype(
-                        jnp.bfloat16
-                    )
-                    raw = jnp.where(same, dot_dims(keys, mine, 1, 1), NEG)
-                    peak = jnp.max(raw, axis=0, keepdims=True)
-                    expo = jnp.exp(raw - peak)
-                    total = jnp.sum(expo, axis=0, keepdims=True)
-                    mixed = jnp.dot(
-                        vt_ref[half * HD : (half + 1) * HD, pl.ds(begin, size)],
-                        expo.astype(jnp.bfloat16),
-                        preferred_element_type=jnp.float32,
-                    )
-                    done.append(mixed * (1.0 / total))
-                    log_ref[0, half : half + 1, rows] = peak + jnp.log(total)
-                ctx_ref[rows, :] = jnp.concatenate(done, axis=0).T.astype(jnp.bfloat16)
+                ctx_ref[rows, :], log_ref[0, :, rows] = attend_tile(
+                    q_ref[rows, :],
+                    keys,
+                    lambda half: vt_ref[half * HD : (half + 1) * HD, pl.ds(begin, size)],
+                    same,
+                )
 
 
 def attend(table, project, marks_col, marks_row, rows, length):
@@ -603,18 +605,16 @@
                         )
                     )
 
-    def start():
-        for number in range(len(moves)):
-            each_move(number, lambda copy: copy.start(), lambda copy: copy.start(), None)
-
-    def finish():
-        for number in range(len(moves)):
-            each_move(
-                number,
-                lambda copy: copy.wait_send(),
-                lambda copy: copy.wait(),
-                lambda copy: copy.wait_recv(),
-            )
+    def start(number):
+        each_move(number, lambda copy: copy.start(), lambda copy: copy.start(), None)
+
+    def finish(number):
+        each_move(
+            number,
+            lambda copy: copy.wait_send(),
+            lambda copy: copy.wait(),
+            lambda copy: copy.wait_recv(),
+        )
 
     return (start, finish)
 
@@ -627,66 +627,159 @@
     greet(peers)
 
 
-def gather_kernel(widths, starts, places, moves, shard_ref, *refs):
+SPAN = 512
+
+
+def front_kernel(
+    widths,
+    starts,
+    shard_ref,
+    inputs_ref,
+    cotangent_ref,
+    bias_ref,
+    col_ref,
+    row_ref,
+    w_qkv,
+    w_out,
+    w_up,
+    w_down,
+    x_out,
+    pull_out,
+    project_ref,
+    context_ref,
+    log_ref,
+    x_buf,
+    w_buf,
+    vt_ref,
+    zeros_ref,
+    send_sem,
+    recv_sem,
+    own_sem,
+    z_send,
+    z_recv,
+    z_own,
+    load_sem,
+):
     count = len(widths)
-    moved_in = refs[: len(moves)]
-    refs = refs[len(moves) :]
-    arrays = 1 + max(number for number, _ in places)
-    outs = refs[:arrays]
-    moved_out = refs[arrays : arrays + len(moves)]
-    send_sem, recv_sem, own_sem, z_send, z_recv, z_own, zeros_ref = refs[arrays + len(moves) :]
+    length = x_buf.shape[0]
+    wide = SIDE * HD
     zeros_ref[...] = jnp.zeros_like(zeros_ref)
     greet_plane(True)
-    start, settle = move_task(moves, moved_in, moved_out, z_send, z_recv, z_own, zeros_ref)
+    move, settle = move_task(
+        ("in", "in"),
+        (inputs_ref, cotangent_ref),
+        (x_out, pull_out),
+        z_send,
+        z_recv,
+        z_own,
+        zeros_ref,
+    )
     begin, go_on, share, finish, sent = gather_tasks(
-        widths, starts, places, shard_ref, outs, send_sem, recv_sem, own_sem
-    )
-    start()
+        widths,
+        starts,
+        [(number, 0) for number in range(count)],
+        shard_ref,
+        [w_qkv, w_out, w_up, w_down],
+        send_sem,
+        recv_sem,
+        own_sem,
+    )
+    move(0)
     for block in range(count):
         begin(block)
-    for step in range(count + 1):
-        if step < count:
-            go_on(step)
-        if step > 0:
-            share(step - 1)
-    for block in range(count):
+    go_on(0)
+    go_on(1)
+    share(0)
+    finish(0)
+    load_w = pltpu.make_async_copy(w_qkv, w_buf, load_sem.at[0])
+    load_w.start()
+    settle(0)
+    move(1)
+    load_x = pltpu.make_async_copy(x_out, x_buf, load_sem.at[1])
+    load_x.start()
+    share(1)
+    load_w.wait()
+    load_x.wait()
+    tasks = {
+        (0, 0): [lambda: go_on(2)],
+        (1, 0): [lambda: share(2)],
+        (1, 2): [lambda: go_on(3)],
+        (2, 1): [lambda: share(3)],
+    }
+    for group in range(D // wide):
+        for part in range(3):
+            columns = slice(part * D + group * wide, part * D + (group + 1) * wide)
+            project_ref[:, columns] = low_of(
+                dot_dims(x_buf[...], w_buf[columns, :], 1, 1) + bias_ref[:, columns]
+            )
+        lanes = slice(group * wide, (group + 1) * wide)
+        values = project_ref[:, 2 * D + group * wide : 2 * D + (group + 1) * wide]
+        vt_ref[...] = low_of(values.astype(jnp.float32).T)
+        for step in range(length // TILE):
+            rows = slice(step * TILE, (step + 1) * TILE)
+            low = max(0, step * TILE - SPAN + 1) // LANES * LANES
+            high = min(length, -(-((step + 1) * TILE + SPAN - 1) // LANES) * LANES)
+            marks = col_ref[low:high, :]
+            same = jnp.concatenate([marks] * (TILE // LANES), axis=1) == row_ref[0, :, rows]
+            context_ref[rows, lanes], log_ref[group, :, rows] = attend_tile(
+                project_ref[rows, lanes],
+                project_ref[low:high, D + group * wide : D + (group + 1) * wide],
+                lambda half: vt_ref[half * HD : (half + 1) * HD, low:high],
+                same,
+            )
+            for task in tasks.get((group, step), []):
+                task()
+    for block in range(1, count):
         finish(block)
     for copy in sent:
         copy.wait_send()
-    settle()
-
-
-def gather_weights(shard, widths, starts, arrays, length):
+    settle(1)
+
+
+def front(shard, inputs, cotangent, bias_qkv, marks_col, marks_row, widths, starts):
     count = len(widths)
-    depth = shard.shape[1]
-    moves = ("in",) * len(arrays)
-    out_shape = [jax.ShapeDtypeStruct((8 * width, depth), shard.dtype) for width in widths]
-    out_shape += [jax.ShapeDtypeStruct((length, depth), shard.dtype) for _ in moves]
+    length = marks_col.shape[0]
+    low = shard.dtype
+    any_spec = pl.BlockSpec(memory_space=pl.ANY)
+    vmem_spec = pl.BlockSpec(memory_space=pltpu.VMEM)
     dma = pltpu.SemaphoreType.DMA
+    rows = jax.ShapeDtypeStruct((length, D), low)
+    wide = SIDE * HD
     return pl.pallas_call(
-        functools.partial(
-            gather_kernel, widths, starts, [(number, 0) for number in range(count)], moves
+        functools.partial(front_kernel, widths, starts),
+        out_shape=tuple(jax.ShapeDtypeStruct((8 * width, D), low) for width in widths)
+        + (
+            rows,
+            rows,
+            jax.ShapeDtypeStruct((length, 3 * D), low),
+            rows,
+            jax.ShapeDtypeStruct((D // wide, SIDE, length), jnp.float32),
         ),
-        out_shape=tuple(out_shape),
-        in_specs=[pl.BlockSpec(memory_space=pltpu.VMEM)] * (1 + len(moves)),
-        out_specs=tuple(pl.BlockSpec(memory_space=pl.ANY) for _ in out_shape),
+        in_specs=[vmem_spec] * 6,
+        out_specs=(any_spec,) * 6 + (vmem_spec,) * 3,
         scratch_shapes=[
+            pltpu.VMEM((length, D), low),
+            pltpu.VMEM((3 * D, D), low),
+            pltpu.VMEM((wide, length), low),
+            pltpu.VMEM((length // 4, D), low),
             dma((count, 9)),
             dma((count, 9)),
             dma((count,)),
-            dma((len(moves), 3)),
-            dma((len(moves), 4)),
-            dma((len(moves), 4)),
-            pltpu.VMEM((length // 4, depth), shard.dtype),
+            dma((2, 3)),
+            dma((2, 4)),
+            dma((2, 4)),
+            dma((2,)),
         ],
         compiler_params=pltpu.CompilerParams(
-            collective_id=1, has_side_effects=True, vmem_limit_bytes=16 * 1024 * 1024
+            collective_id=1, has_side_effects=True, vmem_limit_bytes=56 * 1024 * 1024
         ),
         cost_estimate=pl.CostEstimate(
-            flops=0, bytes_accessed=8 * 16 * shard.shape[0] * depth, transcendentals=0
+            flops=6 * length * D * D + 4 * length * length * D,
+            bytes_accessed=8 * 16 * shard.shape[0] * D,
+            transcendentals=HEADS * length * length,
         ),
-        name="gather_weights",
-    )(shard, *arrays)
+        name="front",
+    )(shard, inputs, cotangent, bias_qkv.reshape(1, 3 * D), marks_col, marks_row)
 
 
 def add_rows(target, target_at, terms, count):
@@ -702,80 +795,221 @@
     lax.fori_loop(0, count // ROWS, step, 0)
 
 
-def reduce_kernel(widths, starts, places, across_planes, *refs):
-    count = len(widths)
-    arrays = 1 + max(place[0] for place in places)
-    blocks = refs[:arrays]
-    refs = refs[arrays:]
-    if across_planes:
-        small_ref, out_ref, small_out = refs[:3]
-        refs = refs[3:]
-    else:
-        out_ref = refs[0]
-        refs = refs[1:]
-    own, given, from_x, from_y, turn_x, turn_y, total = refs[:7]
-    load_sem, sib_send, sib_recv, link_send, link_recv, out_sem = refs[7:13]
-    refs = refs[13:]
-    if across_planes:
-        low_first, high_first, low_second, final, z_send, z_recv = refs[:6]
-        small_all, small_planes, small_sum, small_send, small_recv, wide_send, wide_recv = refs[6:]
+GROUPS = (1, 2, 0)
+PART = 384
+
+
+def group_parts(group, joint):
+    if group == 0:
+        return [(0, joint, 0), (joint, PART, 1)]
+    return [(0, PART, group + 1)]
+
+
+def group_chunks(group, joint):
+    if group == 0:
+        return [(0, step * D) for step in range(3)] + [(1, 0)]
+    return [(0, step * D) for step in range(4)]
+
+
+class Stream:
+    def __init__(self, copies):
+        self.copies, self.next = copies, 0
+        for copy in copies[:2]:
+            copy.start()
+
+    def take(self):
+        self.copies[self.next].wait()
+        self.next += 1
+        return (self.next - 1) % 2
+
+    def free(self):
+        if self.next + 1 < len(self.copies):
+            self.copies[self.next + 1].start()
+
+
+def pieces_of(widths, starts):
+    pieces = []
+    for which in (2, 3, 0, 1):
+        width, start = widths[which], starts[which]
+        size = next(size for size in (192, 96, width) if width % size == 0)
+        pieces += [(size, start + cut, (8 * start + cut, width)) for cut in range(0, width, size)]
+    return [list(part) for part in zip(*pieces)]
+
+
+def reduce_tasks(widths, starts, places, term, buffers, semaphores):
+    given, from_x, from_y, turn_x, turn_y, total = buffers
+    sib_send, sib_recv, link_send, link_recv = semaphores
     me = lax.axis_index("dp")
-    plane = lax.axis_index("seq")
     sib, side_x, side_y, across = partners(me)
     _, sib_x, sib_y, sib_across = partners(sib)
     owners = (me, side_x, side_y, across)
     sib_owners = (sib, sib_x, sib_y, sib_across)
-    if across_planes:
-        others = [(me + step) % 8 for step in range(1, 8)]
-        planes = [(plane + step) % 4 for step in range(1, 4)]
-        greet([("dp", place) for place in others] + [("seq", place) for place in planes])
-    else:
-        greet([("dp", sib), ("dp", side_x), ("dp", side_y)])
-    order = (3, 1, 2, 0)
-    loads, sends = {}, []
-
-    def block_rows(block, owner):
-        number, first, stride = places[block]
-        begin = pl.multiple_of(first + owner * stride, 16)
-        return blocks[number].at[pl.ds(begin, widths[block])]
-
-    for block in range(count):
-        width = widths[block]
-        here = pl.ds(starts[block], width)
-        for which in order:
+    sends, kept = [], {}
+
+    def place_of(piece, owner):
+        first, stride = places[piece]
+        return pl.multiple_of(first + owner * stride, 16)
+
+    def begin(piece):
+        size = widths[piece]
+        for which in (3, 1, 2, 0):
             copy = send(
-                block_rows(block, sib_owners[which]),
-                given.at[which, here],
-                sib_send.at[block, which],
-                sib_recv.at[block, which],
+                term.at[pl.ds(place_of(piece, sib_owners[which]), size)],
+                given.at[which, pl.ds(starts[piece], size)],
+                sib_send.at[piece, which],
+                sib_recv.at[piece, which],
                 "dp",
                 sib,
             )
             copy.start()
             sends.append(copy)
-            load = pltpu.make_async_copy(
-                block_rows(block, owners[which]),
-                own.at[which, here],
-                load_sem.at[block, which],
-            )
-            load.start()
-            loads[block, which] = (load, copy)
-    if across_planes:
-        small_all[me] = small_ref[...]
-        for number, place in enumerate(others):
-            copy = send(
-                small_ref, small_all.at[me], small_send.at[number], small_recv.at[me], "dp", place
-            )
-            copy.start()
-            sends.append(copy)
-
-    def link(block, slot, source, target, place):
-        copy = send(source, target, link_send.at[block, slot], link_recv.at[block, slot], "dp", place)
+            kept[piece, which] = copy
+
+    def link(piece, slot, source, target, place):
+        copy = send(source, target, link_send.at[piece, slot], link_recv.at[piece, slot], "dp", place)
         copy.start()
         sends.append(copy)
 
-    def landed(block, slot, region):
-        send(region, region, link_send.at[block, slot], link_recv.at[block, slot], "dp", sib).wait_recv()
+    def landed(piece, slot, region):
+        send(region, region, link_send.at[piece, slot], link_recv.at[piece, slot], "dp", sib).wait_recv()
+
+    def own_half(piece, which, part):
+        half = widths[piece] // 2
+        return pl.multiple_of(place_of(piece, owners[which]) + part * half, 16)
+
+    def own_rows(piece, which, part):
+        return term.at[pl.ds(own_half(piece, which, part), widths[piece] // 2)]
+
+    def share_rows(ref, piece, part):
+        half = widths[piece] // 2
+        return ref.at[pl.ds(starts[piece] + part * half, half)]
+
+    def turn_rows(ref, piece):
+        return ref.at[pl.ds(starts[piece] // 2, widths[piece] // 2)]
+
+    def pair_sum(piece, which):
+        kept[piece, which].wait_recv()
+        here = place_of(piece, owners[which])
+        add_rows(term, here, [(term, here), (given.at[which], starts[piece])], widths[piece])
+
+    def first_stage(piece):
+        pair_sum(piece, 3)
+        link(piece, 0, own_rows(piece, 3, 0), turn_rows(turn_x, piece), side_x)
+        link(piece, 1, own_rows(piece, 3, 1), turn_rows(turn_y, piece), side_y)
+        pair_sum(piece, 1)
+        link(piece, 2, own_rows(piece, 1, 0), share_rows(from_x, piece, 0), side_x)
+        pair_sum(piece, 2)
+        link(piece, 3, own_rows(piece, 2, 1), share_rows(from_y, piece, 1), side_y)
+        pair_sum(piece, 0)
+
+    def second_stage(piece):
+        half = widths[piece] // 2
+        landed(piece, 0, turn_rows(turn_x, piece))
+        here = own_half(piece, 2, 0)
+        add_rows(term, here, [(term, here), (turn_x, starts[piece] // 2)], half)
+        link(piece, 4, own_rows(piece, 2, 0), share_rows(from_y, piece, 0), side_y)
+        landed(piece, 1, turn_rows(turn_y, piece))
+        here = own_half(piece, 1, 1)
+        add_rows(term, here, [(term, here), (turn_y, starts[piece] // 2)], half)
+        link(piece, 5, own_rows(piece, 1, 1), share_rows(from_x, piece, 1), side_x)
+
+    def third_stage(piece):
+        landed(piece, 2, share_rows(from_x, piece, 0))
+        landed(piece, 5, share_rows(from_x, piece, 1))
+        landed(piece, 3, share_rows(from_y, piece, 1))
+        landed(piece, 4, share_rows(from_y, piece, 0))
+        here = starts[piece]
+        add_rows(
+            total,
+            here,
+            [(term, place_of(piece, me)), (from_x, here), (from_y, here)],
+            widths[piece],
+        )
+
+    return (begin, first_stage, second_stage, third_stage, sends)
+
+
+def reduce_kernel(
+    widths,
+    starts,
+    places,
+    d_up_ref,
+    active_ref,
+    d_qkv_ref,
+    d_att_ref,
+    first_low_ref,
+    d_down_ref,
+    x_ref,
+    context_ref,
+    small_ref,
+    out_ref,
+    small_out,
+    term,
+    given,
+    from_x,
+    from_y,
+    turn_x,
+    turn_y,
+    total,
+    left_buf,
+    sib_send,
+    sib_recv,
+    link_send,
+    link_recv,
+    left_sem,
+    out_sem,
+    low_first,
+    high_first,
+    low_second,
+    final,
+    z_send,
+    z_recv,
+    small_all,
+    small_planes,
+    small_sum,
+    small_send,
+    small_recv,
+    wide_send,
+    wide_recv,
+):
+    count = len(widths)
+    me = lax.axis_index("dp")
+    sib = partners(me)[0]
+    plane = lax.axis_index("seq")
+    left_loads, right_refs = [], []
+    for group in GROUPS:
+        for number in range(4):
+            columns = pl.ds(D * number, D)
+            if group == 1:
+                left, right = d_up_ref.at[:, columns], first_low_ref
+            elif group == 2:
+                left, right = active_ref.at[:, columns], d_down_ref
+            elif number < 3:
+                left, right = d_qkv_ref.at[number], x_ref
+            else:
+                left, right = d_att_ref, context_ref
+            slot = len(left_loads) % 2
+            left_loads.append(pltpu.make_async_copy(left, left_buf.at[slot], left_sem.at[slot]))
+            right_refs.append(right)
+    lefts = Stream(left_loads)
+    others = [(me + step) % 8 for step in range(1, 8)]
+    planes = [(plane + step) % 4 for step in range(1, 4)]
+    greet([("dp", place) for place in others] + [("seq", place) for place in planes])
+    begin, first_stage, second_stage, third_stage, sends = reduce_tasks(
+        widths,
+        starts,
+        places,
+        term,
+        (given, from_x, from_y, turn_x, turn_y, total),
+        (sib_send, sib_recv, link_send, link_recv),
+    )
+    small_all[me] = small_ref[...]
+    for number, place in enumerate(others):
+        copy = send(
+            small_ref, small_all.at[me], small_send.at[number], small_recv.at[me], "dp", place
+        )
+        copy.start()
+        sends.append(copy)
 
     def upper(block):
         return (starts[block], widths[block] // 2)
@@ -789,154 +1023,107 @@
     def half_of(block):
         return pl.ds(starts[block] // 2, widths[block] // 2)
 
-    def pair_sum(block, which):
-        load, copy = loads[block, which]
-        load.wait()
-        copy.wait_recv()
-        add_rows(
-            own.at[which],
-            starts[block],
-            [(own.at[which], starts[block]), (given.at[which], starts[block])],
-            widths[block],
-        )
-
-    def first_stage(block):
-        pair_sum(block, 3)
-        link(block, 0, own.at[3, rows_of(upper(block))], turn_x.at[half_of(block)], side_x)
-        link(block, 1, own.at[3, rows_of(lower(block))], turn_y.at[half_of(block)], side_y)
-        pair_sum(block, 1)
-        link(
-            block, 2, own.at[1, rows_of(upper(block))], from_x.at[rows_of(upper(block))], side_x
-        )
-        pair_sum(block, 2)
-        link(
-            block, 3, own.at[2, rows_of(lower(block))], from_y.at[rows_of(lower(block))], side_y
-        )
-        pair_sum(block, 0)
-
-    def second_stage(block):
-        landed(block, 0, turn_x.at[half_of(block)])
-        begin, size = upper(block)
-        add_rows(own.at[2], begin, [(own.at[2], begin), (turn_x, starts[block] // 2)], size)
-        link(block, 4, own.at[2, rows_of(upper(block))], from_y.at[rows_of(upper(block))], side_y)
-        landed(block, 1, turn_y.at[half_of(block)])
-        begin, size = lower(block)
-        add_rows(own.at[1], begin, [(own.at[1], begin), (turn_y, starts[block] // 2)], size)
-        link(block, 5, own.at[1, rows_of(lower(block))], from_x.at[rows_of(lower(block))], side_x)
-
-    def third_stage(block):
-        landed(block, 2, from_x.at[rows_of(upper(block))])
-        landed(block, 5, from_x.at[rows_of(lower(block))])
-        landed(block, 3, from_y.at[rows_of(lower(block))])
-        landed(block, 4, from_y.at[rows_of(upper(block))])
-        begin = starts[block]
-        add_rows(total, begin, [(own.at[0], begin), (from_x, begin), (from_y, begin)], widths[block])
-
     stages = [first_stage, second_stage, third_stage]
-    results = total
-    if across_planes:
-        results = final
-
-        def z_copy(block, slot, source, target, place):
-            return send(source, target, z_send.at[block, slot], z_recv.at[block, slot], "seq", place)
-
-        def z_put(block, slot, source, target, place):
-            copy = z_copy(block, slot, source, target, place)
-            copy.start()
-            return copy
-
-        def z_landed(block, slot, region):
-            z_copy(block, slot, region, region, (plane + 1) % 4).wait_recv()
-
-        def fourth_stage(block):
-            up, down, half = rows_of(upper(block)), rows_of(lower(block)), half_of(block)
-
-            @pl.when(plane == 0)
-            def _():
-                z_put(block, 0, total.at[up], low_first.at[half], 1)
-                z_put(block, 1, total.at[down], low_second.at[half], 1)
-
-            @pl.when(plane == 2)
-            def _():
-                z_put(block, 2, total.at[up], high_first.at[half], 1)
-
-        def fifth_stage(block):
-            up, down, half = rows_of(upper(block)), rows_of(lower(block)), half_of(block)
-            middle = starts[block] // 2
-
-            @pl.when(plane == 1)
-            def _():
-                z_landed(block, 0, low_first.at[half])
-                z_landed(block, 2, high_first.at[half])
-                begin, size = upper(block)
-                add_rows(
-                    final, begin, [(total, begin), (low_first, middle), (high_first, middle)], size
-                )
-                z_put(block, 3, final.at[up], final.at[up], 0)
-                z_put(block, 4, final.at[up], final.at[up], 2)
-                z_landed(block, 1, low_second.at[half])
-                begin, size = lower(block)
-                add_rows(total, begin, [(total, begin), (low_second, middle)], size)
-                z_put(block, 5, total.at[down], low_second.at[half], 2)
-
-        def sixth_stage(block):
-            up, down, half = rows_of(upper(block)), rows_of(lower(block)), half_of(block)
-            middle = starts[block] // 2
-
-            @pl.when(plane == 2)
-            def _():
-                z_landed(block, 5, low_second.at[half])
-                begin, size = lower(block)
-                add_rows(final, begin, [(total, begin), (low_second, middle)], size)
-                z_put(block, 6, final.at[down], final.at[down], 1)
-                z_put(block, 7, final.at[down], final.at[down], 3)
-                z_landed(block, 4, final.at[up])
-                z_put(block, 8, final.at[up], final.at[up], 3)
-
-        def seventh_stage(block):
-            down = rows_of(lower(block))
-
-            @pl.when(plane == 1)
-            def _():
-                z_landed(block, 6, final.at[down])
-                z_put(block, 9, final.at[down], final.at[down], 0)
-
-        def eighth_stage(block):
-            up, down, half = rows_of(upper(block)), rows_of(lower(block)), half_of(block)
-
-            @pl.when(plane == 0)
-            def _():
-                z_landed(block, 3, final.at[up])
-                z_landed(block, 9, final.at[down])
-                z_copy(block, 0, total.at[up], low_first.at[half], 1).wait_send()
-                z_copy(block, 1, total.at[down], low_second.at[half], 1).wait_send()
-
-            @pl.when(plane == 1)
-            def _():
-                z_copy(block, 3, final.at[up], final.at[up], 0).wait_send()
-                z_copy(block, 4, final.at[up], final.at[up], 2).wait_send()
-                z_copy(block, 5, total.at[down], low_second.at[half], 2).wait_send()
-                z_copy(block, 9, final.at[down], final.at[down], 0).wait_send()
-
-            @pl.when(plane == 2)
-            def _():
-                z_copy(block, 2, total.at[up], high_first.at[half], 1).wait_send()
-                z_copy(block, 6, final.at[down], final.at[down], 1).wait_send()
-                z_copy(block, 7, final.at[down], final.at[down], 3).wait_send()
-                z_copy(block, 8, final.at[up], final.at[up], 3).wait_send()
-
-            @pl.when(plane == 3)
-            def _():
-                z_landed(block, 7, final.at[down])
-                z_landed(block, 8, final.at[up])
-
-        stages += [fourth_stage, fifth_stage, sixth_stage, seventh_stage, eighth_stage]
+    def z_copy(block, slot, source, target, place):
+        return send(source, target, z_send.at[block, slot], z_recv.at[block, slot], "seq", place)
+
+    def z_put(block, slot, source, target, place):
+        copy = z_copy(block, slot, source, target, place)
+        copy.start()
+        return copy
+
+    def z_landed(block, slot, region):
+        z_copy(block, slot, region, region, (plane + 1) % 4).wait_recv()
+
+    def fourth_stage(block):
+        up, down, half = rows_of(upper(block)), rows_of(lower(block)), half_of(block)
+
+        @pl.when(plane == 0)
+        def _():
+            z_put(block, 0, total.at[up], low_first.at[half], 1)
+            z_put(block, 1, total.at[down], low_second.at[half], 1)
+
+        @pl.when(plane == 2)
+        def _():
+            z_put(block, 2, total.at[up], high_first.at[half], 1)
+
+    def fifth_stage(block):
+        up, down, half = rows_of(upper(block)), rows_of(lower(block)), half_of(block)
+        middle = starts[block] // 2
+
+        @pl.when(plane == 1)
+        def _():
+            z_landed(block, 0, low_first.at[half])
+            z_landed(block, 2, high_first.at[half])
+            begin, size = upper(block)
+            add_rows(
+                final, begin, [(total, begin), (low_first, middle), (high_first, middle)], size
+            )
+            z_put(block, 3, final.at[up], final.at[up], 0)
+            z_put(block, 4, final.at[up], final.at[up], 2)
+            z_landed(block, 1, low_second.at[half])
+            begin, size = lower(block)
+            add_rows(total, begin, [(total, begin), (low_second, middle)], size)
+            z_put(block, 5, total.at[down], low_second.at[half], 2)
+
+    def sixth_stage(block):
+        up, down, half = rows_of(upper(block)), rows_of(lower(block)), half_of(block)
+        middle = starts[block] // 2
+
+        @pl.when(plane == 2)
+        def _():
+            z_landed(block, 5, low_second.at[half])
+            begin, size = lower(block)
+            add_rows(final, begin, [(total, begin), (low_second, middle)], size)
+            z_put(block, 6, final.at[down], final.at[down], 1)
+            z_put(block, 7, final.at[down], final.at[down], 3)
+            z_landed(block, 4, final.at[up])
+            z_put(block, 8, final.at[up], final.at[up], 3)
+
+    def seventh_stage(block):
+        down = rows_of(lower(block))
+
+        @pl.when(plane == 1)
+        def _():
+            z_landed(block, 6, final.at[down])
+            z_put(block, 9, final.at[down], final.at[down], 0)
+
+    def eighth_stage(block):
+        up, down, half = rows_of(upper(block)), rows_of(lower(block)), half_of(block)
+
+        @pl.when(plane == 0)
+        def _():
+            z_landed(block, 3, final.at[up])
+            z_landed(block, 9, final.at[down])
+            z_copy(block, 0, total.at[up], low_first.at[half], 1).wait_send()
+            z_copy(block, 1, total.at[down], low_second.at[half], 1).wait_send()
+
+        @pl.when(plane == 1)
+        def _():
+            z_copy(block, 3, final.at[up], final.at[up], 0).wait_send()
+            z_copy(block, 4, final.at[up], final.at[up], 2).wait_send()
+            z_copy(block, 5, total.at[down], low_second.at[half], 2).wait_send()
+            z_copy(block, 9, final.at[down], final.at[down], 0).wait_send()
+
+        @pl.when(plane == 2)
+        def _():
+            z_copy(block, 2, total.at[up], high_first.at[half], 1).wait_send()
+            z_copy(block, 6, final.at[down], final.at[down], 1).wait_send()
+            z_copy(block, 7, final.at[down], final.at[down], 3).wait_send()
+            z_copy(block, 8, final.at[up], final.at[up], 3).wait_send()
+
+        @pl.when(plane == 3)
+        def _():
+            z_landed(block, 7, final.at[down])
+            z_landed(block, 8, final.at[up])
+
+    stages += [fourth_stage, fifth_stage, sixth_stage, seventh_stage, eighth_stage]
 
     outgoing = []
 
     def last_stage(block):
         here = pl.ds(starts[block], widths[block])
-        copy = pltpu.make_async_copy(results.at[here], out_ref.at[here], out_sem.at[block])
+        copy = pltpu.make_async_copy(final.at[here], out_ref.at[here], out_sem.at[block])
         copy.start()
         outgoing.append(copy)
 
@@ -966,64 +1153,82 @@
             ).wait_recv()
         small_out[...] = (small_planes[0] + small_planes[1]) + (small_planes[2] + small_planes[3])
 
+    done = [0] * count
+
+    def advance(piece, upto):
+        while done[piece] < upto:
+            stages[done[piece]](piece)
+            done[piece] += 1
+
+    between = {
+        (1, 0): [(0, 1)],
+        (1, 1): [(1, 1)],
+        (1, 2): [(0, 2)],
+        (1, 3): [(1, 2)],
+        (2, 0): [(2, 1), (0, 4)],
+        (2, 1): [(3, 1), (1, 4)],
+        (2, 2): [(2, 2), (0, 5)],
+        (2, 3): [(3, 2), (1, 5)],
+    }
+    ready = ((0, 1), (2, 3), (4, 5, 6, 7))
+    for turn, group in enumerate(GROUPS):
+        for number in range(4):
+            right = right_refs[4 * turn + number]
+            slot = lefts.take()
+            begin_row = FF * group + D * number
+            term[begin_row : begin_row + D, :] = low_of(dot_dims(left_buf[slot], right[...], 0, 0))
+            lefts.free()
+            for piece, upto in between.get((turn, number), []):
+                advance(piece, upto)
+        for piece in ready[turn]:
+            begin(piece)
+    small_first()
     for tick in range(count + len(stages) - 1):
         for number in range(len(stages) - 1, -1, -1):
-            block = tick - number
-            if 0 <= block < count:
-                stages[number](block)
-        if across_planes and tick == 1:
-            small_first()
-    if across_planes:
-        small_second()
+            piece = tick - number
+            if 0 <= piece < count and done[piece] <= number:
+                advance(piece, number + 1)
+    small_second()
     for copy in sends:
         copy.wait_send()
     for copy in outgoing:
         copy.wait()
 
 
-def pieces_of(widths, starts, joined):
-    pieces = []
-    for which in (2, 3, 0, 1):
-        width, start = widths[which], starts[which]
-        number, first = (0, 8 * start) if joined else (which, 0)
-        size = next(size for size in (192, 96, width) if width % size == 0)
-        pieces += [(size, start + cut, (number, first + cut, width)) for cut in range(0, width, size)]
-    return [list(part) for part in zip(*pieces)]
-
-
-def plane_reduce(terms, widths, starts, small=None):
+def reduce_all(lefts, rights, small, widths, starts):
+    widths, starts, places = pieces_of(widths, starts)
+    count = len(widths)
     share = sum(widths)
-    depth = terms[0].shape[1]
-    across_planes = small is not None
-    widths, starts, places = pieces_of(widths, starts, len(terms) == 1)
-    count = len(widths)
-    low = terms[0].dtype
+    tokens, depth = rights[0].shape
+    low = rights[0].dtype
     whole = pltpu.VMEM((share, depth), low)
     half = pltpu.VMEM((share // 2, depth), low)
     dma = pltpu.SemaphoreType.DMA
-    scratch = [
-        pltpu.VMEM((4, share, depth), low),
-        pltpu.VMEM((4, share, depth), low),
-        whole,
-        whole,
-        half,
-        half,
-        whole,
-        dma((count, 4)),
-        dma((count, 4)),
-        dma((count, 4)),
-        dma((count, 6)),
-        dma((count, 6)),
-        dma((count,)),
-    ]
     any_spec = pl.BlockSpec(memory_space=pl.ANY)
     vmem_spec = pl.BlockSpec(memory_space=pltpu.VMEM)
-    out_shape = [jax.ShapeDtypeStruct((share, depth), low)]
-    in_specs = [any_spec] * len(terms)
-    out_specs = [any_spec]
-    operands = list(terms)
-    if across_planes:
-        scratch += [
+    return pl.pallas_call(
+        functools.partial(reduce_kernel, widths, starts, places),
+        out_shape=(
+            jax.ShapeDtypeStruct((share, depth), low),
+            jax.ShapeDtypeStruct(small.shape, small.dtype),
+        ),
+        in_specs=[any_spec] * 4 + [vmem_spec] * 5,
+        out_specs=(any_spec, vmem_spec),
+        scratch_shapes=[
+            pltpu.VMEM((8 * share, depth), low),
+            pltpu.VMEM((4, share, depth), low),
+            whole,
+            whole,
+            half,
+            half,
+            whole,
+            pltpu.VMEM((2, tokens, depth), low),
+            dma((count, 4)),
+            dma((count, 4)),
+            dma((count, 6)),
+            dma((count, 6)),
+            dma((2,)),
+            dma((count,)),
             half,
             half,
             half,
@@ -1037,59 +1242,15 @@
             dma((8,)),
             dma((3,)),
             dma((4,)),
-        ]
-        operands.append(small)
-        in_specs.append(vmem_spec)
-        out_specs.append(vmem_spec)
-        out_shape.append(jax.ShapeDtypeStruct(small.shape, small.dtype))
-    return pl.pallas_call(
-        functools.partial(reduce_kernel, widths, starts, places, across_planes),
-        out_shape=tuple(out_shape),
-        in_specs=in_specs,
-        out_specs=tuple(out_specs),
-        scratch_shapes=scratch,
+        ],
         compiler_params=pltpu.CompilerParams(
-            collective_id=2 if across_planes else 3,
-            has_side_effects=True,
-            vmem_limit_bytes=48 * 1024 * 1024,
+            collective_id=2, has_side_effects=True, vmem_limit_bytes=60 * 1024 * 1024
         ),
         cost_estimate=pl.CostEstimate(
-            flops=0, bytes_accessed=8 * 20 * share * depth, transcendentals=0
+            flops=2 * tokens * 8 * share * depth, bytes_accessed=8 * 20 * share * depth, transcendentals=0
         ),
-        name="reduce_all" if across_planes else "plane_reduce",
-    )(*operands)
-
-
-GROUPS = (1, 2, 0)
-PART = 384
-
-
-def group_parts(group, joint):
-    if group == 0:
-        return [(0, joint, 0), (joint, PART, 1)]
-    return [(0, PART, group + 1)]
-
-
-def group_chunks(group, joint):
-    if group == 0:
-        return [(0, step * D) for step in range(3)] + [(1, 0)]
-    return [(0, step * D) for step in range(4)]
-
-
-class Stream:
-    def __init__(self, copies):
-        self.copies, self.next = copies, 0
-        for copy in copies[:2]:
-            copy.start()
-
-    def take(self):
-        self.copies[self.next].wait()
-        self.next += 1
-        return (self.next - 1) % 2
-
-    def free(self):
-        if self.next + 1 < len(self.copies):
-            self.copies[self.next + 1].start()
+        name="reduce_all",
+    )(*lefts, *rights, small)
 
 
 def optimize_kernel(
@@ -1143,12 +1304,7 @@
     every_sem,
 ):
     joint = block_widths[0]
-    me = lax.axis_index("dp")
-    sib, side_x, side_y, across = partners(me)
-    _, sib_x, sib_y, sib_across = partners(sib)
-    owners = (me, side_x, side_y, across)
-    sib_owners = (sib, sib_x, sib_y, sib_across)
-    widths, starts, places = pieces_of(block_widths, block_starts, True)
+    widths, starts, places = pieces_of(block_widths, block_starts)
 
     right_loads, basis_loads = [], []
     for group in GROUPS + GROUPS:
@@ -1187,7 +1343,7 @@
         copy.start()
         outgoing[number, turn] = copy
 
-    moment_loads, outgoing, sends, kept = {}, {}, [], {}
+    moment_loads, outgoing = {}, {}
     greet_plane(True)
     move_start, move_finish = move_task(
         ("out", "out"),
@@ -1199,7 +1355,8 @@
         None,
     )
     rights, bases = Stream(right_loads), Stream(basis_loads)
-    move_start()
+    for number in range(2):
+        move_start(number)
     for turn in range(2):
         load_moments(turn)
 
@@ -1236,85 +1393,14 @@
             for task in between[number]:
                 task()
 
-    def place_of(piece, owner):
-        _, first, stride = places[piece]
-        return pl.multiple_of(first + owner * stride, 16)
-
-    def begin(piece):
-        size = widths[piece]
-        for which in (3, 1, 2, 0):
-            copy = send(
-                term.at[pl.ds(place_of(piece, sib_owners[which]), size)],
-                given.at[which, pl.ds(starts[piece], size)],
-                sib_send.at[piece, which],
-                sib_recv.at[piece, which],
-                "dp",
-                sib,
-            )
-            copy.start()
-            sends.append(copy)
-            kept[piece, which] = copy
-
-    def link(piece, slot, source, target, place):
-        copy = send(source, target, link_send.at[piece, slot], link_recv.at[piece, slot], "dp", place)
-        copy.start()
-        sends.append(copy)
-
-    def landed(piece, slot, region):
-        send(region, region, link_send.at[piece, slot], link_recv.at[piece, slot], "dp", sib).wait_recv()
-
-    def own_half(piece, which, part):
-        half = widths[piece] // 2
-        return pl.multiple_of(place_of(piece, owners[which]) + part * half, 16)
-
-    def own_rows(piece, which, part):
-        return term.at[pl.ds(own_half(piece, which, part), widths[piece] // 2)]
-
-    def share_rows(ref, piece, part):
-        half = widths[piece] // 2
-        return ref.at[pl.ds(starts[piece] + part * half, half)]
-
-    def turn_rows(ref, piece):
-        return ref.at[pl.ds(starts[piece] // 2, widths[piece] // 2)]
-
-    def pair_sum(piece, which):
-        kept[piece, which].wait_recv()
-        here = place_of(piece, owners[which])
-        add_rows(term, here, [(term, here), (given.at[which], starts[piece])], widths[piece])
-
-    def first_stage(piece):
-        pair_sum(piece, 3)
-        link(piece, 0, own_rows(piece, 3, 0), turn_rows(turn_x, piece), side_x)
-        link(piece, 1, own_rows(piece, 3, 1), turn_rows(turn_y, piece), side_y)
-        pair_sum(piece, 1)
-        link(piece, 2, own_rows(piece, 1, 0), share_rows(from_x, piece, 0), side_x)
-        pair_sum(piece, 2)
-        link(piece, 3, own_rows(piece, 2, 1), share_rows(from_y, piece, 1), side_y)
-        pair_sum(piece, 0)
-
-    def second_stage(piece):
-        half = widths[piece] // 2
-        landed(piece, 0, turn_rows(turn_x, piece))
-        here = own_half(piece, 2, 0)
-        add_rows(term, here, [(term, here), (turn_x, starts[piece] // 2)], half)
-        link(piece, 4, own_rows(piece, 2, 0), share_rows(from_y, piece, 0), side_y)
-        landed(piece, 1, turn_rows(turn_y, piece))
-        here = own_half(piece, 1, 1)
-        add_rows(term, here, [(term, here), (turn_y, starts[piece] // 2)], half)
-        link(piece, 5, own_rows(piece, 1, 1), share_rows(from_x, piece, 1), side_x)
-
-    def third_stage(piece):
-        landed(piece, 2, share_rows(from_x, piece, 0))
-        landed(piece, 5, share_rows(from_x, piece, 1))
-        landed(piece, 3, share_rows(from_y, piece, 1))
-        landed(piece, 4, share_rows(from_y, piece, 0))
-        here = starts[piece]
-        add_rows(
-            total,
-            here,
-            [(term, place_of(piece, me)), (from_x, here), (from_y, here)],
-            widths[piece],
-        )
+    begin, first_stage, second_stage, third_stage, sends = reduce_tasks(
+        widths,
+        starts,
+        places,
+        term,
+        (given, from_x, from_y, turn_x, turn_y, total),
+        (sib_send, sib_recv, link_send, link_recv),
+    )
 
 
     def adam_group(turn):
@@ -1453,7 +1539,8 @@
         copy.wait_send()
     for number, turn in ((1, 1), (1, 2), (2, 1), (2, 2), (3, 1), (3, 2), (4, 1), (4, 2)):
         outgoing[number, turn].wait()
-    move_finish()
+    for number in range(2):
+        move_finish(number)
 
 
 def optimize(
@@ -1462,7 +1549,7 @@
     share = grad.shape[0]
     length = output.shape[0]
     low = grad.dtype
-    pieces = len(pieces_of(widths, starts, True)[0])
+    pieces = len(pieces_of(widths, starts)[0])
     any_spec = pl.BlockSpec(memory_space=pl.ANY)
     vmem_spec = pl.BlockSpec(memory_space=pltpu.VMEM)
     wide = jax.ShapeDtypeStruct((D, share), jnp.float32)
@@ -1568,9 +1655,21 @@
 
     on_plane = owners == 8 and groups == 4 and number == 3
     shard = weights.astype(jnp.bfloat16).T
+    bias_query, bias_value = small[4 * D : 5 * D], small[5 * D : 6 * D]
+    filler = jnp.broadcast_to(
+        (jnp.arange(length, dtype=jnp.int32) // TILE)[None], (padded - number, length)
+    )
+    marks = lax.dynamic_slice_in_dim(
+        jnp.concatenate([segments, filler], axis=0), place * rows, rows, axis=0
+    )
+    table = key_windows(marks)
+    marks_col = jnp.broadcast_to(marks.reshape(tokens, 1), (tokens, LANES))
+    marks_row = marks.reshape(rows, 1, length)
+
+    bias_qkv = jnp.concatenate([bias_query, jnp.zeros_like(bias_query), bias_value])
     if on_plane:
-        w_qkv, w_out, w_up, w_down, x, pull = gather_weights(
-            shard, block_widths, block_starts, (inputs, cotangent), length
+        w_qkv, w_out, w_up, w_down, x, pull, project, context, log_sum = front(
+            shard, inputs, cotangent, bias_qkv, marks_col, marks_row, block_widths, block_starts
         )
     else:
         x = to_rows(inputs)
@@ -1578,32 +1677,14 @@
         w_qkv, w_out, w_up, w_down = [
             lax.all_gather(block, "dp", axis=0, tiled=True) for block in blocks_of(shard)
         ]
-    bias_query, bias_value = small[4 * D : 5 * D], small[5 * D : 6 * D]
-    filler = jnp.broadcast_to(
-        (jnp.arange(length, dtype=jnp.int32) // TILE)[None], (padded - number, length)
-    )
-    marks = lax.dynamic_slice_in_dim(
-        jnp.concatenate([segments, filler], axis=0), place * rows, rows, axis=0
-    )
-    table = key_windows(marks)
-    marks_col = jnp.broadcast_to(marks.reshape(tokens, 1), (tokens, LANES))
-    marks_row = marks.reshape(rows, 1, length)
-
-    bias_qkv = jnp.concatenate([bias_query, jnp.zeros_like(bias_query), bias_value])
-    project = (dot_dims(x, w_qkv, 1, 1) + bias_qkv).astype(jnp.bfloat16)
-    context, log_sum = attend(table, project, marks_col, marks_row, rows, length)
+        project = low_of(dot_dims(x, w_qkv, 1, 1) + bias_qkv)
+        context, log_sum = attend(table, project, marks_col, marks_row, rows, length)
     output, first_low, active, d_down, d_up, d_att, d_context, sums, up_sums = layer(
         context, x, pull, w_out, w_up, w_down, small
     )
-    grad_down = low_of(dot_dims(active, d_down, 0, 0))
-    grad_up = low_of(dot_dims(d_up, first_low, 0, 0))
-    grad_outw = low_of(dot_dims(d_att, context, 0, 0))
     d_qkv = attend_back(table, project, d_context, marks_col, marks_row, log_sum, rows, length)
     grad_bias_query = jnp.sum(d_qkv[0].astype(jnp.float32), axis=0)
     grad_bias_value = jnp.sum(d_qkv[2].astype(jnp.float32), axis=0)
-    grad_qkv = jnp.concatenate([dot_dims(d_qkv[part], x, 0, 0) for part in range(3)], axis=0).astype(
-        jnp.bfloat16
-    )
     input_grad = d_att.astype(jnp.float32)
     for part in range(3):
         input_grad = input_grad + dot_dims(d_qkv[part], w_qkv[part * D : (part + 1) * D], 1, 0)
@@ -1618,10 +1699,13 @@
             up_sums.reshape(-1),
         ]
     )
-    grads = [grad_qkv, grad_outw, grad_up, grad_down]
     if on_plane:
-        mine, small_grad = plane_reduce(
-            grads, block_widths, block_starts, small_local.reshape(-1, LANES)
+        mine, small_grad = reduce_all(
+            (d_up, active, d_qkv, d_att),
+            (first_low, d_down, x, context),
+            small_local.reshape(-1, LANES),
+            block_widths,
+            block_starts,
         )
         small_grad = small_grad.reshape(-1)
         reduced, first_new, second_new, weights_new, weights_low, _, output, input_grad = optimize(
@@ -1637,6 +1721,16 @@
             block_starts,
         )
     else:
+        grads = [dot_dims(d_qkv[part], x, 0, 0) for part in range(3)]
+        grads = [
+            low_of(grad)
+            for grad in (
+                jnp.concatenate(grads, axis=0),
+                dot_dims(d_att, context, 0, 0),
+                dot_dims(d_up, first_low, 0, 0),
+                dot_dims(active, d_down, 0, 0),
+            )
+        ]
         output = to_quarters(output)
         input_grad = to_quarters(input_grad)
         scatter = lambda array: lax.psum_scatter(array, "dp", scatter_dimension=0, tiled=True)

time: 522 us -> 493 us (0.944)
  matrix products: 33.6 us -> 6.88 us
  Pallas kernels: 430 us -> 443 us
  local copies, waits for them, and re-layouts: 42.4 us -> 29.5 us
    dot_general x10 -> x3, matrix products: 33.6 us -> 6.88 us  [dot_dims(): lax.dot_general(left, right, (((left_dim,), (right_dim,)), ((), ())), pre...]
    pallas_call x3 -> x2, Pallas kernels: 190 us -> 205 us  [the longest x1 106 us: front(): pl.pallas_call(functools.partial(front_kernel, widths, starts), out_shape...]
    unnamed x81 -> x45, local copies, waits for them, and re-layouts: 35.6 us -> 24.3 us
where the time goes in v6:
time: 493 us; the launch traced here: 484 us
  Pallas kernels  443 us (90%)
  local copies, waits for them, and re-layouts  29.5 us (6%)
  matrix products  6.88 us (1%)
    pallas_call x1, Pallas kernels, optimize(): pl.pallas_call(functools.partial(optimize_kernel, widths, starts), out_sh...  156 us
    pallas_call x1, Pallas kernels, front(): pl.pallas_call(functools.partial(front_kernel, widths, starts), out_shape...  106 us
    pallas_call x1, Pallas kernels, reduce_all(): pl.pallas_call(functools.partial(reduce_kernel, widths, starts, places),...  99.5 us
    pallas_call x1, Pallas kernels, layer(): pl.pallas_call(layer_kernel, grid=(tokens // tile,), out_shape=(low_narro...  42.9 us
    pallas_call x1, Pallas kernels, attend_back(): pl.pallas_call(functools.partial(attend_back_kernel, sizes, tile), out_sh...  38.8 us
    unnamed x45, local copies, waits for them, and re-layouts  24.3 us

profile of v6, /device:TPU:1, one launch (start us, length us, event | category | flops | bytes accessed | tf_op | source)
XLA Modules:
  0.0 483.8 jit_solution(5970296348482957261)
XLA Ops:
  0.7 0.7 fusion.6
  1.4 0.0 copy-start.11
  1.4 1.0 broadcast_in_dim.8.col_ref
  2.4 0.8 fusion.14
  3.2 0.6 reshape.395.bias_ref
  3.8 4.3 copy.27
  8.1 0.0 copy-done.11
  8.1 105.7 %front.1 = (bf16[2304,768]{1,0:T(8,128)(2,1)}, bf16[768,768]{1,0:T(8,128)(2,1)}, bf16[3072,768]{1,0:T(8,128)(2,1)}, bf16[3072,768]{1,0:T(8,128)(2,1)}, bf16[1024...) custom-call(bf16[1152,768]{1,0:T(8,128)(2,1)} %bitcast.49, ...), custom_call_target="tpu_custom_call" | custom-call | flops 6845104128 | bytes 113246208 | tf_op jit(solution)/shard_map/front/pallas_call | solution.py:748
  113.9 0.0 slice-done
  113.9 0.6 slice.61.small_ref
  114.5 0.0 copy-done.9
  114.5 0.6 slice.62
  115.1 42.9 %layer.1 = (bf16[1024,768]{1,0:T(8,128)(2,1)}, bf16[1024,768]{1,0:T(8,128)(2,1)}, bf16[1024,3072]{1,0:T(8,128)(2,1)}, bf16[1024,768]{1,0:T(8,128)(2,1)}, bf16[10...) custom-call(bf16[1024,768]{1,0:T(8,128)(2,1)} %get-tuple-element.38., ...), custom_call_target="tpu_custom_call" | custom-call | flops 21743271936 | bytes 34209792 | tf_op jit(solution)/shard_map/layer/pallas_call | solution.py:378
  158.0 0.0 copy-done.12
  158.0 0.1 slice.63
  158.1 0.1 slice.65
  158.2 0.2 convert_reduce_fusion.3
  158.5 0.0 copy-done
  158.5 0.6 gather_fusion
  159.2 0.1 copy.28
  159.3 0.6 reshape.398.table
  159.9 38.8 %attend_back.1.d_qkv_ref = bf16[3,1024,768]{2,1,0:T(8,128)(2,1)} custom-call(s32[1,8]{1,0:T(1,128)} %reshape.398.table, bf16[1024,2304]{1,0:T(8,128)(2,1)} %get-tuple-element.46.q_ref.k_ref.v_ref, bf16[1024,2304]{1,0:T(8,128)(2,1)} %get-tuple-element.46.q_ref.k_ref.v_ref, bf16[1024,2304]{1,0:T(8,128)(2,1)} %get-tuple-element.46.q_ref.k_ref.v_ref, ...), custom_call_target="tpu_custom_call" | custom-call | flops 8053063680 | bytes 11010048 | tf_op jit(solution)/shard_map/attend_back/pallas_call | solution.py:233
  198.6 0.0 copy-done.8
  198.6 2.9 fusion.1
  201.6 0.0 copy-start.7
  201.6 1.4 fusion
  203.0 0.0 copy-done.7
  203.0 2.6 add_convert_fusion.input_grad_ref
  205.6 0.5 convert_reduce_fusion
  206.1 0.2 copy-done.13
  206.4 0.0 copy-start.15
  206.4 0.6 copy-done.15
  207.0 99.5 %reduce_all.1 = (bf16[1152,768]{1,0:T(8,128)(2,1)}, f32[72,128]{1,0:T(8,128)}) custom-call(bf16[1024,3072]{1,0:T(8,128)(2,1)} %get-tuple-element.44.d_up_ref, bf16[1024,3072]{1,0:T(8,128)(2,1)} %get-tuple-element.45.active_ref, bf16[3,1024,768]{2,1,0:T(8,128)(2,1)} %attend_back.1.d_qkv_ref, bf16[1024,768]{1,0:T(8,128)(2,1)} %get-tuple-element.49.d_att_ref, ...), custom_call_target="tpu_custom_call" | custom-call | flops 14495514624 | bytes 141557760 | tf_op jit(solution)/shard_map/reduce_all/pallas_call | solution.py:1209
  306.6 156.0 %optimize.1 = (f32[768,1152]{1,0:T(8,128)}, f32[768,1152]{1,0:T(8,128)}, f32[768,1152]{1,0:T(8,128)}, f32[768,1152]{1,0:T(8,128)}, bf16[768,1152]{1,0:T(8,128)(2...) custom-call(bf16[1152,768]{1,0:T(8,128)(2,1)} %get-tuple-element.54.grad_ref, ...), custom_call_target="tpu_custom_call" | custom-call | flops 13589544960 | bytes 283115520 | tf_op jit(solution)/shard_map/optimize/pallas_call | solution.py:1560
  462.6 1.6 multiply_subtract_fusion
  464.2 2.4 copy.41
  466.6 2.4 copy.42
  468.9 0.0 copy-done.5
  468.9 1.8 copy.43
  470.7 1.5 copy-done.4
  472.2 1.8 copy.44
  474.0 1.5 copy-done.3
  475.5 1.8 copy.45
  477.3 1.5 copy-done.2
  478.8 1.8 copy.46
  480.6 0.9 copy-done.6
  481.5 1.2 copy.47
  482.7 0.6 copy.48
  (33 shorter events, 0.2 us)
Async XLA Ops:
  1.4 6.7 %copy-start.11 = (s32[1,1024]{1,0:T(1,128)}, s32[1,1024]{1,0:T(1,128)S(1)}, u32[]{:S(2)}) copy-start(s32[1,1024]{1,0:T(1,128)S(1)} %fusion.6) | copy-start | bytes 12292
  8.1 105.8 %slice-start = ((f32[9216]{0:T(1024)}), f32[6144]{0:T(1024)S(1)}, s32[]{:S(2)}) async-start(f32[9216]{0:T(1024)} %param.20), calls=%async_computation | async-start | bytes 49152 | tf_op jit(solution)/shard_map/slice | solution.py:421
  8.1 106.4 %copy-start.9 = (f32[9216]{0:T(1024)S(1)}, f32[9216]{0:T(1024)}, u32[]{:S(2)}) copy-start(f32[9216]{0:T(1024)} %param.20) | copy-start | bytes 110596
  115.1 42.9 %copy-start.12 = (s32[1,1024]{1,0:T(1,128)S(1)}, s32[1,1024]{1,0:T(1,128)}, u32[]{:S(2)}) copy-start(s32[1,1024]{1,0:T(1,128)} %copy-done.11) | copy-start | bytes 12292
  115.1 43.4 %copy-start = (s32[5]{0:T(128)S(1)}, s32[5]{0:T(128)}, u32[]{:S(2)}) copy-start(s32[5]{0:T(128)} %constant.76.clone) | copy-start | bytes 64
  159.9 38.8 %copy-start.8 = (bf16[2304,768]{1,0:T(8,128)(2,1)S(1)}, bf16[2304,768]{1,0:T(8,128)(2,1)}, u32[]{:S(2)}) copy-start(bf16[2304,768]{1,0:T(8,128)(2,1)} %get-tuple-element.56) | copy-start | bytes 10616836
  198.6 3.0 copy-start.1
  201.6 1.4 copy-start.7
  205.6 0.7 copy-start.13
  205.6 0.8 copy-start.14
  206.4 0.6 copy-start.15
  462.6 6.4 %copy-start.5 = (f32[768,1152]{1,0:T(8,128)S(1)}, f32[768,1152]{1,0:T(8,128)}, u32[]{:S(2)}) copy-start(f32[768,1152]{1,0:T(8,128)} %get-tuple-element.89) | copy-start | bytes 10616836
  468.9 3.3 copy-start.4
  472.2 3.3 copy-start.3
  475.5 3.3 copy-start.2
  478.8 2.8 copy-start.6
  481.5 1.2 copy-start.10
